TPU v7x, 256 devices: a whole 4x4x8 slice. The times are simulated.
256 devices in a mesh: item: 128 (over x, y_hi, z, core), grp: 2 (over y_lo).
Axes of the slice: x: 4, y: 4 (y_hi: 2, y_lo: 2; y = y_hi * 2 + y_lo), z: 8, core: 2. Of those that a mesh axis runs over, the one named last changes fastest.
Arguments:
- hidden: bfloat16 [768, 256], P(('grp', 'item')), may hold values from -400 to 400
- item_table: bfloat16 [1048576, 256], P('item'), may hold values from -1.5 to 1.5
- targets: int32 [768], P(('grp', 'item')), may hold values from 0 to 1048575
- lengths: int32 [2, 16], replicated, may hold values from 1 to 96, 384 in all within a row
Outputs:
- row_loss: float32 [768], P(('grp', 'item'))
- hidden_grad: bfloat16 [768, 256], P(('grp', 'item'))
- table_grad: bfloat16 [1048576, 256], P(('item', 'grp'))
Inputs may be any that keep to these rules, and one draw needn't show every extreme that they name: Each row holds the lengths of the 16 user sequences that fill one group's 384 positions in order, and sums to 384.
All inputs are finite; a program needn't handle non-finite values.
Results may differ from a plain program's by a relative error of at most 0.0047.
Values may be sent and summed in bfloat16 or wider, within the bound.
No kernel may reach another device: no remote copies, remote signals or barrier semaphores. Data moves between devices by JAX's collectives and lax.ppermute only.
A program may use at most 64 MiB of HBM per device.

v0:
```python
import jax
import jax.numpy as jnp
from jax import lax
from jax.sharding import Mesh
from jax.sharding import PartitionSpec as P

ITEM = ("item_0", "item_1", "item_2", "item_3")
GRP_ITEM = ("grp", "item_0", "item_1", "item_2", "item_3")
ITEM_GRP = ("item_0", "item_1", "item_2", "item_3", "grp")


def sent_to_all(x, axis):
    length = lax.axis_size(axis)
    return lax.all_to_all(jnp.broadcast_to(x[None], (length, *x.shape)), axis, 0, 0, tiled=True)


def in_order(blocks, dim):
    blocks = jnp.moveaxis(blocks, 0, dim)
    lengths = blocks.shape
    return blocks.reshape(*lengths[:dim], lengths[dim] * lengths[dim + 1], *lengths[dim + 2 :])


def whole_of(x, axes, dim):
    far, near = axes
    initial = sent_to_all(x, far)
    blocks = jnp.swapaxes(sent_to_all(initial, near), 0, 1)
    return in_order(blocks.reshape(-1, *x.shape), dim)


def gather_directly(x, axis, dim):
    return in_order(sent_to_all(x, axis), dim)


def gathered_once(x, axis):
    leaves = jax.tree.leaves(x)
    sequence = sorted(range(len(leaves)), key=lambda k: -leaves[k].size)
    width = (1, *leaves[sequence[0]].shape)[-1]
    lines = [
        jnp.pad(leaves[k].reshape(-1), (0, -leaves[k].size % width)).reshape(-1, width)
        for k in sequence
    ]
    both, at, found = (lax.all_gather(jnp.concatenate(lines), axis), 0, {})
    for k, line in zip(sequence, lines):
        section = both[:, at : at + len(line)].reshape(len(both), -1)
        found[k] = section[:, : leaves[k].size].reshape(-1, *leaves[k].shape)
        at += len(line)
    numbers = iter(range(len(leaves)))
    return jax.tree.map(lambda _: found[next(numbers)], x)


def merged_by_axis(x, axes, combine):
    for axis in axes:
        pieces = gathered_once(x, axis)
        x = jax.tree.map(lambda part: part[0], pieces)
        for k in range(1, lax.axis_size(axis)):
            x = combine(x, jax.tree.map(lambda part: part[k], pieces))
    return x


def in_blocks(x, dim, length):
    before, after = (x.shape[:dim], x.shape[dim + 1 :])
    return jnp.moveaxis(x.reshape(*before, length, -1, *after), dim, 0)


def sent_and_summed(x, axis, dim):
    blocks = in_blocks(x, dim, lax.axis_size(axis))
    arrived = lax.all_to_all(blocks, axis, split_axis=0, concat_axis=0, tiled=True)
    return arrived.sum(axis=0)


def sum_by_axis(x, axes, dim):
    far, near = axes
    blocks = in_blocks(x, dim, lax.axis_size(far))
    nearer = sent_and_summed(blocks, near, dim + 1)
    arrived = lax.all_to_all(nearer, far, split_axis=0, concat_axis=0, tiled=True)
    return arrived.sum(axis=0)


def block_width():
    return 2048


def weights_for(lengths, group_index, group_rows):
    seq_count = lengths.shape[1]
    own_lengths = lax.dynamic_index_in_dim(lengths, group_index, 0, keepdims=False)
    seq_ends = jnp.cumsum(own_lengths)
    starts = seq_ends - own_lengths
    places = jnp.arange(group_rows, dtype=jnp.int32)
    inside = (places[:, None] >= starts[None, :]) & (places[:, None] < seq_ends[None, :])
    row_length = jnp.sum(
        jnp.where(inside, own_lengths[None, :].astype(jnp.float32), jnp.float32(0.0)), axis=1
    )
    return group_rows / seq_count / row_length


def split_blocks(item_table, first_item, block_size):
    block_count = item_table.shape[0] // block_size
    blocks = item_table.reshape(block_count, block_size, item_table.shape[1])
    block_starts = first_item + block_size * jnp.arange(block_count, dtype=jnp.int32)
    return (blocks, block_starts)


def partial_stats(states, target_ids, item_table, first_item, block_size):
    blocks, block_starts = split_blocks(item_table, first_item, block_size)
    row_count = states.shape[0]

    def partial_visit(carried, block_pair):
        highest, running, picked = carried
        item_block, block_start = block_pair
        scores = jnp.einsum("rd,id->ri", states, item_block, preferred_element_type=jnp.float32)
        new_max = jnp.maximum(highest, jnp.max(scores, axis=1))
        running = running * jnp.exp(highest - new_max) + jnp.sum(
            jnp.exp(scores - new_max[:, None]), axis=1
        )
        columns = block_start + jnp.arange(block_size, dtype=jnp.int32)
        matched = target_ids[:, None] == columns[None, :]
        picked = picked + jnp.sum(jnp.where(matched, scores, jnp.float32(0.0)), axis=1)
        return ((new_max, running, picked), None)

    start_stats = (
        jnp.full((row_count,), -jnp.inf, dtype=jnp.float32),
        jnp.zeros((row_count,), jnp.float32),
        jnp.zeros((row_count,), jnp.float32),
    )
    final_stats, unused = lax.scan(partial_visit, start_stats, (blocks, block_starts))
    return final_stats


def combine_stats(first, second):
    max_first, sum_first, pick_first = first
    max_second, sum_second, pick_second = second
    highest = jnp.maximum(max_first, max_second)
    merged_sum = sum_first * jnp.exp(max_first - highest) + sum_second * jnp.exp(
        max_second - highest
    )
    return (highest, merged_sum, pick_first + pick_second)


def backward(states, target_ids, item_table, first_item, block_size, log_total, row_weight):
    blocks, block_starts = split_blocks(item_table, first_item, block_size)

    def backward_visit(state_grad, block_pair):
        item_block, block_start = block_pair
        scores = jnp.einsum("rd,id->ri", states, item_block, preferred_element_type=jnp.float32)
        columns = block_start + jnp.arange(block_size, dtype=jnp.int32)
        matched = (target_ids[:, None] == columns[None, :]).astype(jnp.float32)
        signal = (row_weight[:, None] * (jnp.exp(scores - log_total[:, None]) - matched)).astype(
            jnp.bfloat16
        )
        state_grad = state_grad + jnp.dot(signal, item_block, preferred_element_type=jnp.float32)
        item_grad = jnp.einsum("ri,rd->id", signal, states, preferred_element_type=jnp.float32)
        return (state_grad, item_grad)

    start_grad = jnp.zeros((states.shape[0], states.shape[1]), jnp.float32)
    state_grad, item_grads = lax.scan(backward_visit, start_grad, (blocks, block_starts))
    return (state_grad, item_grads.reshape(item_table.shape[0], item_table.shape[1]))


def local(hidden, item_table, targets, lengths):
    rows_local = hidden.shape[0]
    items_local = item_table.shape[0]
    block_size = block_width()
    item_rank = lax.axis_index(ITEM)
    group_rank = lax.axis_index("grp")
    first_item = item_rank * items_local
    group_states, group_targets = (
        whole_of(hidden, (("item_0", "item_1", "item_2"), "item_3"), 0),
        whole_of(targets, (("item_0", "item_1", "item_2"), "item_3"), 0),
    )
    group_rows = group_states.shape[0]
    states, target_ids = (
        gather_directly(group_states, "grp", 0),
        gather_directly(group_targets, "grp", 0),
    )
    row_weight = jnp.concatenate(
        [weights_for(lengths, member, group_rows) for member in range(lengths.shape[0])]
    )
    own_start = group_rank * group_rows + item_rank * rows_local
    highest, running, picked = partial_stats(states, target_ids, item_table, first_item, block_size)
    row_max, exp_total, target_score = merged_by_axis(
        (highest, running, picked), ITEM, combine_stats
    )
    log_total = row_max + jnp.log(exp_total)
    losses = log_total - target_score
    row_loss = lax.dynamic_slice_in_dim(losses, own_start, rows_local)
    half_items = items_local // 2
    own_items = lax.dynamic_slice_in_dim(item_table, group_rank * half_items, half_items)
    state_grad, table_grad = backward(
        states,
        target_ids,
        own_items,
        first_item + group_rank * half_items,
        block_width(),
        log_total,
        row_weight,
    )
    group_grad = sent_and_summed(state_grad, "grp", 0)
    hidden_grad = sum_by_axis(group_grad, (("item_0", "item_1", "item_2"), "item_3"), 0)
    return (row_loss, hidden_grad.astype(jnp.bfloat16), table_grad.astype(jnp.bfloat16))


def solution(mesh):
    split = Mesh(
        mesh.devices.reshape(4, 2, 8, 2, mesh.shape["grp"]),
        ("item_0", "item_1", "item_2", "item_3", "grp"),
    )
    return jax.shard_map(
        local,
        mesh=split,
        in_specs=(P(GRP_ITEM, None), P(ITEM, None), P(GRP_ITEM), P()),
        out_specs=(P(GRP_ITEM), P(GRP_ITEM, None), P(ITEM_GRP, None)),
        check_vma=False,
    )
```

profile of v0, /device:TPU:8, one launch (start us, length us, event | category | flops | bytes accessed | tf_op | source)
XLA Modules:
  0.0 189.7 jit_solution(7618823905540694022)
XLA Ops:
  0.6 1.3 broadcast_in_dim.99
  1.9 13.7 %all-to-all-start.3 = ((s32[64,1,3]{2,1,0:T(1,128)}), s32[64,1,3]{2,1,0:T(1,128)S(1)}, u32[]{:S(2)}, u32[]{:S(2)}) async-start(s32[64,1,3]{2,1,0:T(1,128)} %broadcast_in_dim.99), calls=%async_computation.3 | async-start | bytes 65536 | tf_op jit(solution)/shard_map/all_to_all | solution.py:14
  15.6 0.8 slice_bitcast_fusion.29
  16.9 0.8 fusion.70
  17.7 1.7 constant_dynamic-slice_fusion
  19.5 8.0 %all-to-all-done.3 = s32[64,1,3]{2,1,0:T(1,128)S(1)} async-done(((s32[64,1,3]{2,1,0:T(1,128)}), s32[64,1,3]{2,1,0:T(1,128)S(1)}, u32[]{:S(2)}, u32[]{:S(2)}) %all-to-all-start.3) | async-done | bytes 800 | tf_op jit(solution)/shard_map/all_to_all | solution.py:14
  27.6 3.7 %all_to_all.50 = s32[2,1,192]{2,1,0:T(1,128)S(1)} all-to-all(s32[2,1,192]{2,1,0:T(1,128)S(1)} %reshape.977), channel_id=1, replica_groups=mesh['item_0'=4,'item_1'=2,'item_2'=8,'item_3'=2,'grp'=2] {'item_3'}, dimensions={0} | all-to-all | bytes 3072 | tf_op jit(solution)/shard_map/all_to_all | solution.py:14
  31.3 0.7 broadcast_in_dim.95
  32.0 4.8 %all-to-all-start = ((bf16[64,3,256]{2,1,0:T(4,128)(2,1)}), bf16[64,3,256]{2,1,0:T(4,128)(2,1)S(1)}, u32[]{:S(2)}, u32[]{:S(2)}) async-start(bf16[64,3,256]{2,1,0:T(4,128)(2,1)} %broadcast_in_dim.95), calls=%async_computation | async-start | bytes 262144 | tf_op jit(solution)/shard_map/all_to_all | solution.py:14
  38.4 11.4 %all-to-all-done = bf16[64,3,256]{2,1,0:T(4,128)(2,1)S(1)} async-done(((bf16[64,3,256]{2,1,0:T(4,128)(2,1)}), bf16[64,3,256]{2,1,0:T(4,128)(2,1)S(1)}, u32[]{:S(2)}, u32[]{:S(2)}) %all-to-all-start) | async-done | bytes 98336 | tf_op jit(solution)/shard_map/all_to_all | solution.py:14
  49.9 3.9 %all_to_all.51 = bf16[2,64,3,256]{3,1,2,0:T(8,128)(2,1)S(1)} all-to-all(bf16[2,64,3,256]{3,1,2,0:T(8,128)(2,1)S(1)} %broadcast_in_dim.96), channel_id=1, replica_groups=mesh['item_0'=4,'item_1'=2,'item_2'=8,'item_3'=2,'grp'=2] {'item_3'}, dimensions={0} | all-to-all | bytes 393216 | tf_op jit(solution)/shard_map/all_to_all | solution.py:14
  54.4 4.6 %all-to-all-start.5 = ((s32[2,1,384]{2,1,0:T(1,128)}), s32[2,1,384]{2,1,0:T(1,128)S(1)}, u32[]{:S(2)}, u32[]{:S(2)}) async-start(s32[2,1,384]{2,1,0:T(1,128)} %broadcast_in_dim.103), calls=%async_computation.5 | async-start | bytes 6144 | tf_op jit(solution)/shard_map/all_to_all | solution.py:14
  59.3 1.4 all-to-all-done.5
  60.7 0.8 broadcast_in_dim.98
  61.4 5.5 %all-to-all-start.2 = ((bf16[2,384,256]{2,1,0:T(8,128)(2,1)}), bf16[2,384,256]{2,1,0:T(8,128)(2,1)S(1)}, u32[]{:S(2)}, u32[]{:S(2)}) async-start(bf16[2,384,256]{2,1,0:T(8,128)(2,1)} %broadcast_in_dim.98), calls=%async_computation.2 | async-start | bytes 786432 | tf_op jit(solution)/shard_map/all_to_all | solution.py:14
  66.9 4.3 %all-to-all-done.2 = bf16[2,384,256]{2,1,0:T(8,128)(2,1)S(1)} async-done(((bf16[2,384,256]{2,1,0:T(8,128)(2,1)}), bf16[2,384,256]{2,1,0:T(8,128)(2,1)S(1)}, u32[]{:S(2)}, u32[]{:S(2)}) %all-to-all-start.2) | async-done | bytes 393248 | tf_op jit(solution)/shard_map/all_to_all | solution.py:14
  71.2 20.8 %while.28 = (s32[]{:T(128)}, f32[768]{0:T(1024)S(1)}, f32[768]{0:T(1024)S(1)}, f32[768]{0:T(1024)S(1)}, bf16[4,2048,256]{2,1,0:T(8,128)(2,1)}, /*index=5*/bf16[7...) while((s32[]{:T(128)}, f32[768]{0:T(1024)S(1)}, ...), condition=%wide.region_4.5_spmd.clone, body=%wide.region_0.4_spmd.clone.sunk | while | flops 814750208 | bytes 14102668 | solution.py:125
  71.9 0.7 iota_add_fusion.4
  72.6 2.3 %fusion.93 = (f32[768]{0:T(1024)S(1)}, f32[2048,768]{1,0:T(8,128)S(1)}) fusion(bf16[768,256]{1,0:T(8,128)(2,1)S(1)} %get-tuple-element.359, bf16[4,2048,256]{2,1,0:T(8,128)(2,1)} %get-tuple-element.358, s32[]{:T(128)S(6)} %copy.48), kind=kOutput, calls=%fused_computation.151.clone.1 | convolution fusion | flops 806878464 | bytes 7736324 | tf_op jit(solution)/shard_map/while/body/eval_jaxpr/rd,id->ri/dot_general | solution.py:110
  74.8 1.5 fusion.94
  76.4 0.7 dynamic_slice.64
  77.1 0.7 iota_add_fusion.4
  77.8 2.2 %fusion.93 = (f32[768]{0:T(1024)S(1)}, f32[2048,768]{1,0:T(8,128)S(1)}) fusion(bf16[768,256]{1,0:T(8,128)(2,1)S(1)} %get-tuple-element.359, bf16[4,2048,256]{2,1,0:T(8,128)(2,1)} %get-tuple-element.358, s32[]{:T(128)S(6)} %copy.48), kind=kOutput, calls=%fused_computation.151.clone.1 | convolution fusion | flops 806878464 | bytes 7736324 | tf_op jit(solution)/shard_map/while/body/eval_jaxpr/rd,id->ri/dot_general | solution.py:110
  80.1 1.5 fusion.94
  81.6 0.7 dynamic_slice.64
  82.3 0.7 iota_add_fusion.4
  83.0 2.3 %fusion.93 = (f32[768]{0:T(1024)S(1)}, f32[2048,768]{1,0:T(8,128)S(1)}) fusion(bf16[768,256]{1,0:T(8,128)(2,1)S(1)} %get-tuple-element.359, bf16[4,2048,256]{2,1,0:T(8,128)(2,1)} %get-tuple-element.358, s32[]{:T(128)S(6)} %copy.48), kind=kOutput, calls=%fused_computation.151.clone.1 | convolution fusion | flops 806878464 | bytes 7736324 | tf_op jit(solution)/shard_map/while/body/eval_jaxpr/rd,id->ri/dot_general | solution.py:110
  85.3 1.5 fusion.94
  86.8 0.7 dynamic_slice.64
  87.5 0.7 iota_add_fusion.4
  88.2 2.2 %fusion.93 = (f32[768]{0:T(1024)S(1)}, f32[2048,768]{1,0:T(8,128)S(1)}) fusion(bf16[768,256]{1,0:T(8,128)(2,1)S(1)} %get-tuple-element.359, bf16[4,2048,256]{2,1,0:T(8,128)(2,1)} %get-tuple-element.358, s32[]{:T(128)S(6)} %copy.48), kind=kOutput, calls=%fused_computation.151.clone.1 | convolution fusion | flops 806878464 | bytes 7736324 | tf_op jit(solution)/shard_map/while/body/eval_jaxpr/rd,id->ri/dot_general | solution.py:110
  90.5 1.5 fusion.94
  92.1 11.9 %all-gather.4 = f32[4,3,768]{2,1,0:T(4,128)S(1)} all-gather(f32[1,3,768]{2,1,0:T(4,128)S(1)} %maximum_bitcast_fusion), channel_id=2, replica_groups=mesh['item_0'=4,'item_1'=2,'item_2'=8,'item_3'=2,'grp'=2] {'item_0'}, dimensions={0}, use_global_device_ids=true | all-gather | bytes 46080 | tf_op jit(solution)/shard_map/all_gather | solution.py:42
  104.1 5.9 %all-gather.5 = f32[2,3,768]{2,1,0:T(4,128)S(1)} all-gather(f32[1,3,768]{2,1,0:T(4,128)S(1)} %maximum_bitcast_fusion.1), channel_id=3, replica_groups=mesh['item_0'=4,'item_1'=2,'item_2'=8,'item_3'=2,'grp'=2] {'item_1'}, dimensions={0}, use_global_device_ids=true | all-gather | bytes 27648 | tf_op jit(solution)/shard_map/all_gather | solution.py:42
  110.1 24.6 %all-gather.6 = f32[8,3,768]{2,1,0:T(4,128)S(1)} all-gather(f32[1,3,768]{2,1,0:T(4,128)S(1)} %maximum_bitcast_fusion.2), channel_id=4, replica_groups=mesh['item_0'=4,'item_1'=2,'item_2'=8,'item_3'=2,'grp'=2] {'item_2'}, dimensions={0}, use_global_device_ids=true | all-gather | bytes 82944 | tf_op jit(solution)/shard_map/all_gather | solution.py:42
  134.8 1.8 all-gather.7
  136.7 12.8 %while.29 = (s32[]{:T(128)}, f32[768,256]{1,0:T(8,128)S(1)}, bf16[2,2048,256]{2,1,0:T(8,128)(2,1)}, f32[768]{0:T(1024)S(1)}, bf16[2,2048,256]{2,1,0:T(8,128)(2,1...) while((s32[]{:T(128)}, f32[768,256]{1,0:T(8,128)S(1)}, ...), condition=%wide.region_10.11_spmd.clone, body=%wide.region_9.10_spmd.clone.sunk | while | flops 2425751552 | bytes 16025755 | solution.py:155
  138.0 1.9 %fusion.101 = bf16[768,2048]{0,1:T(8,128)(2,1)S(1)} fusion(bf16[768,256]{1,0:T(8,128)(2,1)S(1)} %get-tuple-element.391, s32[768]{0:T(1024)S(1)} %eq.59, f32[768]{0:T(1024)S(1)} %get-tuple-element.392, f32[768]{0:T(1024)S(1)} %get-tuple-element.389, s32[2048]{0:T(1024)S(1)} %iota_add_fusion.5, bf16[2,2048,256]{2,1,0:T(8,128)(2,1)S(1)} %get-tuple-element.390, ...), kind=kOutput, calls=%fused_computation.16.clone.1 | convolution fusion | flops 814743552 | bytes 4608004 | tf_op jit(solution)/shard_map/while/body/eval_jaxpr/rd,id->ri/dot_general | solution.py:144
  139.9 1.2 convolution_add_fusion.2
  141.1 2.0 %fusion.102 = bf16[2,2048,256]{2,1,0:T(8,128)(2,1)} fusion(bf16[2,2048,256]{2,1,0:T(8,128)(2,1)} %get-tuple-element.377, s32[]{:T(128)S(6)} %copy.59, bf16[768,2048]{0,1:T(8,128)(2,1)S(1)} %fusion.101, bf16[768,256]{1,0:T(8,128)(2,1)S(1)} %get-tuple-element.391), kind=kOutput, calls=%fused_computation.18.clone.1 | convolution fusion | flops 805306368 | bytes 5636100 | tf_op jit(solution)/shard_map/while/body/eval_jaxpr/ri,rd->id/dot_general | solution.py:151
  144.3 1.9 %fusion.101 = bf16[768,2048]{0,1:T(8,128)(2,1)S(1)} fusion(bf16[768,256]{1,0:T(8,128)(2,1)S(1)} %get-tuple-element.391, s32[768]{0:T(1024)S(1)} %eq.59, f32[768]{0:T(1024)S(1)} %get-tuple-element.392, f32[768]{0:T(1024)S(1)} %get-tuple-element.389, s32[2048]{0:T(1024)S(1)} %iota_add_fusion.5, bf16[2,2048,256]{2,1,0:T(8,128)(2,1)S(1)} %get-tuple-element.390, ...), kind=kOutput, calls=%fused_computation.16.clone.1 | convolution fusion | flops 814743552 | bytes 4608004 | tf_op jit(solution)/shard_map/while/body/eval_jaxpr/rd,id->ri/dot_general | solution.py:144
  146.3 1.2 convolution_add_fusion.2
  147.5 2.0 %fusion.102 = bf16[2,2048,256]{2,1,0:T(8,128)(2,1)} fusion(bf16[2,2048,256]{2,1,0:T(8,128)(2,1)} %get-tuple-element.377, s32[]{:T(128)S(6)} %copy.59, bf16[768,2048]{0,1:T(8,128)(2,1)S(1)} %fusion.101, bf16[768,256]{1,0:T(8,128)(2,1)S(1)} %get-tuple-element.391), kind=kOutput, calls=%fused_computation.18.clone.1 | convolution fusion | flops 805306368 | bytes 5636100 | tf_op jit(solution)/shard_map/while/body/eval_jaxpr/ri,rd->id/dot_general | solution.py:151
  149.5 13.8 %all_to_all.52 = f32[2,384,256]{2,1,0:T(8,128)S(1)} all-to-all(f32[2,384,256]{2,1,0:T(8,128)S(1)} %bitcast.368), channel_id=1, replica_groups=mesh['item_0'=4,'item_1'=2,'item_2'=8,'item_3'=2,'grp'=2] {'grp'}, dimensions={0} | all-to-all | bytes 1572864 | tf_op jit(solution)/shard_map/all_to_all | solution.py:67
  163.7 4.0 %all_to_all.53 = f32[2,64,3,256]{3,1,2,0:T(8,128)S(1)} all-to-all(f32[2,64,3,256]{3,1,2,0:T(8,128)S(1)} %copy.38), channel_id=1, replica_groups=mesh['item_0'=4,'item_1'=2,'item_2'=8,'item_3'=2,'grp'=2] {'item_3'}, dimensions={0} | all-to-all | bytes 786432 | tf_op jit(solution)/shard_map/all_to_all | solution.py:67
  167.7 0.8 copy.39
  168.6 5.1 %all-to-all-start.8 = ((f32[64,3,256]{2,1,0:T(4,128)}), f32[64,3,256]{2,1,0:T(4,128)S(1)}, u32[]{:S(2)}, u32[]{:S(2)}) async-start(f32[64,3,256]{2,1,0:T(4,128)} %copy.39), calls=%async_computation.8 | async-start | bytes 524288 | tf_op jit(solution)/shard_map/all_to_all | solution.py:75
  174.3 14.8 %all-to-all-done.8 = f32[64,3,256]{2,1,0:T(4,128)S(1)} async-done(((f32[64,3,256]{2,1,0:T(4,128)}), f32[64,3,256]{2,1,0:T(4,128)S(1)}, u32[]{:S(2)}, u32[]{:S(2)}) %all-to-all-start.8) | async-done | bytes 196640 | tf_op jit(solution)/shard_map/all_to_all | solution.py:75
  (78 shorter events, 8.5 us)
Async XLA Ops:
  0.6 30.7 %copy-start = (bf16[3,256]{1,0:T(4,128)(2,1)S(1)}, bf16[3,256]{1,0:T(4,128)(2,1)}, u32[]{:S(2)}) copy-start(bf16[3,256]{1,0:T(4,128)(2,1)} %param.8) | copy-start | bytes 4612
  1.9 25.5 %all-to-all-start.3 = ((s32[64,1,3]{2,1,0:T(1,128)}), s32[64,1,3]{2,1,0:T(1,128)S(1)}, u32[]{:S(2)}, u32[]{:S(2)}) async-start(s32[64,1,3]{2,1,0:T(1,128)} %broadcast_in_dim.99), calls=%async_computation.3 | async-start | bytes 65536 | tf_op jit(solution)/shard_map/all_to_all | solution.py:14
  32.0 17.8 %all-to-all-start = ((bf16[64,3,256]{2,1,0:T(4,128)(2,1)}), bf16[64,3,256]{2,1,0:T(4,128)(2,1)S(1)}, u32[]{:S(2)}, u32[]{:S(2)}) async-start(bf16[64,3,256]{2,1,0:T(4,128)(2,1)} %broadcast_in_dim.95), calls=%async_computation | async-start | bytes 262144 | tf_op jit(solution)/shard_map/all_to_all | solution.py:14
  54.4 6.3 %all-to-all-start.5 = ((s32[2,1,384]{2,1,0:T(1,128)}), s32[2,1,384]{2,1,0:T(1,128)S(1)}, u32[]{:S(2)}, u32[]{:S(2)}) async-start(s32[2,1,384]{2,1,0:T(1,128)} %broadcast_in_dim.103), calls=%async_computation.5 | async-start | bytes 6144 | tf_op jit(solution)/shard_map/all_to_all | solution.py:14
  61.4 9.8 %all-to-all-start.2 = ((bf16[2,384,256]{2,1,0:T(8,128)(2,1)}), bf16[2,384,256]{2,1,0:T(8,128)(2,1)S(1)}, u32[]{:S(2)}, u32[]{:S(2)}) async-start(bf16[2,384,256]{2,1,0:T(8,128)(2,1)} %broadcast_in_dim.98), calls=%async_computation.2 | async-start | bytes 786432 | tf_op jit(solution)/shard_map/all_to_all | solution.py:14
  168.6 20.5 %all-to-all-start.8 = ((f32[64,3,256]{2,1,0:T(4,128)}), f32[64,3,256]{2,1,0:T(4,128)S(1)}, u32[]{:S(2)}, u32[]{:S(2)}) async-start(f32[64,3,256]{2,1,0:T(4,128)} %copy.39), calls=%async_computation.8 | async-start | bytes 524288 | tf_op jit(solution)/shard_map/all_to_all | solution.py:75
where the time goes:
time: 191 us; the launch traced here: 190 us
  blocking collectives  69.7 us (36%)
  waiting for transfers between devices  39.8 us (21%)
  starting transfers between devices  33.6 us (18%)
  matrix products  19.2 us (10%)
  local copies, waits for them, and re-layouts  13.1 us (7%)
  other arithmetic  13.1 us (7%)
    all_gather x4, blocking collectives, gathered_once(): both, at, found = (lax.all_gather(jnp.concatenate(lines), axis), 0, {})  44.2 us
    all_to_all x4, starting transfers between devices, sent_to_all(): lax.all_to_all(jnp.broadcast_to(x[None], (length, *x.shape)), axis, 0, 0,...  28.5 us
    all_to_all x4, waiting for transfers between devices, sent_to_all(): lax.all_to_all(jnp.broadcast_to(x[None], (length, *x.shape)), axis, 0, 0,...  25.1 us
    all_to_all x2, blocking collectives, sent_and_summed(): lax.all_to_all(blocks, axis, split_axis=0, concat_axis=0, tiled=True)  17.9 us
    all_to_all x1, waiting for transfers between devices, sum_by_axis(): lax.all_to_all(nearer, far, split_axis=0, concat_axis=0, tiled=True)  14.8 us
    dot_general x4, matrix products, partial_visit(): jnp.einsum('rd,id->ri', states, item_block, preferred_element_type=jnp.fl...  9 us
    all_to_all x2, blocking collectives, sent_to_all(): lax.all_to_all(jnp.broadcast_to(x[None], (length, *x.shape)), axis, 0, 0,...  7.59 us
    reduce_sum x4, other arithmetic, partial_visit(): jnp.sum(jnp.where(matched, scores, jnp.float32(0.0)), axis=1)  6.04 us
  transfers between devices with their start and end apart: 5, of which 5 were waited for; matrix products, arithmetic and copies ran while one was open for 3% of the time, Pallas kernels for 0%

commit v1 on v0

v1 whole, which is shorter than its diff:
```python
import jax
import jax.numpy as jnp
from jax import lax
from jax.experimental import pallas as pl
from jax.experimental.pallas import tpu as pltpu
from jax.sharding import Mesh
from jax.sharding import PartitionSpec as P

ITEM = ("x", "yh", "z", "core")
GRP_ITEM = ("grp", "x", "yh", "z", "core")
ITEM_GRP = ("x", "yh", "z", "core", "grp")
PLANE = ("x", "yh", "grp")
CHIPS = ("x", "yh", "grp", "z")
DIGIT = 128
BLOCK = 512
F32 = jnp.float32
BF16 = jnp.bfloat16


def sent_to_all(x, axes):
    length = lax.axis_size(axes)
    return lax.all_to_all(jnp.broadcast_to(x[None], (length, *x.shape)), axes, 0, 0, tiled=True)


def from_pair(x):
    return lax.ppermute(x, "core", [(0, 1), (1, 0)])


def gathered(hidden, targets):
    rows, width = hidden.shape
    digits = jnp.stack([targets % DIGIT, targets // DIGIT % DIGIT, targets // DIGIT**2])
    digits = jnp.pad(digits.reshape(-1), (0, width - 3 * rows)).astype(BF16)
    mine = sent_to_all(jnp.concatenate([hidden, digits[None]]), CHIPS)
    other = from_pair(mine)
    first = lax.axis_index("core") == 0
    both = jnp.concatenate([jnp.where(first, mine, other), jnp.where(first, other, mine)])
    states = both[:, :rows].reshape(-1, width)
    digits = both[:, rows, : 3 * rows].reshape(-1, 3, rows).astype(jnp.int32)
    target_ids = digits[:, 0] + DIGIT * digits[:, 1] + DIGIT**2 * digits[:, 2]
    return states, target_ids.reshape(1, -1)


def weights_for(lengths, rows):
    groups, seq_count = lengths.shape
    sizes = [lax.axis_size(axis) for axis in ("core", "x", "yh", "grp", "z")]
    core, x, yh, grp, z, k = jnp.unravel_index(
        jnp.arange(sizes[0] * sizes[1] * sizes[2] * sizes[3] * sizes[4] * rows), (*sizes, rows)
    )
    place = (((x * sizes[2] + yh) * sizes[4] + z) * sizes[0] + core) * rows + k
    group_rows = place.shape[0] // groups
    before = jnp.arange(seq_count)[:, None] < jnp.arange(seq_count)[None, :]
    starts = jnp.sum(jnp.where(before[None], lengths[:, :, None], 0), axis=1)
    inside = (
        (grp[:, None, None] == jnp.arange(groups)[None, :, None])
        & (place[:, None, None] >= starts[None])
        & (place[:, None, None] < (starts + lengths)[None])
    )
    row_length = jnp.sum(jnp.where(inside, lengths[None].astype(F32), F32(0.0)), axis=(1, 2))
    return (group_rows / seq_count / row_length).reshape(1, -1)


def share_kernel(half_ref, target_ref, states_ref, items_ref, grad_ref, rows_ref, log_ref, high, total, grad, picked):
    step = pl.program_id(0)
    block = items_ref.shape[0]

    @pl.when(step == 0)
    def _():
        high[...] = jnp.full(high.shape, -jnp.inf, F32)
        total[...] = jnp.zeros(total.shape, F32)
        grad[...] = jnp.zeros(grad.shape, F32)
        picked[...] = jnp.zeros(picked.shape, F32)

    items = items_ref[...]
    scores = lax.dot_general(
        items, states_ref[...], (((1,), (1,)), ((), ())), preferred_element_type=F32
    )
    top = jnp.maximum(high[...], jnp.max(scores, axis=0, keepdims=True))
    shrink = jnp.exp(high[...] - top)
    parts = jnp.exp(scores - top)
    total[...] = total[...] * shrink + jnp.sum(parts, axis=0, keepdims=True)
    high[...] = top
    place = lax.broadcasted_iota(jnp.int32, parts.shape, 0)
    matched = place == target_ref[...] - step * block
    others = jnp.where(matched, 0.0, parts).astype(BF16)
    hot = jnp.where(matched, 1.0, 0.0).astype(BF16)
    across = items.T
    grad[...] = grad[...] * shrink + jnp.dot(across, others, preferred_element_type=F32)
    picked[...] += jnp.dot(across, hot, preferred_element_type=F32)

    @pl.when(step == pl.num_programs(0) - 1)
    def _():
        log_sum = high[...] + jnp.log(total[...])
        log_ref[...] = log_sum
        grad_ref[...] = grad[...] * jnp.exp(high[...] - log_sum)
        rows_ref[...] = picked[...].astype(BF16)


def shares(half, target_place, states, item_table):
    own = item_table.shape[0] // 2
    block = min(BLOCK, own)
    width, count = states.shape[1], states.shape[0]
    steps = own // block
    whole = lambda i, half: (0, 0)
    return pl.pallas_call(
        share_kernel,
        name="shares",
        out_shape=(
            jax.ShapeDtypeStruct((width, count), F32),
            jax.ShapeDtypeStruct((width, count), BF16),
            jax.ShapeDtypeStruct((1, count), F32),
        ),
        grid_spec=pltpu.PrefetchScalarGridSpec(
            num_scalar_prefetch=1,
            grid=(steps,),
            in_specs=[
                pl.BlockSpec((1, count), whole),
                pl.BlockSpec((count, width), whole),
                pl.BlockSpec((block, width), lambda i, half: (half[0] * steps + i, 0)),
            ],
            out_specs=[
                pl.BlockSpec((width, count), whole),
                pl.BlockSpec((width, count), whole),
                pl.BlockSpec((1, count), whole),
            ],
            scratch_shapes=[
                pltpu.VMEM((1, count), F32),
                pltpu.VMEM((1, count), F32),
                pltpu.VMEM((width, count), F32),
                pltpu.VMEM((width, count), F32),
            ],
        ),
        compiler_params=pltpu.CompilerParams(dimension_semantics=("arbitrary",)),
    )(half, target_place, states, item_table)


def table_kernel(half_ref, target_ref, log_ref, weight_ref, states_ref, items_ref, out_ref):
    step = pl.program_id(0)
    block = items_ref.shape[0]
    states = states_ref[...]
    scores = lax.dot_general(
        items_ref[...], states, (((1,), (1,)), ((), ())), preferred_element_type=F32
    )
    parts = jnp.exp(scores - log_ref[...])
    place = lax.broadcasted_iota(jnp.int32, parts.shape, 0)
    matched = place == target_ref[...] - step * block
    signal = (weight_ref[...] * jnp.where(matched, parts - 1.0, parts)).astype(BF16)
    out_ref[...] = jnp.dot(signal, states, preferred_element_type=F32).astype(BF16)


def table_gradient(half, target_place, log_total, weight, states, item_table):
    own = item_table.shape[0] // 2
    block = min(BLOCK, own)
    width, count = states.shape[1], states.shape[0]
    steps = own // block
    whole = lambda i, half: (0, 0)
    line = pl.BlockSpec((1, count), whole)
    return pl.pallas_call(
        table_kernel,
        name="table_gradient",
        out_shape=jax.ShapeDtypeStruct((own, width), BF16),
        grid_spec=pltpu.PrefetchScalarGridSpec(
            num_scalar_prefetch=1,
            grid=(steps,),
            in_specs=[
                line,
                line,
                line,
                pl.BlockSpec((count, width), whole),
                pl.BlockSpec((block, width), lambda i, half: (half[0] * steps + i, 0)),
            ],
            out_specs=pl.BlockSpec((block, width), lambda i, half: (i, 0)),
        ),
        compiler_params=pltpu.CompilerParams(dimension_semantics=("arbitrary",)),
    )(half, target_place, log_total, weight, states, item_table)


def thirds(x):
    high = lax.reduce_precision(x, 8, 7)
    rest = x - high
    middle = lax.reduce_precision(rest, 8, 7)
    return jnp.concatenate([high, middle, rest - middle]).astype(BF16)


def merged_logs(parts):
    top = jnp.max(parts, axis=0)
    return top + jnp.log(jnp.sum(jnp.exp(parts - top[None]), axis=0))


def exchanged(grad, picked, logs, axes):
    length = lax.axis_size(axes)
    width = grad.shape[-1]
    lines = thirds(logs).reshape(-1, width)
    lines = jnp.broadcast_to(lines[None], (length, *lines.shape))
    sent = jnp.concatenate(
        [grad.reshape(length, -1, width).astype(BF16), picked.reshape(length, -1, width), lines],
        axis=1,
    )
    arrived = lax.all_to_all(sent, axes, 0, 0, tiled=True)
    rows = grad.shape[0] // length
    given = arrived[:, 2 * rows :].astype(F32).reshape(length, 3, -1).sum(axis=1)
    return arrived[:, :rows].astype(F32), arrived[:, rows : 2 * rows], given


def local(hidden, item_table, targets, lengths):
    rows = hidden.shape[0]
    items_local = item_table.shape[0]
    core = lax.axis_index("core")
    group = lax.axis_index("grp")
    half = group.reshape(1).astype(jnp.int32)
    states, target_ids = gathered(hidden, targets)
    weight = weights_for(lengths, rows)
    first_own = lax.axis_index(ITEM) * items_local + group * (items_local // 2)
    target_place = target_ids - first_own
    count = states.shape[0]
    grad, picked, logs = shares(half, target_place, states, item_table)
    part = count // 2
    own_at = core * part
    other_at = part - own_at
    take = lambda x, at: lax.dynamic_slice_in_dim(x, at, part, 1)
    other_logs = from_pair(logs)
    other_grad = from_pair(take(grad, other_at))
    other_picked = from_pair(take(picked, other_at))
    both_logs = merged_logs(jnp.stack([logs, other_logs]))
    scale = lambda x: jnp.exp(take(x, own_at) - take(both_logs, own_at))
    grad = (take(grad, own_at) * scale(logs) + other_grad * scale(other_logs)).T
    picked = (take(picked, own_at) + other_picked).T
    at = own_at
    logs = both_logs.reshape(-1)
    for axes in (PLANE, "z"):
        grads, pickeds, given = exchanged(grad, picked, logs, axes)
        logs = merged_logs(given)
        kept = grads.shape[1]
        at = at + lax.axis_index(axes) * kept
        scale = jnp.exp(
            lax.dynamic_slice_in_dim(given, at, kept, 1) - lax.dynamic_slice_in_dim(logs, at, kept)
        )
        grad = jnp.sum(grads * scale[:, :, None], axis=0)
        picked = jnp.sum(pickeds.astype(F32), axis=0).astype(BF16)
    own_logs = lax.dynamic_slice_in_dim(logs, at, rows)
    own_weight = lax.dynamic_slice_in_dim(weight[0], at, rows)
    picked = picked.astype(F32)
    target_score = jnp.sum(hidden.astype(F32) * picked, axis=1)
    row_loss = own_logs - target_score
    pull = lax.reduce_precision(own_weight * (jnp.exp(target_score - own_logs) - 1.0), 8, 7)
    hidden_grad = (own_weight[:, None] * grad + pull[:, None] * picked).astype(BF16)
    table_grad = table_gradient(half, target_place, logs[None], weight, states, item_table)
    return (row_loss, hidden_grad, table_grad)


def mapped(split):
    return jax.shard_map(
        local,
        mesh=split,
        in_specs=(P(GRP_ITEM, None), P(ITEM, None), P(GRP_ITEM), P()),
        out_specs=(P(GRP_ITEM), P(GRP_ITEM, None), P(ITEM_GRP, None)),
        check_vma=False,
    )


def solution(mesh):
    return mapped(
        Mesh(
            mesh.devices.reshape(4, 2, 8, 2, mesh.shape["grp"]),
            ("x", "yh", "z", "core", "grp"),
        )
    )
```

time: 191 us -> 101 us (0.53)
  blocking collectives: 69.7 us -> 0 us
  Pallas kernels: 0 us -> 22.6 us
  matrix products: 19.2 us -> 0 us
  waiting for transfers between devices: 39.8 us -> 31.7 us
  starting transfers between devices: 33.6 us -> 25.8 us
  local copies, waits for them, and re-layouts: 13.1 us -> 7.49 us
    all_gather x4 -> x0, blocking collectives: 44.2 us -> none  [gathered_once(): both, at, found = (lax.all_gather(jnp.concatenate(lines), axis), 0, {})]
    all_to_all x4 -> x0, blocking collectives: 25.5 us -> none  [the longest x2 17.9 us: sent_and_summed(): lax.all_to_all(blocks, axis, split_axis=0, concat_axis=0, tiled=True)]
    pallas_call x0 -> x2, Pallas kernels: none -> 22.6 us  [the longest x1 13.9 us: shares(): pl.pallas_call(share_kernel, name='shares', out_shape=(jax.ShapeDtypeStru...]
    dot_general x10 -> x0, matrix products: 19.2 us -> none  [the longest x4 9 us: partial_visit(): jnp.einsum('rd,id->ri', states, item_block, preferred_element_type=jnp.fl...]
    all_to_all x5 -> x3, starting transfers between devices: 33.6 us -> 24.5 us  [the longest x1 15.3 us: sent_to_all(): lax.all_to_all(jnp.broadcast_to(x[None], (length, *x.shape)), axes, 0, 0,...]
    all_to_all x5 -> x3, waiting for transfers between devices: 39.8 us -> 31.7 us  [the longest x2 18.2 us: exchanged(): arrived = lax.all_to_all(sent, axes, 0, 0, tiled=True)]
    reduce_sum x8 -> x12, other arithmetic: 6.88 us -> 2.18 us  [the longest x1 0.77 us: weights_for(): starts = jnp.sum(jnp.where(before[None], lengths[:, :, None], 0), axis=1)]
    dynamic_slice x8 -> x3, local copies, waits for them, and re-layouts: 6.16 us -> 2.05 us  [the longest x2 1.97 us: local(): take = lambda x, at: lax.dynamic_slice_in_dim(x, at, part, 1)]
  transfers between devices with their start and end apart: 5 -> 7, of which waited for: 5 -> 3; matrix products, arithmetic and copies ran while one was open for 3% -> 8% of each run, Pallas kernels for 0% -> 0%
where the time goes in v1:
time: 101 us; the launch traced here: 99.8 us
  waiting for transfers between devices  31.7 us (31%)
  starting transfers between devices  25.8 us (26%)
  Pallas kernels  22.6 us (22%)
  other arithmetic  11.3 us (11%)
  local copies, waits for them, and re-layouts  7.49 us (7%)
    all_to_all x2, waiting for transfers between devices, exchanged(): arrived = lax.all_to_all(sent, axes, 0, 0, tiled=True)  18.2 us
    all_to_all x1, starting transfers between devices, sent_to_all(): lax.all_to_all(jnp.broadcast_to(x[None], (length, *x.shape)), axes, 0, 0,...  15.3 us
    pallas_call x1, Pallas kernels, shares(): pl.pallas_call(share_kernel, name='shares', out_shape=(jax.ShapeDtypeStru...  13.9 us
    all_to_all x1, waiting for transfers between devices, sent_to_all(): lax.all_to_all(jnp.broadcast_to(x[None], (length, *x.shape)), axes, 0, 0,...  13.5 us
    all_to_all x2, starting transfers between devices, exchanged(): arrived = lax.all_to_all(sent, axes, 0, 0, tiled=True)  9.15 us
    pallas_call x1, Pallas kernels, table_gradient(): pl.pallas_call(table_kernel, name='table_gradient', out_shape=jax.ShapeDt...  8.67 us
  transfers between devices with their start and end apart: 7, of which 3 were waited for; matrix products, arithmetic and copies ran while one was open for 8% of the time, Pallas kernels for 0%

profile of v1, /device:TPU:8, one launch (start us, length us, event | category | flops | bytes accessed | tf_op | source)
XLA Modules:
  0.0 99.8 jit_solution(5365823107372510792)
XLA Ops:
  0.6 0.7 fusion.57
  1.3 0.1 reshape.316
  1.4 0.7 pad_maximum_fusion.5
  2.1 0.8 broadcast_in_dim.92
  2.9 15.3 %all-to-all-start = ((bf16[128,4,256]{2,1,0:T(4,128)(2,1)}), bf16[128,4,256]{2,1,0:T(4,128)(2,1)S(1)}, u32[]{:S(2)}, u32[]{:S(2)}) async-start(bf16[128,4,256]{2,1,0:T(4,128)(2,1)} %broadcast_in_dim.92), calls=%async_computation | async-start | bytes 524288 | tf_op jit(solution)/shard_map/all_to_all | solution.py:22
  18.3 13.5 %all-to-all-done = bf16[128,4,256]{2,1,0:T(4,128)(2,1)S(1)} async-done(((bf16[128,4,256]{2,1,0:T(4,128)(2,1)}), bf16[128,4,256]{2,1,0:T(4,128)(2,1)S(1)}, u32[]{:S(2)}, u32[]{:S(2)}) %all-to-all-start) | async-done | bytes 262176 | tf_op jit(solution)/shard_map/all_to_all | solution.py:22
  31.8 0.2 copy.33
  32.0 0.1 collective-permute-start
  32.1 0.8 select_reduce_fusion.1
  32.9 0.8 fusion.62
  33.8 0.3 pad_maximum_fusion
  34.0 0.6 copy.36
  34.7 1.1 %reshape.317.states_ref = bf16[768,256]{1,0:T(8,128)(2,1)} reshape(bf16[256,3,256]{2,1,0:T(4,128)(2,1)S(1)} %copy.36) | data formatting | bytes 786432 | tf_op jit(solution)/shard_map/reshape | solution.py:37
  35.8 0.1 copy.35
  35.9 0.8 sub.115.target_ref
  36.7 13.9 %shares.1 = (f32[256,768]{1,0:T(8,128)}, bf16[256,768]{1,0:T(8,128)(2,1)}, f32[1,768]{1,0:T(1,128)}) custom-call(s32[1]{0:T(128)} %bitcast.half_ref, s32[1,768]{1,0:T(1,128)} %sub.115.target_ref, bf16[768,256]{1,0:T(8,128)(2,1)} %reshape.317.states_ref, bf16[8192,256]{1,0:T(8,128)(2,1)} %items_ref.3), custom_call_target="tpu_custom_call" | custom-call | tf_op jit(solution)/shard_map/shares/pallas_call | solution.py:104
  50.7 0.5 collective-permute-start.1
  51.2 0.9 constant_dynamic-slice_fusion.1
  52.1 0.1 collective-permute-start.3
  52.2 1.0 %constant_dynamic-slice_fusion.3 = f32[256,384]{1,0:T(8,128)S(1)} fusion(f32[256,768]{1,0:T(8,128)} %get-tuple-element.35, s32[]{:T(128)S(6)} %select_n.158), kind=kLoop, calls=%fused_computation.125 | loop fusion | bytes 786436 | tf_op jit(solution)/shard_map/dynamic_slice | solution.py:219
  53.2 0.6 collective-permute-start.2
  53.8 0.7 fusion.61
  54.5 0.7 fusion.7
  55.3 0.7 fusion.55
  56.0 1.0 add_bitcast_fusion
  57.0 0.1 copy.38
  57.2 1.1 %fusion = bf16[384,256]{0,1:T(8,128)(2,1)S(1)} fusion(f32[256,384]{1,0:T(8,128)S(1)} %collective-permute-done.2, f32[256,768]{1,0:T(8,128)} %get-tuple-element.35, s32[]{:T(128)S(6)} %select_n.157, f32[384]{0:T(512)S(1)} %get-tuple-element.51, f32[384]{0:T(512)S(1)} %get-tuple-element.50), kind=kLoop, calls=%fused_computation.6 | loop fusion | flops 393216 | bytes 986116 | tf_op jit(solution)/shard_map/convert_element_type | solution.py:195
  58.2 0.1 copy.37
  58.4 0.9 pad_maximum_fusion.1
  59.2 5.8 %all-to-all-start.1 = ((bf16[16,57,256]{2,1,0:T(8,128)(2,1)}), bf16[16,57,256]{2,1,0:T(8,128)(2,1)S(1)}, u32[]{:S(2)}, u32[]{:S(2)}) async-start(bf16[16,57,256]{2,1,0:T(8,128)(2,1)} %pad_maximum_fusion.1), calls=%async_computation.1 | async-start | bytes 1048576 | tf_op jit(solution)/shard_map/all_to_all | solution.py:198
  65.1 0.1 select_reduce_fusion
  65.2 10.5 %all-to-all-done.1 = bf16[16,57,256]{2,1,0:T(8,128)(2,1)S(1)} async-done(((bf16[16,57,256]{2,1,0:T(8,128)(2,1)}), bf16[16,57,256]{2,1,0:T(8,128)(2,1)S(1)}, u32[]{:S(2)}, u32[]{:S(2)}) %all-to-all-start.1) | async-done | bytes 466976 | tf_op jit(solution)/shard_map/all_to_all | solution.py:198
  75.8 0.1 reshape.326
  75.9 0.1 reduce_sum.115
  76.1 0.1 dynamic_slice.46
  76.2 0.1 subtract_exponential_fusion
  76.3 0.1 multiply_reduce_fusion
  76.4 0.7 pad_maximum_fusion.2
  77.1 3.4 %all-to-all-start.2 = ((bf16[8,15,256]{2,1,0:T(8,128)(2,1)}), bf16[8,15,256]{2,1,0:T(8,128)(2,1)S(1)}, u32[]{:S(2)}, u32[]{:S(2)}) async-start(bf16[8,15,256]{2,1,0:T(8,128)(2,1)} %pad_maximum_fusion.2), calls=%async_computation.2 | async-start | bytes 131072 | tf_op jit(solution)/shard_map/all_to_all | solution.py:198
  80.5 0.6 div.79.weight_ref
  81.1 7.7 %all-to-all-done.2 = bf16[8,15,256]{2,1,0:T(8,128)(2,1)S(1)} async-done(((bf16[8,15,256]{2,1,0:T(8,128)(2,1)}), bf16[8,15,256]{2,1,0:T(8,128)(2,1)S(1)}, u32[]{:S(2)}, u32[]{:S(2)}) %all-to-all-start.2) | async-done | bytes 61472 | tf_op jit(solution)/shard_map/all_to_all | solution.py:198
  88.8 0.1 fusion.10
  89.1 0.6 add.199.log_ref
  89.7 0.1 multiply_reduce-precision_fusion
  89.9 0.5 sub.131
  90.4 8.7 %table_gradient.1 = bf16[4096,256]{1,0:T(8,128)(2,1)} custom-call(s32[1]{0:T(128)} %bitcast.half_ref, s32[1,768]{1,0:T(1,128)} %sub.115.target_ref, f32[1,768]{1,0:T(1,128)} %add.199.log_ref, f32[1,768]{1,0:T(1,128)} %div.79.weight_ref, bf16[768,256]{1,0:T(8,128)(2,1)} %reshape.317.states_ref, bf16[8192,256]{1,0:T(8,128)(2,1)} %items_ref.3), custom_call_target="tpu_custom_call" | custom-call | tf_op jit(solution)/shard_map/table_gradient/pallas_call | solution.py:157
  99.0 0.1 multiply_reduce_fusion.1
  99.1 0.7 fusion.12
  (43 shorter events, 0.7 us)
Async XLA Ops:
  2.9 28.9 %all-to-all-start = ((bf16[128,4,256]{2,1,0:T(4,128)(2,1)}), bf16[128,4,256]{2,1,0:T(4,128)(2,1)S(1)}, u32[]{:S(2)}, u32[]{:S(2)}) async-start(bf16[128,4,256]{2,1,0:T(4,128)(2,1)} %broadcast_in_dim.92), calls=%async_computation | async-start | bytes 524288 | tf_op jit(solution)/shard_map/all_to_all | solution.py:22
  32.0 1.6 %collective-permute-start = (bf16[128,4,256]{0,1,2:T(4,128)(2,1)S(1)}, bf16[128,4,256]{0,1,2:T(4,128)(2,1)S(1)}, u32[]{:S(2)}, u32[]{:S(2)}) collective-permute-start(bf16[128,4,256]{0,1,2:T(4,128)(2,1)S(1)} %copy.33), channel_id=1, source_target_pairs={{0,2},{2,0},{1,3},{3,1},{4,6},{6,4},{5,7},{7,5},{8,10},{10,8},{9,1... | collective-permute-start | bytes 786440 | tf_op jit(solution)/shard_map/ppermute | solution.py:26
  50.7 38.1 %copy-start = (bf16[3,256]{1,0:T(4,128)(2,1)S(1)}, bf16[3,256]{1,0:T(4,128)(2,1)}, u32[]{:S(2)}) copy-start(bf16[3,256]{1,0:T(4,128)(2,1)} %param.12) | copy-start | bytes 4612
  50.7 3.2 %collective-permute-start.1 = (f32[1,768]{1,0:T(1,128)}, f32[1,768]{1,0:T(1,128)S(1)}, u32[]{:S(2)}, u32[]{:S(2)}) collective-permute-start(f32[1,768]{1,0:T(1,128)} %get-tuple-element.36), channel_id=1, source_target_pairs={{0,2},{2,0},{1,3},{3,1},{4,6},{6,4},{5,7},{7,5},{8,10},{10,8},{9,1... | collective-permute-start | bytes 9224 | tf_op jit(solution)/shard_map/ppermute | solution.py:26
  52.1 3.9 %collective-permute-start.3 = (bf16[256,384]{1,0:T(8,128)(2,1)S(1)}, bf16[256,384]{1,0:T(8,128)(2,1)S(1)}, u32[]{:S(2)}, u32[]{:S(2)}) collective-permute-start(bf16[256,384]{1,0:T(8,128)(2,1)S(1)} %constant_dynamic-slice_fusion.1), channel_id=1, source_target_pairs={{0,2},{2,0},{1,3},{3,1},{4,6},{6,4},{5,7},{7,5},{8,10},{10,8},{9,1... | collective-permute-start | bytes 589832 | tf_op jit(solution)/shard_map/ppermute | solution.py:26
  53.2 3.9 %collective-permute-start.2 = (f32[256,384]{1,0:T(8,128)S(1)}, f32[256,384]{1,0:T(8,128)S(1)}, u32[]{:S(2)}, u32[]{:S(2)}) collective-permute-start(f32[256,384]{1,0:T(8,128)S(1)} %constant_dynamic-slice_fusion.3), channel_id=1, source_target_pairs={{0,2},{2,0},{1,3},{3,1},{4,6},{6,4},{5,7},{7,5},{8,10},{10,8},{9,1... | collective-permute-start | bytes 1179656 | tf_op jit(solution)/shard_map/ppermute | solution.py:26
  59.2 16.5 %all-to-all-start.1 = ((bf16[16,57,256]{2,1,0:T(8,128)(2,1)}), bf16[16,57,256]{2,1,0:T(8,128)(2,1)S(1)}, u32[]{:S(2)}, u32[]{:S(2)}) async-start(bf16[16,57,256]{2,1,0:T(8,128)(2,1)} %pad_maximum_fusion.1), calls=%async_computation.1 | async-start | bytes 1048576 | tf_op jit(solution)/shard_map/all_to_all | solution.py:198
  77.1 11.7 %all-to-all-start.2 = ((bf16[8,15,256]{2,1,0:T(8,128)(2,1)}), bf16[8,15,256]{2,1,0:T(8,128)(2,1)S(1)}, u32[]{:S(2)}, u32[]{:S(2)}) async-start(bf16[8,15,256]{2,1,0:T(8,128)(2,1)} %pad_maximum_fusion.2), calls=%async_computation.2 | async-start | bytes 131072 | tf_op jit(solution)/shard_map/all_to_all | solution.py:198

commit v2 on v1

v2 whole, which is shorter than its diff:
```python
import functools

import jax
import jax.numpy as jnp
from jax import lax
from jax.experimental import pallas as pl
from jax.experimental.pallas import tpu as pltpu
from jax.sharding import Mesh
from jax.sharding import PartitionSpec as P

ITEM = ("x", "yh", "z", "core")
GRP_ITEM = ("grp", "x", "yh", "z", "core")
ITEM_GRP = ("x", "yh", "z", "core", "grp")
PLANE = ("x", "yh", "grp")
CHIPS = ("x", "yh", "grp", "z")
DIGIT = 128
BLOCK = 512
VMEM_LIMIT = 40 << 20
F32 = jnp.float32
BF16 = jnp.bfloat16


def sent_to_all(x, axes):
    length = lax.axis_size(axes)
    return lax.all_to_all(jnp.broadcast_to(x[None], (length, *x.shape)), axes, 0, 0, tiled=True)


def from_pair(x):
    return lax.ppermute(x, "core", [(0, 1), (1, 0)])


def gathered(hidden, targets):
    rows, width = hidden.shape
    digits = jnp.stack([targets % DIGIT, targets // DIGIT % DIGIT, targets // DIGIT**2])
    digits = jnp.pad(digits.reshape(-1), (0, width - 3 * rows)).astype(BF16)
    mine = sent_to_all(jnp.concatenate([hidden, digits[None]]), CHIPS)
    mine = jnp.swapaxes(mine, 0, 1)
    return mine, from_pair(mine)


def weights_for(lengths, rows):
    groups, seq_count = lengths.shape
    cores, x, yh, grps, z = (lax.axis_size(axis) for axis in ("core", "x", "yh", "grp", "z"))
    half, k, at_x, at_yh, at_grp, at_z = jnp.unravel_index(
        jnp.arange(cores * rows * x * yh * grps * z), (cores, rows, x, yh, grps, z)
    )
    core = (half + lax.axis_index("core")) % cores
    place = (((at_x * yh + at_yh) * z + at_z) * cores + core) * rows + k
    group_rows = place.shape[0] // groups
    before = jnp.arange(seq_count)[:, None] < jnp.arange(seq_count)[None, :]
    starts = jnp.sum(jnp.where(before[None], lengths[:, :, None], 0), axis=1)
    inside = (
        (at_grp[:, None, None] == jnp.arange(groups)[None, :, None])
        & (place[:, None, None] >= starts[None])
        & (place[:, None, None] < (starts + lengths)[None])
    )
    row_length = jnp.sum(jnp.where(inside, lengths[None].astype(F32), F32(0.0)), axis=(1, 2))
    return (group_rows / seq_count / row_length).reshape(1, -1)


def column(line):
    return jnp.broadcast_to(line, (128, line.shape[1])).T[:, :1]


def share_kernel(
    first_ref, mine_ref, other_ref, items_ref,
    own_grad_ref, other_grad_ref, own_rows_ref, other_rows_ref, log_ref, place_ref, states_ref,
    scores, places, grad, picked,
):
    rows = mine_ref.shape[0] - 1
    chips = mine_ref.shape[1]
    count, width = states_ref.shape
    items = items_ref.shape[0]
    part = count // 2
    block = min(BLOCK, items)
    lanes = min(128, block)
    for half, ref in enumerate((mine_ref, other_ref)):
        digits = ref[rows].astype(F32)
        across = digits.T
        for k in range(rows):
            at = half * part + k * chips
            states_ref[at : at + chips, :] = ref[k]
            found = [digits[:, j * rows + k : j * rows + k + 1].astype(jnp.int32) for j in range(3)]
            found = found[0] + DIGIT * found[1] + DIGIT**2 * found[2] - first_ref[0]
            places[at : at + chips, :] = jnp.broadcast_to(found, (chips, lanes))
            found = [across[j * rows + k : j * rows + k + 1, :].astype(jnp.int32) for j in range(3)]
            found = found[0] + DIGIT * found[1] + DIGIT**2 * found[2] - first_ref[0]
            place_ref[:, at : at + chips] = found
    states = states_ref[...]
    high = None
    for at in range(0, items, block):
        found = lax.dot_general(
            states, items_ref[at : at + block, :], (((1,), (1,)), ((), ())), preferred_element_type=F32
        )
        scores[:, at : at + block] = found
        for c in range(0, block, lanes):
            top = found[:, c : c + lanes]
            high = top if high is None else jnp.maximum(high, top)
    high = jnp.max(high, axis=1, keepdims=True)
    total = None
    lane = lax.broadcasted_iota(jnp.int32, (count, lanes), 1)
    for at in range(0, items, block):
        others, hot = [], []
        for c in range(at, at + block, lanes):
            parts = jnp.exp(scores[:, c : c + lanes] - high)
            total = parts if total is None else total + parts
            matched = places[...] == lane + c
            others.append(jnp.where(matched, 0.0, parts).astype(BF16))
            hot.append(jnp.where(matched, 1.0, 0.0).astype(BF16))
        table = items_ref[at : at + block, :]
        more = jnp.dot(jnp.concatenate(others, axis=1), table, preferred_element_type=F32)
        grad[...] = more if at == 0 else grad[...] + more
        more = jnp.dot(jnp.concatenate(hot, axis=1), table, preferred_element_type=F32)
        picked[...] = more if at == 0 else picked[...] + more
    log_sum = high + jnp.log(jnp.sum(total, axis=1, keepdims=True))
    log_ref[...] = jnp.broadcast_to(log_sum, (count, 128)).T[:1, :]
    share = grad[...] * jnp.exp(high - log_sum)
    own_grad_ref[...] = share[:part]
    other_grad_ref[...] = share[part:]
    own_rows_ref[...] = picked[:part, :].astype(BF16)
    other_rows_ref[...] = picked[part:, :].astype(BF16)


def in_vmem(count):
    return [pl.BlockSpec(memory_space=pltpu.VMEM) for _ in range(count)]


def shares(first, mine, other, items):
    rows, chips, width = mine.shape
    part = (rows - 1) * chips
    count = 2 * part
    return pl.pallas_call(
        share_kernel,
        name="shares",
        out_shape=(
            jax.ShapeDtypeStruct((part, width), F32),
            jax.ShapeDtypeStruct((part, width), F32),
            jax.ShapeDtypeStruct((part, width), BF16),
            jax.ShapeDtypeStruct((part, width), BF16),
            jax.ShapeDtypeStruct((1, count), F32),
            jax.ShapeDtypeStruct((1, count), jnp.int32),
            jax.ShapeDtypeStruct((count, width), BF16),
        ),
        in_specs=[pl.BlockSpec(memory_space=pltpu.SMEM), *in_vmem(3)],
        out_specs=in_vmem(7),
        scratch_shapes=[
            pltpu.VMEM((count, items.shape[0]), F32),
            pltpu.VMEM((count, min(128, items.shape[0])), jnp.int32),
            pltpu.VMEM((count, width), F32),
            pltpu.VMEM((count, width), F32),
        ],
        compiler_params=pltpu.CompilerParams(vmem_limit_bytes=VMEM_LIMIT),
    )(first, mine, other, items)


def three_parts(x):
    high = x.astype(BF16).astype(F32)
    rest = x - high
    middle = rest.astype(BF16).astype(F32)
    return [high, middle, rest - middle]


def pack_kernel(rows, own_grad_ref, other_grad_ref, own_rows_ref, other_rows_ref, own_log_ref, other_log_ref, out_ref):
    length, _, width = out_ref.shape
    part = own_grad_ref.shape[0]
    own = own_log_ref[...]
    other = jnp.concatenate([other_log_ref[:, part:], other_log_ref[:, :part]], axis=1)
    top = jnp.maximum(own, other)
    both = top + jnp.log(jnp.exp(own - top) + jnp.exp(other - top))
    grad = own_grad_ref[...] * column(jnp.exp(own - both)[:, :part])
    grad += other_grad_ref[...] * column(jnp.exp(other - both)[:, :part])
    picked = own_rows_ref[...].astype(F32) + other_rows_ref[...].astype(F32)
    lines = [
        piece[:, at : at + width] for piece in three_parts(both) for at in range(0, 2 * part, width)
    ]
    lines = jnp.concatenate(lines + [jnp.zeros((-len(lines) % 8, width), F32)])
    across = lambda x: [
        x.reshape(rows, length, -1, width)[k] for k in range(rows)
    ]
    sent = across(grad) + across(picked) + [jnp.broadcast_to(lines[None], (length, *lines.shape))]
    out_ref[...] = jnp.concatenate(sent, axis=1).astype(BF16)


def packed(rows, length, *pieces):
    part, width = pieces[0].shape
    lines = 3 * 2 * part // width
    height = 2 * (part // length) + lines + -lines % 8
    return pl.pallas_call(
        functools.partial(pack_kernel, rows),
        name="packed",
        out_shape=jax.ShapeDtypeStruct((length, height, width), BF16),
        in_specs=in_vmem(6),
        out_specs=pl.BlockSpec(memory_space=pltpu.VMEM),
        compiler_params=pltpu.CompilerParams(vmem_limit_bytes=VMEM_LIMIT),
    )(*pieces)


def table_kernel(place_ref, log_ref, weight_ref, states_ref, items_ref, out_ref, *scratch):
    buffers, sems = scratch
    items = items_ref.shape[0]
    block = min(BLOCK, items)
    copies = []
    for step, at in enumerate(range(0, items, block)):
        scores = lax.dot_general(
            items_ref[at : at + block, :], states_ref[...], (((1,), (1,)), ((), ())),
            preferred_element_type=F32,
        )
        parts = jnp.exp(scores - log_ref[...])
        matched = lax.broadcasted_iota(jnp.int32, parts.shape, 0) == place_ref[...] - at
        signal = (weight_ref[...] * jnp.where(matched, parts - 1.0, parts)).astype(BF16)
        buffers[at : at + block, :] = jnp.dot(
            signal, states_ref[...], preferred_element_type=F32
        ).astype(BF16)
        copies.append(
            pltpu.make_async_copy(
                buffers.at[pl.ds(at, block)], out_ref.at[pl.ds(at, block)], sems.at[step]
            )
        )
        copies[-1].start()
    for copy in copies:
        copy.wait()


def table_gradient(place, log_total, weight, states, items):
    return pl.pallas_call(
        table_kernel,
        name="table_gradient",
        out_shape=jax.ShapeDtypeStruct(items.shape, BF16),
        in_specs=in_vmem(5),
        out_specs=pl.BlockSpec(memory_space=pl.ANY),
        scratch_shapes=[
            pltpu.VMEM(items.shape, BF16),
            pltpu.SemaphoreType.DMA((items.shape[0] // min(BLOCK, items.shape[0]),)),
        ],
        compiler_params=pltpu.CompilerParams(vmem_limit_bytes=VMEM_LIMIT),
    )(place, log_total, weight, states, items)


def thirds(x):
    high = lax.reduce_precision(x, 8, 7)
    rest = x - high
    middle = lax.reduce_precision(rest, 8, 7)
    return jnp.concatenate([high, middle, rest - middle]).astype(BF16)


def merged_logs(parts):
    top = jnp.max(parts, axis=0)
    return top + jnp.log(jnp.sum(jnp.exp(parts - top[None]), axis=0))


def merged(arrived, kept, count, own):
    length, _, width = arrived.shape
    given = arrived[:, 2 * kept : 2 * kept + 3 * count // width]
    given = given.astype(F32).reshape(length, 3, count).sum(axis=1)
    logs = merged_logs(given)
    scale = jnp.exp(own(given) - own(logs[None]))
    grad = jnp.sum(arrived[:, :kept].astype(F32) * scale[:, :, None], axis=0)
    picked = jnp.sum(arrived[:, kept : 2 * kept].astype(F32), axis=0)
    return grad, picked, logs


def local(hidden, item_table, targets, lengths):
    rows, width = hidden.shape
    group = lax.axis_index("grp")
    own_items = item_table.shape[0] // 2
    items = lax.dynamic_slice_in_dim(item_table, group * own_items, own_items)
    first_own = (lax.axis_index(ITEM) * 2 + group) * own_items
    plane, depth = lax.axis_size(PLANE), lax.axis_size("z")
    weight = weights_for(lengths, rows)
    mine, other = gathered(hidden, targets)
    own_grad, other_grad, own_picked, other_picked, logs, place, states = shares(
        first_own.reshape(1).astype(jnp.int32), mine, other, items
    )
    count = states.shape[0]
    sent = packed(
        rows, plane, own_grad, from_pair(other_grad), own_picked, from_pair(other_picked),
        logs, from_pair(logs),
    )
    arrived = lax.all_to_all(sent, PLANE, 0, 0, tiled=True)
    in_plane = lambda x: lax.dynamic_index_in_dim(
        x.reshape(x.shape[0], 2, rows, plane, depth)[:, 0], lax.axis_index(PLANE), 2, False
    )
    grad, picked, logs = merged(
        arrived, rows * depth, count, lambda x: in_plane(x).reshape(x.shape[0], -1)
    )
    by_depth = lambda x: jnp.swapaxes(x.reshape(rows, depth, width), 0, 1).astype(BF16)
    lines = thirds(logs).reshape(-1, width)
    lines = jnp.broadcast_to(lines[None], (depth, *lines.shape))
    sent = jnp.concatenate([by_depth(grad), by_depth(picked), lines], axis=1)
    arrived = lax.all_to_all(sent, "z", 0, 0, tiled=True)
    own = lambda x: lax.dynamic_index_in_dim(in_plane(x), lax.axis_index("z"), 2, False)
    grad, picked, logs = merged(arrived, rows, count, own)
    own_logs = own(logs[None])[0]
    own_weight = own(weight)[0]
    target_score = jnp.sum(hidden.astype(F32) * picked, axis=1)
    row_loss = own_logs - target_score
    pull = lax.reduce_precision(own_weight * (jnp.exp(target_score - own_logs) - 1.0), 8, 7)
    hidden_grad = (own_weight[:, None] * grad + pull[:, None] * picked).astype(BF16)
    table_grad = table_gradient(place, logs[None], weight, states, items)
    return (row_loss, hidden_grad, table_grad)


def mapped(split):
    return jax.shard_map(
        local,
        mesh=split,
        in_specs=(P(GRP_ITEM, None), P(ITEM, None), P(GRP_ITEM), P()),
        out_specs=(P(GRP_ITEM), P(GRP_ITEM, None), P(ITEM_GRP, None)),
        check_vma=False,
    )


def solution(mesh):
    return mapped(
        Mesh(
            mesh.devices.reshape(4, 2, 8, 2, mesh.shape["grp"]),
            ("x", "yh", "z", "core", "grp"),
        )
    )
```

time: 101 us -> 82.9 us (0.82)
  Pallas kernels: 22.6 us -> 12.2 us
  other arithmetic: 11.3 us -> 5.09 us
  local copies, waits for them, and re-layouts: 7.49 us -> 4.98 us
  waiting for transfers between devices: 31.7 us -> 33.2 us
    pallas_call x1, Pallas kernels: 13.9 us -> 6.57 us  [shares(): pl.pallas_call(share_kernel, name='shares', out_shape=(jax.ShapeDtypeStru...]
    pallas_call x1, Pallas kernels: 8.67 us -> 4.46 us  [table_gradient(): pl.pallas_call(table_kernel, name='table_gradient', out_shape=jax.ShapeDt...]
    pallas_call x0 -> x1, Pallas kernels: none -> 1.18 us  [packed(): pl.pallas_call(functools.partial(pack_kernel, rows), name='packed', out_s...]
    concatenate x3 -> x1, other arithmetic: 1.8 us -> 0.68 us  [local(): sent = jnp.concatenate([by_depth(grad), by_depth(picked), lines], axis=1)]
    convert_element_type x2 -> x0, other arithmetic: 1.1 us -> none  [the longest x1 1.06 us: exchanged(): grad.reshape(length, -1, width).astype(BF16)]
    dynamic_slice x3 -> x6, local copies, waits for them, and re-layouts: 2.05 us -> 2.32 us  [the longest x1 1.73 us: local(): items = lax.dynamic_slice_in_dim(item_table, group * own_items, own_items)]
  transfers between devices with their start and end apart: 7 -> 7, of which waited for: 3 -> 4; matrix products, arithmetic and copies ran while one was open for 8% -> 3% of each run, Pallas kernels for 0% -> 0%
where the time goes in v2:
time: 82.9 us; the launch traced here: 82.4 us
  waiting for transfers between devices  33.2 us (40%)
  starting transfers between devices  25.7 us (31%)
  Pallas kernels  12.2 us (15%)
  other arithmetic  5.09 us (6%)
  local copies, waits for them, and re-layouts  4.98 us (6%)
  between operations  1.15 us (1%)
    all_to_all x1, starting transfers between devices, sent_to_all(): lax.all_to_all(jnp.broadcast_to(x[None], (length, *x.shape)), axes, 0, 0,...  15.3 us
    all_to_all x1, waiting for transfers between devices, sent_to_all(): lax.all_to_all(jnp.broadcast_to(x[None], (length, *x.shape)), axes, 0, 0,...  13.5 us
    all_to_all x1, waiting for transfers between devices, local(): arrived = lax.all_to_all(sent, PLANE, 0, 0, tiled=True)  10.8 us
    all_to_all x1, waiting for transfers between devices, local(): arrived = lax.all_to_all(sent, 'z', 0, 0, tiled=True)  7.98 us
    pallas_call x1, Pallas kernels, shares(): pl.pallas_call(share_kernel, name='shares', out_shape=(jax.ShapeDtypeStru...  6.57 us
    all_to_all x1, starting transfers between devices, local(): arrived = lax.all_to_all(sent, PLANE, 0, 0, tiled=True)  5.8 us
    pallas_call x1, Pallas kernels, table_gradient(): pl.pallas_call(table_kernel, name='table_gradient', out_shape=jax.ShapeDt...  4.46 us
    all_to_all x1, starting transfers between devices, local(): arrived = lax.all_to_all(sent, 'z', 0, 0, tiled=True)  3.35 us
  transfers between devices with their start and end apart: 7, of which 4 were waited for; matrix products, arithmetic and copies ran while one was open for 3% of the time, Pallas kernels for 0%

profile of v2, /device:TPU:8, one launch (start us, length us, event | category | flops | bytes accessed | tf_op | source)
XLA Modules:
  0.0 82.4 jit_solution(3684663377443260098)
XLA Ops:
  0.6 0.7 fusion.45
  1.3 0.1 reshape.268
  1.4 0.7 pad_maximum_fusion.2
  2.1 0.8 broadcast_in_dim.83
  2.9 15.3 %all-to-all-start = ((bf16[128,4,256]{2,1,0:T(4,128)(2,1)}), bf16[128,4,256]{2,1,0:T(4,128)(2,1)S(1)}, u32[]{:S(2)}, u32[]{:S(2)}) async-start(bf16[128,4,256]{2,1,0:T(4,128)(2,1)} %broadcast_in_dim.83), calls=%async_computation | async-start | bytes 524288 | tf_op jit(solution)/shard_map/all_to_all | solution.py:25
  18.3 13.5 %all-to-all-done = bf16[128,4,256]{2,1,0:T(4,128)(2,1)S(1)} async-done(((bf16[128,4,256]{2,1,0:T(4,128)(2,1)}), bf16[128,4,256]{2,1,0:T(4,128)(2,1)S(1)}, u32[]{:S(2)}, u32[]{:S(2)}) %all-to-all-start) | async-done | bytes 262176 | tf_op jit(solution)/shard_map/all_to_all | solution.py:25
  31.8 0.1 collective-permute-start
  31.9 1.7 %constant_dynamic-slice_fusion.1.items_ref = bf16[4096,256]{1,0:T(8,128)(2,1)S(1)} fusion(bf16[8192,256]{1,0:T(8,128)(2,1)} %param.13, s32[]{:T(128)S(6)} %select_n.132), kind=kLoop, calls=%fused_computation.118 | loop fusion | bytes 4194308 | tf_op jit(solution)/shard_map/dynamic_slice | solution.py:266
  33.6 0.0 copy-start.1
  33.7 6.6 %shares.1 = (f32[384,256]{1,0:T(8,128)S(1)}, f32[384,256]{1,0:T(8,128)S(1)}, bf16[384,256]{1,0:T(8,128)(2,1)S(1)}, bf16[384,256]{1,0:T(8,128)(2,1)S(1)}, f32[1,7...) custom-call(s32[1]{0:T(128)} %bitcast.first_ref, bf16[4,128,256]{2,1,0:T(8,128)(2,1)S(1)} %bitcast.28, ...), custom_call_target="tpu_custom_call" | custom-call | tf_op jit(solution)/shard_map/shares/pallas_call | solution.py:132
  40.2 0.6 collective-permute-start.1
  40.8 0.1 select_reduce_fusion.1
  40.9 0.1 collective-permute-start.2
  41.0 0.5 collective-permute-start.3
  41.5 0.9 %collective-permute-done.3.other_log_ref = f32[1,768]{1,0:T(1,128)S(1)} collective-permute-done((f32[1,768]{1,0:T(1,128)S(1)}, f32[1,768]{1,0:T(1,128)S(1)}, u32[]{:S(2)}, u32[]{:S(2)}) %collective-permute-start.3) | collective-permute-done | bytes 3104 | tf_op jit(solution)/shard_map/ppermute | solution.py:29
  42.4 1.2 %packed.1 = bf16[16,64,256]{2,1,0:T(8,128)(2,1)} custom-call(f32[384,256]{1,0:T(8,128)S(1)} %get-tuple-element.40.own_grad_ref, f32[384,256]{1,0:T(8,128)S(1)} %collective-permute-done.1.other_grad_ref, bf16[384,256]{1,0:T(8,128)(2,1)S(1)} %get-tuple-element.42.own_rows_ref, bf16[384,256]{1,0:T(8,128)(2,1)S(1)} %collective-permute-done.2.other_rows_ref, ...), custom_call_target="tpu_custom_call" | custom-call | tf_op jit(solution)/shard_map/packed/pallas_call | solution.py:188
  43.6 5.8 %all-to-all-start.1 = ((bf16[16,64,256]{2,1,0:T(8,128)(2,1)}), bf16[16,64,256]{2,1,0:T(8,128)(2,1)S(1)}, u32[]{:S(2)}, u32[]{:S(2)}) async-start(bf16[16,64,256]{2,1,0:T(8,128)(2,1)} %packed.1), calls=%async_computation.1 | async-start | bytes 1048576 | tf_op jit(solution)/shard_map/all_to_all | solution.py:279
  49.4 0.1 fusion.11
  49.5 0.1 select_reduce_fusion
  49.7 10.8 %all-to-all-done.1 = bf16[16,64,256]{2,1,0:T(8,128)(2,1)S(1)} async-done(((bf16[16,64,256]{2,1,0:T(8,128)(2,1)}), bf16[16,64,256]{2,1,0:T(8,128)(2,1)S(1)}, u32[]{:S(2)}, u32[]{:S(2)}) %all-to-all-start.1) | async-done | bytes 524320 | tf_op jit(solution)/shard_map/all_to_all | solution.py:279
  60.5 0.1 reshape.277
  60.6 0.0 copy-start
  60.6 0.1 reduce_sum.102
  60.7 0.2 copy.26
  61.0 0.1 add.186
  61.1 0.7 slice.47
  61.8 0.1 sub.87
  61.9 0.8 fusion
  62.7 0.1 copy.27
  62.8 0.1 multiply_reduce_fusion
  63.0 0.7 pad_maximum_fusion
  63.6 3.4 %all-to-all-start.2 = ((bf16[8,15,256]{2,1,0:T(8,128)(2,1)}), bf16[8,15,256]{2,1,0:T(8,128)(2,1)S(1)}, u32[]{:S(2)}, u32[]{:S(2)}) async-start(bf16[8,15,256]{2,1,0:T(8,128)(2,1)} %pad_maximum_fusion), calls=%async_computation.2 | async-start | bytes 131072 | tf_op jit(solution)/shard_map/all_to_all | solution.py:290
  67.0 0.1 div.89
  67.1 0.2 dynamic-slice_reduce_fusion
  67.3 8.0 %all-to-all-done.2 = bf16[8,15,256]{2,1,0:T(8,128)(2,1)S(1)} async-done(((bf16[8,15,256]{2,1,0:T(8,128)(2,1)}), bf16[8,15,256]{2,1,0:T(8,128)(2,1)S(1)}, u32[]{:S(2)}, u32[]{:S(2)}) %all-to-all-start.2) | async-done | bytes 61472 | tf_op jit(solution)/shard_map/all_to_all | solution.py:290
  75.4 0.1 reduce_sum.106
  75.4 0.2 reshape.275
  75.7 0.1 add.189
  75.8 0.1 constant_dynamic-slice_fusion
  76.0 0.1 copy.30
  76.1 0.2 dynamic-slice_reduce_fusion.1
  76.2 0.1 fusion.43
  76.3 0.1 copy.31
  76.4 0.1 multiply_reduce_fusion.1
  76.5 0.1 multiply_reduce_fusion.2
  76.6 0.5 multiply_reduce-precision_fusion
  77.1 0.7 add_convert_fusion
  77.8 4.5 %table_gradient.1 = bf16[4096,256]{1,0:T(8,128)(2,1)} custom-call(s32[1,768]{1,0:T(1,128)S(1)} %get-tuple-element.57.place_ref, f32[1,768]{1,0:T(1,128)S(1)} %add.200.log_ref, f32[1,768]{1,0:T(1,128)S(1)} %div.90.weight_ref, bf16[768,256]{1,0:T(8,128)(2,1)S(1)} %get-tuple-element.58.states_ref, bf16[4096,256]{1,0:T(8,128)(2,1)S(1)} %constant_dynamic-slice_fusion.1.items_ref), custom_call_target="tpu_custom_call" | custom-call | tf_op jit(solution)/shard_map/table_gradient/pallas_call | solution.py:225
  (37 shorter events, 0.4 us)
Async XLA Ops:
  2.9 28.9 %all-to-all-start = ((bf16[128,4,256]{2,1,0:T(4,128)(2,1)}), bf16[128,4,256]{2,1,0:T(4,128)(2,1)S(1)}, u32[]{:S(2)}, u32[]{:S(2)}) async-start(bf16[128,4,256]{2,1,0:T(4,128)(2,1)} %broadcast_in_dim.83), calls=%async_computation | async-start | bytes 524288 | tf_op jit(solution)/shard_map/all_to_all | solution.py:25
  31.8 1.9 %collective-permute-start = (bf16[4,128,256]{2,1,0:T(8,128)(2,1)S(1)}, bf16[4,128,256]{2,1,0:T(8,128)(2,1)S(1)}, u32[]{:S(2)}, u32[]{:S(2)}) collective-permute-start(bf16[4,128,256]{2,1,0:T(8,128)(2,1)S(1)} %bitcast.27), channel_id=1, source_target_pairs={{0,2},{2,0},{1,3},{3,1},{4,6},{6,4},{5,7},{7,5},{8,10},{10,8},{9,1... | collective-permute-start | bytes 786440 | tf_op jit(solution)/shard_map/ppermute | solution.py:29
  33.6 7.2 %copy-start.1 = (s32[2,16]{1,0:T(2,128)S(1)}, s32[2,16]{1,0:T(2,128)}, u32[]{:S(2)}) copy-start(s32[2,16]{1,0:T(2,128)} %param.15) | copy-start | bytes 388
  40.2 2.2 %collective-permute-start.1 = (f32[384,256]{1,0:T(8,128)S(1)}, f32[384,256]{1,0:T(8,128)S(1)}, u32[]{:S(2)}, u32[]{:S(2)}) collective-permute-start(f32[384,256]{1,0:T(8,128)S(1)} %get-tuple-element.41), channel_id=1, source_target_pairs={{0,2},{2,0},{1,3},{3,1},{4,6},{6,4},{5,7},{7,5},{8,10},{10,8},{9,1... | collective-permute-start | bytes 1179656 | tf_op jit(solution)/shard_map/ppermute | solution.py:29
  40.9 1.5 %collective-permute-start.2 = (bf16[384,256]{1,0:T(8,128)(2,1)S(1)}, bf16[384,256]{1,0:T(8,128)(2,1)S(1)}, u32[]{:S(2)}, u32[]{:S(2)}) collective-permute-start(bf16[384,256]{1,0:T(8,128)(2,1)S(1)} %get-tuple-element.43), channel_id=1, source_target_pairs={{0,2},{2,0},{1,3},{3,1},{4,6},{6,4},{5,7},{7,5},{8,10},{10,8},{9,1... | collective-permute-start | bytes 589832 | tf_op jit(solution)/shard_map/ppermute | solution.py:29
  41.0 1.4 %collective-permute-start.3 = (f32[1,768]{1,0:T(1,128)S(1)}, f32[1,768]{1,0:T(1,128)S(1)}, u32[]{:S(2)}, u32[]{:S(2)}) collective-permute-start(f32[1,768]{1,0:T(1,128)S(1)} %get-tuple-element.44.own_log_ref), channel_id=1, source_target_pairs={{0,2},{2,0},{1,3},{3,1},{4,6},{6,4},{5,7},{7,5},{8,10},{10,8},{9,1... | collective-permute-start | bytes 9224 | tf_op jit(solution)/shard_map/ppermute | solution.py:29
  43.6 16.8 %all-to-all-start.1 = ((bf16[16,64,256]{2,1,0:T(8,128)(2,1)}), bf16[16,64,256]{2,1,0:T(8,128)(2,1)S(1)}, u32[]{:S(2)}, u32[]{:S(2)}) async-start(bf16[16,64,256]{2,1,0:T(8,128)(2,1)} %packed.1), calls=%async_computation.1 | async-start | bytes 1048576 | tf_op jit(solution)/shard_map/all_to_all | solution.py:279
  60.6 15.9 %copy-start = (bf16[3,256]{1,0:T(4,128)(2,1)S(1)}, bf16[3,256]{1,0:T(4,128)(2,1)}, u32[]{:S(2)}) copy-start(bf16[3,256]{1,0:T(4,128)(2,1)} %param.12) | copy-start | bytes 4612
  63.6 11.7 %all-to-all-start.2 = ((bf16[8,15,256]{2,1,0:T(8,128)(2,1)}), bf16[8,15,256]{2,1,0:T(8,128)(2,1)S(1)}, u32[]{:S(2)}, u32[]{:S(2)}) async-start(bf16[8,15,256]{2,1,0:T(8,128)(2,1)} %pad_maximum_fusion), calls=%async_computation.2 | async-start | bytes 131072 | tf_op jit(solution)/shard_map/all_to_all | solution.py:290

commit v3 on v2

--- a/solution.py
+++ b/solution.py
@@ -1,5 +1,3 @@
-import functools
-
 import jax
 import jax.numpy as jnp
 from jax import lax
@@ -15,27 +13,43 @@
 CHIPS = ("x", "yh", "grp", "z")
 DIGIT = 128
 BLOCK = 512
-VMEM_LIMIT = 40 << 20
+MIB = 1 << 20
 F32 = jnp.float32
 BF16 = jnp.bfloat16
 
 
-def sent_to_all(x, axes):
-    length = lax.axis_size(axes)
-    return lax.all_to_all(jnp.broadcast_to(x[None], (length, *x.shape)), axes, 0, 0, tiled=True)
-
-
 def from_pair(x):
     return lax.ppermute(x, "core", [(0, 1), (1, 0)])
 
 
-def gathered(hidden, targets):
+def spread_kernel(targets_ref, hidden_ref, out_ref):
+    _, height, width = out_ref.shape
+    rows = height - 1
+    lane = lax.broadcasted_iota(jnp.int32, (1, width), 1)
+    digits = jnp.zeros((1, width), jnp.int32)
+    for k in range(rows):
+        rest = targets_ref[k]
+        for j in range(3):
+            digits = jnp.where(lane == j * rows + k, rest % DIGIT, digits)
+            rest = rest // DIGIT
+    line = jnp.concatenate([hidden_ref[...].astype(F32), digits.astype(F32)])
+    out_ref[...] = jnp.broadcast_to(line[None], out_ref.shape).astype(BF16)
+
+
+def spread(hidden, targets, chips):
     rows, width = hidden.shape
-    digits = jnp.stack([targets % DIGIT, targets // DIGIT % DIGIT, targets // DIGIT**2])
-    digits = jnp.pad(digits.reshape(-1), (0, width - 3 * rows)).astype(BF16)
-    mine = sent_to_all(jnp.concatenate([hidden, digits[None]]), CHIPS)
-    mine = jnp.swapaxes(mine, 0, 1)
-    return mine, from_pair(mine)
+    return pl.pallas_call(
+        spread_kernel,
+        name="spread",
+        out_shape=jax.ShapeDtypeStruct((chips, rows + 1, width), BF16),
+        in_specs=[pl.BlockSpec(memory_space=pltpu.SMEM), *in_vmem(1)],
+        out_specs=pl.BlockSpec(memory_space=pltpu.VMEM),
+        compiler_params=pltpu.CompilerParams(vmem_limit_bytes=4 * MIB),
+    )(targets, hidden)
+
+
+def in_vmem(count):
+    return [pl.BlockSpec(memory_space=pltpu.VMEM) for _ in range(count)]
 
 
 def weights_for(lengths, rows):
@@ -69,7 +83,7 @@
 ):
     rows = mine_ref.shape[0] - 1
     chips = mine_ref.shape[1]
-    count, width = states_ref.shape
+    count, _ = states_ref.shape
     items = items_ref.shape[0]
     part = count // 2
     block = min(BLOCK, items)
@@ -121,10 +135,6 @@
     other_rows_ref[...] = picked[part:, :].astype(BF16)
 
 
-def in_vmem(count):
-    return [pl.BlockSpec(memory_space=pltpu.VMEM) for _ in range(count)]
-
-
 def shares(first, mine, other, items):
     rows, chips, width = mine.shape
     part = (rows - 1) * chips
@@ -149,7 +159,7 @@
             pltpu.VMEM((count, width), F32),
             pltpu.VMEM((count, width), F32),
         ],
-        compiler_params=pltpu.CompilerParams(vmem_limit_bytes=VMEM_LIMIT),
+        compiler_params=pltpu.CompilerParams(vmem_limit_bytes=32 * MIB),
     )(first, mine, other, items)
 
 
@@ -160,11 +170,21 @@
     return [high, middle, rest - middle]
 
 
+def swapped(x):
+    part = x.shape[1] // 2
+    return jnp.concatenate([x[:, part:], x[:, :part]], axis=1)
+
+
+def swapped(x):
+    part = x.shape[1] // 2
+    return jnp.concatenate([x[:, part:], x[:, :part]], axis=1)
+
+
 def pack_kernel(rows, own_grad_ref, other_grad_ref, own_rows_ref, other_rows_ref, own_log_ref, other_log_ref, out_ref):
     length, _, width = out_ref.shape
     part = own_grad_ref.shape[0]
     own = own_log_ref[...]
-    other = jnp.concatenate([other_log_ref[:, part:], other_log_ref[:, :part]], axis=1)
+    other = swapped(other_log_ref[...])
     top = jnp.maximum(own, other)
     both = top + jnp.log(jnp.exp(own - top) + jnp.exp(other - top))
     grad = own_grad_ref[...] * column(jnp.exp(own - both)[:, :part])
@@ -186,123 +206,183 @@
     lines = 3 * 2 * part // width
     height = 2 * (part // length) + lines + -lines % 8
     return pl.pallas_call(
-        functools.partial(pack_kernel, rows),
+        lambda *refs: pack_kernel(rows, *refs),
         name="packed",
         out_shape=jax.ShapeDtypeStruct((length, height, width), BF16),
         in_specs=in_vmem(6),
         out_specs=pl.BlockSpec(memory_space=pltpu.VMEM),
-        compiler_params=pltpu.CompilerParams(vmem_limit_bytes=VMEM_LIMIT),
+        compiler_params=pltpu.CompilerParams(vmem_limit_bytes=12 * MIB),
     )(*pieces)
 
 
-def table_kernel(place_ref, log_ref, weight_ref, states_ref, items_ref, out_ref, *scratch):
-    buffers, sems = scratch
+def merged(arrived_ref, at, wide):
+    lines = arrived_ref[...].astype(F32)
+    parts = sum(lines[:, at + j * wide : at + (j + 1) * wide] for j in range(3))
+    top = jnp.max(parts, axis=0)
+    logs = top + jnp.log(jnp.sum(jnp.exp(parts - top[None]), axis=0))
+    return lines, jnp.exp(parts - logs[None]), logs
+
+
+def middle_kernel(rows, plane_ref, arrived_ref, out_ref, turned, built):
+    length = arrived_ref.shape[0]
+    depth, height, width = out_ref.shape
+    chips = length * depth
+    wide = 2 * rows * chips // width
+    kept = rows * depth
+    lines, scale, logs = merged(arrived_ref, 2 * kept, wide)
+    scale = scale.reshape(length * wide, width)
+    pad = jnp.zeros((-(length * wide) % 128, width), F32)
+    turned[...] = jnp.concatenate([scale, pad]).T
+    for k in range(rows):
+        c, lane = k * chips // width, k * chips % width
+        across = turned[pl.ds(pl.multiple_of(plane_ref[0] * depth + lane, depth), depth), :]
+        grad = jnp.zeros((depth, width), F32)
+        picked = jnp.zeros((depth, width), F32)
+        for j in range(length):
+            at = j * wide + c
+            grad += lines[j, k * depth : (k + 1) * depth] * across[:, at : at + 1]
+            picked += lines[j, kept + k * depth : kept + (k + 1) * depth]
+        for z in range(depth):
+            built[z, k : k + 1, :] = grad[z : z + 1]
+            built[z, rows + k : rows + k + 1, :] = picked[z : z + 1]
+    lines = jnp.concatenate(three_parts(logs))
+    at = 2 * rows
+    built[:, at : at + 3 * wide, :] = jnp.broadcast_to(lines[None], (depth, 3 * wide, width))
+    at += 3 * wide
+    if height > at:
+        built[:, at:, :] = jnp.zeros((depth, height - at, width), F32)
+    out_ref[...] = built[...].astype(BF16)
+
+
+def middle(rows, depth, plane, arrived):
+    length, _, width = arrived.shape
+    wide = 2 * rows * length * depth // width
+    height = 2 * rows + 3 * wide
+    height += -height % 8
+    return pl.pallas_call(
+        lambda *refs: middle_kernel(rows, *refs),
+        name="middle",
+        out_shape=jax.ShapeDtypeStruct((depth, height, width), BF16),
+        in_specs=[pl.BlockSpec(memory_space=pltpu.SMEM), *in_vmem(1)],
+        out_specs=pl.BlockSpec(memory_space=pltpu.VMEM),
+        scratch_shapes=[
+            pltpu.VMEM((width, length * wide + -(length * wide) % 128), F32),
+            pltpu.VMEM((depth, height, width), F32),
+        ],
+        compiler_params=pltpu.CompilerParams(vmem_limit_bytes=12 * MIB),
+    )(plane, arrived)
+
+
+def last_kernel(
+    chip_ref, arrived_ref, place_ref, weight_ref, hidden_ref, states_ref, items_ref,
+    loss_ref, hidden_grad_ref, table_grad_ref, buffer, sems,
+):
+    rows, width = hidden_ref.shape
+    depth = arrived_ref.shape[0]
     items = items_ref.shape[0]
+    count = states_ref.shape[0]
     block = min(BLOCK, items)
+    chips = count // (2 * rows)
+    wide = count // width
+    lines, scale, logs = merged(arrived_ref, 2 * rows, wide)
+    line = jnp.concatenate([logs[c : c + 1] for c in range(wide)], axis=1)
+    weight = weight_ref[...]
+    states = states_ref[...]
     copies = []
     for step, at in enumerate(range(0, items, block)):
         scores = lax.dot_general(
-            items_ref[at : at + block, :], states_ref[...], (((1,), (1,)), ((), ())),
+            items_ref[at : at + block, :], states, (((1,), (1,)), ((), ())),
             preferred_element_type=F32,
         )
-        parts = jnp.exp(scores - log_ref[...])
+        parts = jnp.exp(scores - line)
         matched = lax.broadcasted_iota(jnp.int32, parts.shape, 0) == place_ref[...] - at
-        signal = (weight_ref[...] * jnp.where(matched, parts - 1.0, parts)).astype(BF16)
-        buffers[at : at + block, :] = jnp.dot(
-            signal, states_ref[...], preferred_element_type=F32
+        signal = (weight * jnp.where(matched, parts - 1.0, parts)).astype(BF16)
+        buffer[at : at + block, :] = jnp.dot(
+            signal, states, preferred_element_type=F32
         ).astype(BF16)
         copies.append(
             pltpu.make_async_copy(
-                buffers.at[pl.ds(at, block)], out_ref.at[pl.ds(at, block)], sems.at[step]
+                buffer.at[pl.ds(at, block)], table_grad_ref.at[pl.ds(at, block)], sems.at[step]
             )
         )
         copies[-1].start()
+    lane = lax.broadcasted_iota(jnp.int32, (1, width), 1)
+    hidden = hidden_ref[...].astype(F32)
+    place = lax.broadcasted_iota(jnp.int32, loss_ref.shape, 1)
+    losses = jnp.zeros(loss_ref.shape, F32)
+    grads = []
+    for k in range(rows):
+        c, first = k * chips // width, k * chips % width
+        mine = lambda x: jnp.sum(
+            jnp.where(lane == chip_ref[0] + first, x, 0.0), axis=1, keepdims=True
+        )
+        log_total = mine(logs[c : c + 1])
+        own_weight = mine(weight[:, c * width : (c + 1) * width])
+        grad = jnp.zeros((1, width), F32)
+        picked = jnp.zeros((1, width), F32)
+        for j in range(depth):
+            grad += lines[j, k : k + 1] * mine(scale[j, c : c + 1])
+            picked += lines[j, rows + k : rows + k + 1]
+        score = jnp.sum(hidden[k : k + 1] * picked, axis=1, keepdims=True)
+        losses = jnp.where(place == k, log_total - score, losses)
+        pull = (own_weight * (jnp.exp(score - log_total) - 1.0)).astype(BF16).astype(F32)
+        grads.append(own_weight * grad + pull * picked)
+    loss_ref[...] = losses
+    hidden_grad_ref[...] = jnp.concatenate(grads).astype(BF16)
     for copy in copies:
         copy.wait()
 
 
-def table_gradient(place, log_total, weight, states, items):
-    return pl.pallas_call(
-        table_kernel,
-        name="table_gradient",
-        out_shape=jax.ShapeDtypeStruct(items.shape, BF16),
-        in_specs=in_vmem(5),
-        out_specs=pl.BlockSpec(memory_space=pl.ANY),
+def last(chip, arrived, place, weight, hidden, states, items):
+    rows, width = hidden.shape
+    return pl.pallas_call(
+        last_kernel,
+        name="last",
+        out_shape=(
+            jax.ShapeDtypeStruct((1, rows), F32),
+            jax.ShapeDtypeStruct((rows, width), BF16),
+            jax.ShapeDtypeStruct(items.shape, BF16),
+        ),
+        in_specs=[pl.BlockSpec(memory_space=pltpu.SMEM), *in_vmem(6)],
+        out_specs=[*in_vmem(2), pl.BlockSpec(memory_space=pl.ANY)],
         scratch_shapes=[
             pltpu.VMEM(items.shape, BF16),
             pltpu.SemaphoreType.DMA((items.shape[0] // min(BLOCK, items.shape[0]),)),
         ],
-        compiler_params=pltpu.CompilerParams(vmem_limit_bytes=VMEM_LIMIT),
-    )(place, log_total, weight, states, items)
-
-
-def thirds(x):
-    high = lax.reduce_precision(x, 8, 7)
-    rest = x - high
-    middle = lax.reduce_precision(rest, 8, 7)
-    return jnp.concatenate([high, middle, rest - middle]).astype(BF16)
-
-
-def merged_logs(parts):
-    top = jnp.max(parts, axis=0)
-    return top + jnp.log(jnp.sum(jnp.exp(parts - top[None]), axis=0))
-
-
-def merged(arrived, kept, count, own):
-    length, _, width = arrived.shape
-    given = arrived[:, 2 * kept : 2 * kept + 3 * count // width]
-    given = given.astype(F32).reshape(length, 3, count).sum(axis=1)
-    logs = merged_logs(given)
-    scale = jnp.exp(own(given) - own(logs[None]))
-    grad = jnp.sum(arrived[:, :kept].astype(F32) * scale[:, :, None], axis=0)
-    picked = jnp.sum(arrived[:, kept : 2 * kept].astype(F32), axis=0)
-    return grad, picked, logs
-
-
-def local(hidden, item_table, targets, lengths):
-    rows, width = hidden.shape
+        compiler_params=pltpu.CompilerParams(vmem_limit_bytes=16 * MIB),
+    )(chip, arrived, place, weight, hidden, states, items)
+
+
+def steps(hidden, item_table, targets, lengths):
+    rows, _ = hidden.shape
     group = lax.axis_index("grp")
+    chip = lax.axis_index(CHIPS).reshape(1)
     own_items = item_table.shape[0] // 2
     items = lax.dynamic_slice_in_dim(item_table, group * own_items, own_items)
     first_own = (lax.axis_index(ITEM) * 2 + group) * own_items
-    plane, depth = lax.axis_size(PLANE), lax.axis_size("z")
     weight = weights_for(lengths, rows)
-    mine, other = gathered(hidden, targets)
+    sent = spread(hidden, targets, lax.axis_size(CHIPS))
+    mine = lax.all_to_all(sent, CHIPS, 0, 0, tiled=True)
+    mine = jnp.swapaxes(mine, 0, 1)
     own_grad, other_grad, own_picked, other_picked, logs, place, states = shares(
-        first_own.reshape(1).astype(jnp.int32), mine, other, items
-    )
-    count = states.shape[0]
+        first_own.reshape(1), mine, from_pair(mine), items
+    )
     sent = packed(
-        rows, plane, own_grad, from_pair(other_grad), own_picked, from_pair(other_picked),
-        logs, from_pair(logs),
+        rows, lax.axis_size(PLANE), own_grad, from_pair(other_grad), own_picked,
+        from_pair(other_picked), logs, from_pair(logs),
     )
     arrived = lax.all_to_all(sent, PLANE, 0, 0, tiled=True)
-    in_plane = lambda x: lax.dynamic_index_in_dim(
-        x.reshape(x.shape[0], 2, rows, plane, depth)[:, 0], lax.axis_index(PLANE), 2, False
-    )
-    grad, picked, logs = merged(
-        arrived, rows * depth, count, lambda x: in_plane(x).reshape(x.shape[0], -1)
-    )
-    by_depth = lambda x: jnp.swapaxes(x.reshape(rows, depth, width), 0, 1).astype(BF16)
-    lines = thirds(logs).reshape(-1, width)
-    lines = jnp.broadcast_to(lines[None], (depth, *lines.shape))
-    sent = jnp.concatenate([by_depth(grad), by_depth(picked), lines], axis=1)
+    sent = middle(rows, lax.axis_size("z"), lax.axis_index(PLANE).reshape(1), arrived)
     arrived = lax.all_to_all(sent, "z", 0, 0, tiled=True)
-    own = lambda x: lax.dynamic_index_in_dim(in_plane(x), lax.axis_index("z"), 2, False)
-    grad, picked, logs = merged(arrived, rows, count, own)
-    own_logs = own(logs[None])[0]
-    own_weight = own(weight)[0]
-    target_score = jnp.sum(hidden.astype(F32) * picked, axis=1)
-    row_loss = own_logs - target_score
-    pull = lax.reduce_precision(own_weight * (jnp.exp(target_score - own_logs) - 1.0), 8, 7)
-    hidden_grad = (own_weight[:, None] * grad + pull[:, None] * picked).astype(BF16)
-    table_grad = table_gradient(place, logs[None], weight, states, items)
-    return (row_loss, hidden_grad, table_grad)
+    row_loss, hidden_grad, table_grad = last(
+        chip, arrived, place, weight, hidden, states, items
+    )
+    return (row_loss.reshape(-1), hidden_grad, table_grad)
 
 
 def mapped(split):
     return jax.shard_map(
-        local,
+        steps,
         mesh=split,
         in_specs=(P(GRP_ITEM, None), P(ITEM, None), P(GRP_ITEM), P()),
         out_specs=(P(GRP_ITEM), P(GRP_ITEM, None), P(ITEM_GRP, None)),
@@ -311,9 +391,8 @@
 
 
 def solution(mesh):
-    return mapped(
-        Mesh(
-            mesh.devices.reshape(4, 2, 8, 2, mesh.shape["grp"]),
-            ("x", "yh", "z", "core", "grp"),
-        )
-    )
+    split = Mesh(
+        mesh.devices.reshape(4, 2, 8, 2, mesh.shape["grp"]),
+        ("x", "yh", "z", "core", "grp"),
+    )
+    return mapped(split)

time: 82.9 us -> 79.5 us (0.959)
  other arithmetic: 5.09 us -> 0.31 us
  Pallas kernels: 12.2 us -> 15.4 us
  local copies, waits for them, and re-layouts: 4.98 us -> 3.11 us
    pallas_call x2 -> x4, Pallas kernels: 5.63 us -> 8.82 us  [the longest x1 5.27 us: last(): pl.pallas_call(last_kernel, name='last', out_shape=(jax.ShapeDtypeStruct(...]
    concatenate x3 -> x0, other arithmetic: 1.38 us -> none  [the longest x1 0.69 us: gathered(): mine = sent_to_all(jnp.concatenate([hidden, digits[None]]), CHIPS)]
    unnamed x4 -> x8, local copies, waits for them, and re-layouts: 0.01 us -> 1.34 us
    exp x2 -> x0, other arithmetic: 0.86 us -> none  [merged(): scale = jnp.exp(own(given) - own(logs[None]))]
    dynamic_slice x6 -> x1, local copies, waits for them, and re-layouts: 2.32 us -> 1.73 us  [steps(): items = lax.dynamic_slice_in_dim(item_table, group * own_items, own_items)]
  transfers between devices with their start and end apart: 7 -> 7, of which waited for: 4 -> 5; matrix products, arithmetic and copies ran while one was open for 3% -> 3% of each run, Pallas kernels for 0% -> 0%
where the time goes in v3:
time: 79.5 us; the launch traced here: 79.1 us
  waiting for transfers between devices  33.6 us (42%)
  starting transfers between devices  25.7 us (32%)
  Pallas kernels  15.4 us (19%)
  local copies, waits for them, and re-layouts  3.11 us (4%)
  between operations  0.94 us (1%)
    all_to_all x1, starting transfers between devices, steps(): mine = lax.all_to_all(sent, CHIPS, 0, 0, tiled=True)  15.3 us
    all_to_all x1, waiting for transfers between devices, steps(): mine = lax.all_to_all(sent, CHIPS, 0, 0, tiled=True)  13.5 us
    all_to_all x1, waiting for transfers between devices, steps(): arrived = lax.all_to_all(sent, PLANE, 0, 0, tiled=True)  10.8 us
    all_to_all x1, waiting for transfers between devices, steps(): arrived = lax.all_to_all(sent, 'z', 0, 0, tiled=True)  8.27 us
    pallas_call x1, Pallas kernels, shares(): pl.pallas_call(share_kernel, name='shares', out_shape=(jax.ShapeDtypeStru...  6.56 us
    all_to_all x1, starting transfers between devices, steps(): arrived = lax.all_to_all(sent, PLANE, 0, 0, tiled=True)  5.8 us
    pallas_call x1, Pallas kernels, last(): pl.pallas_call(last_kernel, name='last', out_shape=(jax.ShapeDtypeStruct(...  5.27 us
    all_to_all x1, starting transfers between devices, steps(): arrived = lax.all_to_all(sent, 'z', 0, 0, tiled=True)  3.35 us
  transfers between devices with their start and end apart: 7, of which 5 were waited for; matrix products, arithmetic and copies ran while one was open for 3% of the time, Pallas kernels for 0%

profile of v3, /device:TPU:8, one launch (start us, length us, event | category | flops | bytes accessed | tf_op | source)
XLA Modules:
  0.0 79.1 jit_solution(12738844835645730852)
XLA Ops:
  0.6 0.0 copy-start
  0.6 0.7 copy-done
  1.3 0.0 copy-start.2
  1.3 0.7 copy-done.2
  2.0 1.4 %spread.1 = bf16[128,4,256]{2,1,0:T(4,128)(2,1)} custom-call(s32[3]{0:T(128)S(1)} %copy-done.2, bf16[3,256]{1,0:T(4,128)(2,1)S(1)} %copy-done), custom_call_target="tpu_custom_call" | custom-call | tf_op jit(solution)/shard_map/spread/pallas_call | solution.py:41
  3.3 15.3 %all-to-all-start = ((bf16[128,4,256]{2,1,0:T(4,128)(2,1)}), bf16[128,4,256]{2,1,0:T(4,128)(2,1)S(1)}, u32[]{:S(2)}, u32[]{:S(2)}) async-start(bf16[128,4,256]{2,1,0:T(4,128)(2,1)} %spread.1), calls=%async_computation | async-start | bytes 524288 | tf_op jit(solution)/shard_map/all_to_all | solution.py:365
  18.7 13.5 %all-to-all-done = bf16[128,4,256]{2,1,0:T(4,128)(2,1)S(1)} async-done(((bf16[128,4,256]{2,1,0:T(4,128)(2,1)}), bf16[128,4,256]{2,1,0:T(4,128)(2,1)S(1)}, u32[]{:S(2)}, u32[]{:S(2)}) %all-to-all-start) | async-done | bytes 262176 | tf_op jit(solution)/shard_map/all_to_all | solution.py:365
  32.2 0.1 collective-permute-start
  32.3 1.7 %constant_dynamic-slice_fusion.items_ref = bf16[4096,256]{1,0:T(8,128)(2,1)S(1)} fusion(bf16[8192,256]{1,0:T(8,128)(2,1)} %param.13, s32[]{:T(128)S(6)} %select_n.87), kind=kLoop, calls=%fused_computation.83 | loop fusion | bytes 4194308 | tf_op jit(solution)/shard_map/dynamic_slice | solution.py:361
  34.1 0.0 copy-start.3
  34.1 0.0 collective-permute-done.other_ref
  34.1 6.6 %shares.1 = (f32[384,256]{1,0:T(8,128)S(1)}, f32[384,256]{1,0:T(8,128)S(1)}, bf16[384,256]{1,0:T(8,128)(2,1)S(1)}, bf16[384,256]{1,0:T(8,128)(2,1)S(1)}, f32[1,7...) custom-call(s32[1]{0:T(128)} %bitcast.2.first_ref, bf16[4,128,256]{2,1,0:T(8,128)(2,1)S(1)} %bitcast.8, ...), custom_call_target="tpu_custom_call" | custom-call | tf_op jit(solution)/shard_map/shares/pallas_call | solution.py:142
  40.7 0.0 copy-start.1
  40.7 0.6 collective-permute-start.1
  41.3 0.0 copy-done.3
  41.3 0.1 select_reduce_fusion.1
  41.3 0.1 collective-permute-start.3
  41.4 0.5 collective-permute-start.2
  41.9 0.7 collective-permute-done.3.refs_5_
  42.6 0.4 collective-permute-done.2.refs_3_
  43.0 0.0 collective-permute-done.1.refs_1_
  43.0 1.2 %packed.1 = bf16[16,64,256]{2,1,0:T(8,128)(2,1)} custom-call(f32[384,256]{1,0:T(8,128)S(1)} %get-tuple-element.43.refs_0_, f32[384,256]{1,0:T(8,128)S(1)} %collective-permute-done.1.refs_1_, bf16[384,256]{1,0:T(8,128)(2,1)S(1)} %get-tuple-element.45.refs_2_, bf16[384,256]{1,0:T(8,128)(2,1)S(1)} %collective-permute-done.2.refs_3_, ...), custom_call_target="tpu_custom_call" | custom-call | tf_op jit(solution)/shard_map/packed/pallas_call | solution.py:208
  44.2 5.8 %all-to-all-start.1 = ((bf16[16,64,256]{2,1,0:T(8,128)(2,1)}), bf16[16,64,256]{2,1,0:T(8,128)(2,1)S(1)}, u32[]{:S(2)}, u32[]{:S(2)}) async-start(bf16[16,64,256]{2,1,0:T(8,128)(2,1)} %packed.1), calls=%async_computation.1 | async-start | bytes 1048576 | tf_op jit(solution)/shard_map/all_to_all | solution.py:374
  50.0 0.1 fusion.9
  50.1 0.1 select_reduce_fusion
  50.2 10.8 %all-to-all-done.1.refs_1_ = bf16[16,64,256]{2,1,0:T(8,128)(2,1)S(1)} async-done(((bf16[16,64,256]{2,1,0:T(8,128)(2,1)}), bf16[16,64,256]{2,1,0:T(8,128)(2,1)S(1)}, u32[]{:S(2)}, u32[]{:S(2)}) %all-to-all-start.1) | async-done | bytes 524320 | tf_op jit(solution)/shard_map/all_to_all | solution.py:374
  61.0 1.0 %middle.1 = bf16[8,16,256]{2,1,0:T(8,128)(2,1)} custom-call(s32[1]{0:T(128)} %bitcast.1.refs_0_, bf16[16,64,256]{2,1,0:T(8,128)(2,1)S(1)} %all-to-all-done.1.refs_1_), custom_call_target="tpu_custom_call" | custom-call | tf_op jit(solution)/shard_map/middle/pallas_call | solution.py:262
  62.0 3.4 %all-to-all-start.2 = ((bf16[8,16,256]{2,1,0:T(8,128)(2,1)}), bf16[8,16,256]{2,1,0:T(8,128)(2,1)S(1)}, u32[]{:S(2)}, u32[]{:S(2)}) async-start(bf16[8,16,256]{2,1,0:T(8,128)(2,1)} %middle.1), calls=%async_computation.2 | async-start | bytes 131072 | tf_op jit(solution)/shard_map/all_to_all | solution.py:376
  65.4 8.3 %all-to-all-done.2.arrived_ref = bf16[8,16,256]{2,1,0:T(8,128)(2,1)S(1)} async-done(((bf16[8,16,256]{2,1,0:T(8,128)(2,1)}), bf16[8,16,256]{2,1,0:T(8,128)(2,1)S(1)}, u32[]{:S(2)}, u32[]{:S(2)}) %all-to-all-start.2) | async-done | bytes 65568 | tf_op jit(solution)/shard_map/all_to_all | solution.py:376
  73.7 0.0 copy-done.1
  73.7 5.3 %last.1 = (f32[1,3]{1,0:T(1,128)}, bf16[3,256]{1,0:T(4,128)(2,1)}, bf16[4096,256]{1,0:T(8,128)(2,1)}) custom-call(s32[1]{0:T(128)} %bitcast.chip_ref, bf16[8,16,256]{2,1,0:T(8,128)(2,1)S(1)} %all-to-all-done.2.arrived_ref, s32[1,768]{1,0:T(1,128)S(1)} %get-tuple-element.48.place_ref, f32[1,768]{1,0:T(1,128)S(1)} %div.49.weight_ref, ...), custom_call_target="tpu_custom_call" | custom-call | tf_op jit(solution)/shard_map/last/pallas_call | solution.py:338
  (7 shorter events, 0.1 us)
Async XLA Ops:
  0.6 0.7 copy-start
  1.3 0.7 copy-start.2
  3.3 28.9 %all-to-all-start = ((bf16[128,4,256]{2,1,0:T(4,128)(2,1)}), bf16[128,4,256]{2,1,0:T(4,128)(2,1)S(1)}, u32[]{:S(2)}, u32[]{:S(2)}) async-start(bf16[128,4,256]{2,1,0:T(4,128)(2,1)} %spread.1), calls=%async_computation | async-start | bytes 524288 | tf_op jit(solution)/shard_map/all_to_all | solution.py:365
  32.2 1.9 %collective-permute-start = (bf16[4,128,256]{2,1,0:T(8,128)(2,1)S(1)}, bf16[4,128,256]{2,1,0:T(8,128)(2,1)S(1)}, u32[]{:S(2)}, u32[]{:S(2)}) collective-permute-start(bf16[4,128,256]{2,1,0:T(8,128)(2,1)S(1)} %bitcast.7), channel_id=1, source_target_pairs={{0,2},{2,0},{1,3},{3,1},{4,6},{6,4},{5,7},{7,5},{8,10},{10,8},{9,1... | collective-permute-start | bytes 786440 | tf_op jit(solution)/shard_map/ppermute | solution.py:22
  34.1 7.2 %copy-start.3 = (s32[2,16]{1,0:T(2,128)S(1)}, s32[2,16]{1,0:T(2,128)}, u32[]{:S(2)}) copy-start(s32[2,16]{1,0:T(2,128)} %param.15) | copy-start | bytes 388
  40.7 33.0 %copy-start.1 = (bf16[3,256]{1,0:T(4,128)(2,1)S(1)}, bf16[3,256]{1,0:T(4,128)(2,1)}, u32[]{:S(2)}) copy-start(bf16[3,256]{1,0:T(4,128)(2,1)} %hidden_ref.3) | copy-start | bytes 4612
  40.7 2.3 %collective-permute-start.1 = (f32[384,256]{1,0:T(8,128)S(1)}, f32[384,256]{1,0:T(8,128)S(1)}, u32[]{:S(2)}, u32[]{:S(2)}) collective-permute-start(f32[384,256]{1,0:T(8,128)S(1)} %get-tuple-element.44), channel_id=1, source_target_pairs={{0,2},{2,0},{1,3},{3,1},{4,6},{6,4},{5,7},{7,5},{8,10},{10,8},{9,1... | collective-permute-start | bytes 1179656 | tf_op jit(solution)/shard_map/ppermute | solution.py:22
  41.3 1.3 %collective-permute-start.3 = (f32[1,768]{1,0:T(1,128)S(1)}, f32[1,768]{1,0:T(1,128)S(1)}, u32[]{:S(2)}, u32[]{:S(2)}) collective-permute-start(f32[1,768]{1,0:T(1,128)S(1)} %get-tuple-element.47.refs_4_), channel_id=1, source_target_pairs={{0,2},{2,0},{1,3},{3,1},{4,6},{6,4},{5,7},{7,5},{8,10},{10,8},{9,1... | collective-permute-start | bytes 9224 | tf_op jit(solution)/shard_map/ppermute | solution.py:22
  41.4 1.6 %collective-permute-start.2 = (bf16[384,256]{1,0:T(8,128)(2,1)S(1)}, bf16[384,256]{1,0:T(8,128)(2,1)S(1)}, u32[]{:S(2)}, u32[]{:S(2)}) collective-permute-start(bf16[384,256]{1,0:T(8,128)(2,1)S(1)} %get-tuple-element.46), channel_id=1, source_target_pairs={{0,2},{2,0},{1,3},{3,1},{4,6},{6,4},{5,7},{7,5},{8,10},{10,8},{9,1... | collective-permute-start | bytes 589832 | tf_op jit(solution)/shard_map/ppermute | solution.py:22
  44.2 16.8 %all-to-all-start.1 = ((bf16[16,64,256]{2,1,0:T(8,128)(2,1)}), bf16[16,64,256]{2,1,0:T(8,128)(2,1)S(1)}, u32[]{:S(2)}, u32[]{:S(2)}) async-start(bf16[16,64,256]{2,1,0:T(8,128)(2,1)} %packed.1), calls=%async_computation.1 | async-start | bytes 1048576 | tf_op jit(solution)/shard_map/all_to_all | solution.py:374
  62.0 11.7 %all-to-all-start.2 = ((bf16[8,16,256]{2,1,0:T(8,128)(2,1)}), bf16[8,16,256]{2,1,0:T(8,128)(2,1)S(1)}, u32[]{:S(2)}, u32[]{:S(2)}) async-start(bf16[8,16,256]{2,1,0:T(8,128)(2,1)} %middle.1), calls=%async_computation.2 | async-start | bytes 131072 | tf_op jit(solution)/shard_map/all_to_all | solution.py:376

commit v4 on v3

--- a/solution.py
+++ b/solution.py
@@ -22,7 +22,15 @@
     return lax.ppermute(x, "core", [(0, 1), (1, 0)])
 
 
-def spread_kernel(targets_ref, hidden_ref, out_ref):
+def spread_kernel(targets_hbm, hidden_hbm, out_ref, targets_ref, hidden_ref, sems):
+    copies = [
+        pltpu.make_async_copy(targets_hbm, targets_ref, sems.at[0]),
+        pltpu.make_async_copy(hidden_hbm, hidden_ref, sems.at[1]),
+    ]
+    for copy in copies:
+        copy.start()
+    for copy in copies:
+        copy.wait()
     _, height, width = out_ref.shape
     rows = height - 1
     lane = lax.broadcasted_iota(jnp.int32, (1, width), 1)
@@ -42,10 +50,19 @@
         spread_kernel,
         name="spread",
         out_shape=jax.ShapeDtypeStruct((chips, rows + 1, width), BF16),
-        in_specs=[pl.BlockSpec(memory_space=pltpu.SMEM), *in_vmem(1)],
+        in_specs=[pl.BlockSpec(memory_space=pltpu.HBM)] * 2,
         out_specs=pl.BlockSpec(memory_space=pltpu.VMEM),
+        scratch_shapes=[
+            pltpu.SMEM(targets.shape, jnp.int32),
+            pltpu.VMEM(hidden.shape, BF16),
+            pltpu.SemaphoreType.DMA((2,)),
+        ],
         compiler_params=pltpu.CompilerParams(vmem_limit_bytes=4 * MIB),
-    )(targets, hidden)
+    )(in_hbm(targets), in_hbm(hidden))
+
+
+def in_hbm(x):
+    return pltpu.with_memory_space_constraint(x, pltpu.HBM)
 
 
 def in_vmem(count):
@@ -77,29 +94,26 @@
 
 
 def share_kernel(
-    first_ref, mine_ref, other_ref, items_ref,
-    own_grad_ref, other_grad_ref, own_rows_ref, other_rows_ref, log_ref, place_ref, states_ref,
+    first_ref, given_ref, items_ref, grad_ref, rows_ref, log_ref, place_ref, states_ref,
     scores, places, grad, picked,
 ):
-    rows = mine_ref.shape[0] - 1
-    chips = mine_ref.shape[1]
+    rows = given_ref.shape[0] - 1
+    chips = given_ref.shape[1]
     count, _ = states_ref.shape
     items = items_ref.shape[0]
-    part = count // 2
     block = min(BLOCK, items)
     lanes = min(128, block)
-    for half, ref in enumerate((mine_ref, other_ref)):
-        digits = ref[rows].astype(F32)
-        across = digits.T
-        for k in range(rows):
-            at = half * part + k * chips
-            states_ref[at : at + chips, :] = ref[k]
-            found = [digits[:, j * rows + k : j * rows + k + 1].astype(jnp.int32) for j in range(3)]
-            found = found[0] + DIGIT * found[1] + DIGIT**2 * found[2] - first_ref[0]
-            places[at : at + chips, :] = jnp.broadcast_to(found, (chips, lanes))
-            found = [across[j * rows + k : j * rows + k + 1, :].astype(jnp.int32) for j in range(3)]
-            found = found[0] + DIGIT * found[1] + DIGIT**2 * found[2] - first_ref[0]
-            place_ref[:, at : at + chips] = found
+    digits = given_ref[rows].astype(F32)
+    across = digits.T
+    for k in range(rows):
+        at = k * chips
+        states_ref[at : at + chips, :] = given_ref[k]
+        found = [digits[:, j * rows + k : j * rows + k + 1].astype(jnp.int32) for j in range(3)]
+        found = found[0] + DIGIT * found[1] + DIGIT**2 * found[2] - first_ref[0]
+        places[at : at + chips, :] = jnp.broadcast_to(found, (chips, lanes))
+        found = [across[j * rows + k : j * rows + k + 1, :].astype(jnp.int32) for j in range(3)]
+        found = found[0] + DIGIT * found[1] + DIGIT**2 * found[2] - first_ref[0]
+        place_ref[:, at : at + chips] = found
     states = states_ref[...]
     high = None
     for at in range(0, items, block):
@@ -112,7 +126,7 @@
             high = top if high is None else jnp.maximum(high, top)
     high = jnp.max(high, axis=1, keepdims=True)
     total = None
-    lane = lax.broadcasted_iota(jnp.int32, (count, lanes), 1)
+    lane = lax.broadcasted_iota(jnp.int32, (1, lanes), 1)
     for at in range(0, items, block):
         others, hot = [], []
         for c in range(at, at + block, lanes):
@@ -128,39 +142,33 @@
         picked[...] = more if at == 0 else picked[...] + more
     log_sum = high + jnp.log(jnp.sum(total, axis=1, keepdims=True))
     log_ref[...] = jnp.broadcast_to(log_sum, (count, 128)).T[:1, :]
-    share = grad[...] * jnp.exp(high - log_sum)
-    own_grad_ref[...] = share[:part]
-    other_grad_ref[...] = share[part:]
-    own_rows_ref[...] = picked[:part, :].astype(BF16)
-    other_rows_ref[...] = picked[part:, :].astype(BF16)
-
-
-def shares(first, mine, other, items):
-    rows, chips, width = mine.shape
-    part = (rows - 1) * chips
-    count = 2 * part
+    grad_ref[...] = grad[...] * jnp.exp(high - log_sum)
+    rows_ref[...] = picked[...].astype(BF16)
+
+
+def shares(first, given, items):
+    height, chips, width = given.shape
+    count = (height - 1) * chips
     return pl.pallas_call(
         share_kernel,
         name="shares",
         out_shape=(
-            jax.ShapeDtypeStruct((part, width), F32),
-            jax.ShapeDtypeStruct((part, width), F32),
-            jax.ShapeDtypeStruct((part, width), BF16),
-            jax.ShapeDtypeStruct((part, width), BF16),
+            jax.ShapeDtypeStruct((count, width), F32),
+            jax.ShapeDtypeStruct((count, width), BF16),
             jax.ShapeDtypeStruct((1, count), F32),
             jax.ShapeDtypeStruct((1, count), jnp.int32),
             jax.ShapeDtypeStruct((count, width), BF16),
         ),
-        in_specs=[pl.BlockSpec(memory_space=pltpu.SMEM), *in_vmem(3)],
-        out_specs=in_vmem(7),
+        in_specs=[pl.BlockSpec(memory_space=pltpu.SMEM), *in_vmem(2)],
+        out_specs=in_vmem(5),
         scratch_shapes=[
             pltpu.VMEM((count, items.shape[0]), F32),
-            pltpu.VMEM((count, min(128, items.shape[0])), jnp.int32),
+            pltpu.VMEM((count, min(128, BLOCK)), jnp.int32),
             pltpu.VMEM((count, width), F32),
             pltpu.VMEM((count, width), F32),
         ],
-        compiler_params=pltpu.CompilerParams(vmem_limit_bytes=32 * MIB),
-    )(first, mine, other, items)
+        compiler_params=pltpu.CompilerParams(vmem_limit_bytes=24 * MIB),
+    )(first, given, items)
 
 
 def three_parts(x):
@@ -170,21 +178,14 @@
     return [high, middle, rest - middle]
 
 
-def swapped(x):
-    part = x.shape[1] // 2
-    return jnp.concatenate([x[:, part:], x[:, :part]], axis=1)
-
-
-def swapped(x):
-    part = x.shape[1] // 2
-    return jnp.concatenate([x[:, part:], x[:, :part]], axis=1)
-
-
-def pack_kernel(rows, own_grad_ref, other_grad_ref, own_rows_ref, other_rows_ref, own_log_ref, other_log_ref, out_ref):
+def pack_kernel(
+    rows, own_grad_ref, other_grad_ref, own_rows_ref, other_rows_ref,
+    own_log_ref, far_log_ref, other_log_ref, other_far_log_ref, out_ref,
+):
     length, _, width = out_ref.shape
     part = own_grad_ref.shape[0]
-    own = own_log_ref[...]
-    other = swapped(other_log_ref[...])
+    own = jnp.concatenate([own_log_ref[...], far_log_ref[...]], axis=1)
+    other = jnp.concatenate([other_far_log_ref[...], other_log_ref[...]], axis=1)
     top = jnp.maximum(own, other)
     both = top + jnp.log(jnp.exp(own - top) + jnp.exp(other - top))
     grad = own_grad_ref[...] * column(jnp.exp(own - both)[:, :part])
@@ -209,7 +210,7 @@
         lambda *refs: pack_kernel(rows, *refs),
         name="packed",
         out_shape=jax.ShapeDtypeStruct((length, height, width), BF16),
-        in_specs=in_vmem(6),
+        in_specs=in_vmem(8),
         out_specs=pl.BlockSpec(memory_space=pltpu.VMEM),
         compiler_params=pltpu.CompilerParams(vmem_limit_bytes=12 * MIB),
     )(*pieces)
@@ -274,38 +275,25 @@
 
 
 def last_kernel(
-    chip_ref, arrived_ref, place_ref, weight_ref, hidden_ref, states_ref, items_ref,
-    loss_ref, hidden_grad_ref, table_grad_ref, buffer, sems,
+    chip_ref, arrived_ref, place_ref, far_place_ref, weight_ref, hidden_ref, states_ref,
+    far_states_ref, items_ref, loss_hbm, hidden_grad_hbm, table_grad_hbm,
+    states, buffer, loss_ref, hidden_grad_ref, sems,
 ):
     rows, width = hidden_ref.shape
     depth = arrived_ref.shape[0]
     items = items_ref.shape[0]
-    count = states_ref.shape[0]
+    count = states.shape[0]
     block = min(BLOCK, items)
     chips = count // (2 * rows)
     wide = count // width
+    copies = []
+
+    def send(source, target):
+        copies.append(pltpu.make_async_copy(source, target, sems.at[len(copies)]))
+        copies[-1].start()
+
     lines, scale, logs = merged(arrived_ref, 2 * rows, wide)
-    line = jnp.concatenate([logs[c : c + 1] for c in range(wide)], axis=1)
     weight = weight_ref[...]
-    states = states_ref[...]
-    copies = []
-    for step, at in enumerate(range(0, items, block)):
-        scores = lax.dot_general(
-            items_ref[at : at + block, :], states, (((1,), (1,)), ((), ())),
-            preferred_element_type=F32,
-        )
-        parts = jnp.exp(scores - line)
-        matched = lax.broadcasted_iota(jnp.int32, parts.shape, 0) == place_ref[...] - at
-        signal = (weight * jnp.where(matched, parts - 1.0, parts)).astype(BF16)
-        buffer[at : at + block, :] = jnp.dot(
-            signal, states, preferred_element_type=F32
-        ).astype(BF16)
-        copies.append(
-            pltpu.make_async_copy(
-                buffer.at[pl.ds(at, block)], table_grad_ref.at[pl.ds(at, block)], sems.at[step]
-            )
-        )
-        copies[-1].start()
     lane = lax.broadcasted_iota(jnp.int32, (1, width), 1)
     hidden = hidden_ref[...].astype(F32)
     place = lax.broadcasted_iota(jnp.int32, loss_ref.shape, 1)
@@ -314,7 +302,7 @@
     for k in range(rows):
         c, first = k * chips // width, k * chips % width
         mine = lambda x: jnp.sum(
-            jnp.where(lane == chip_ref[0] + first, x, 0.0), axis=1, keepdims=True
+            jnp.where(lane == chip_ref[0] + first, x, 0.0), axis=-1, keepdims=True
         )
         log_total = mine(logs[c : c + 1])
         own_weight = mine(weight[:, c * width : (c + 1) * width])
@@ -328,12 +316,30 @@
         pull = (own_weight * (jnp.exp(score - log_total) - 1.0)).astype(BF16).astype(F32)
         grads.append(own_weight * grad + pull * picked)
     loss_ref[...] = losses
+    send(loss_ref, loss_hbm)
     hidden_grad_ref[...] = jnp.concatenate(grads).astype(BF16)
+    send(hidden_grad_ref, hidden_grad_hbm)
+    line = jnp.concatenate([logs[c : c + 1] for c in range(wide)], axis=1)
+    places = jnp.concatenate([place_ref[...], far_place_ref[...]], axis=1)
+    states[: count // 2, :] = states_ref[...]
+    states[count // 2 :, :] = far_states_ref[...]
+    for at in range(0, items, block):
+        scores = lax.dot_general(
+            items_ref[at : at + block, :], states[...], (((1,), (1,)), ((), ())),
+            preferred_element_type=F32,
+        )
+        parts = jnp.exp(scores - line)
+        matched = lax.broadcasted_iota(jnp.int32, parts.shape, 0) == places - at
+        signal = (weight * jnp.where(matched, parts - 1.0, parts)).astype(BF16)
+        buffer[at : at + block, :] = jnp.dot(
+            signal, states[...], preferred_element_type=F32
+        ).astype(BF16)
+        send(buffer.at[pl.ds(at, block)], table_grad_hbm.at[pl.ds(at, block)])
     for copy in copies:
         copy.wait()
 
 
-def last(chip, arrived, place, weight, hidden, states, items):
+def last(chip, arrived, place, far_place, weight, hidden, states, far_states, items):
     rows, width = hidden.shape
     return pl.pallas_call(
         last_kernel,
@@ -343,14 +349,17 @@
             jax.ShapeDtypeStruct((rows, width), BF16),
             jax.ShapeDtypeStruct(items.shape, BF16),
         ),
-        in_specs=[pl.BlockSpec(memory_space=pltpu.SMEM), *in_vmem(6)],
-        out_specs=[*in_vmem(2), pl.BlockSpec(memory_space=pl.ANY)],
+        in_specs=[pl.BlockSpec(memory_space=pltpu.SMEM), *in_vmem(8)],
+        out_specs=[pl.BlockSpec(memory_space=pltpu.HBM)] * 3,
         scratch_shapes=[
+            pltpu.VMEM((2 * states.shape[0], width), BF16),
             pltpu.VMEM(items.shape, BF16),
-            pltpu.SemaphoreType.DMA((items.shape[0] // min(BLOCK, items.shape[0]),)),
+            pltpu.VMEM((1, rows), F32),
+            pltpu.VMEM((rows, width), BF16),
+            pltpu.SemaphoreType.DMA((2 + items.shape[0] // min(BLOCK, items.shape[0]),)),
         ],
         compiler_params=pltpu.CompilerParams(vmem_limit_bytes=16 * MIB),
-    )(chip, arrived, place, weight, hidden, states, items)
+    )(chip, arrived, place, far_place, weight, hidden, states, far_states, items)
 
 
 def steps(hidden, item_table, targets, lengths):
@@ -364,18 +373,19 @@
     sent = spread(hidden, targets, lax.axis_size(CHIPS))
     mine = lax.all_to_all(sent, CHIPS, 0, 0, tiled=True)
     mine = jnp.swapaxes(mine, 0, 1)
-    own_grad, other_grad, own_picked, other_picked, logs, place, states = shares(
-        first_own.reshape(1), mine, from_pair(mine), items
-    )
+    first_own = first_own.reshape(1)
+    other = from_pair(mine)
+    own_grad, own_picked, own_logs, place, states = shares(first_own, mine, items)
+    far_grad, far_picked, far_logs, far_place, far_states = shares(first_own, other, items)
     sent = packed(
-        rows, lax.axis_size(PLANE), own_grad, from_pair(other_grad), own_picked,
-        from_pair(other_picked), logs, from_pair(logs),
+        rows, lax.axis_size(PLANE), own_grad, from_pair(far_grad), own_picked,
+        from_pair(far_picked), own_logs, far_logs, from_pair(own_logs), from_pair(far_logs),
     )
     arrived = lax.all_to_all(sent, PLANE, 0, 0, tiled=True)
     sent = middle(rows, lax.axis_size("z"), lax.axis_index(PLANE).reshape(1), arrived)
     arrived = lax.all_to_all(sent, "z", 0, 0, tiled=True)
     row_loss, hidden_grad, table_grad = last(
-        chip, arrived, place, weight, hidden, states, items
+        chip, arrived, place, far_place, weight, hidden, states, far_states, items
     )
     return (row_loss.reshape(-1), hidden_grad, table_grad)
 

time: 79.5 us -> 78.3 us (0.985)
  local copies, waits for them, and re-layouts: 3.11 us -> 1.78 us
    unnamed x8 -> x4, local copies, waits for them, and re-layouts: 1.34 us -> 0.01 us
    pallas_call x1 -> x2, Pallas kernels: 6.56 us -> 6.93 us  [shares(): pl.pallas_call(share_kernel, name='shares', out_shape=(jax.ShapeDtypeStru...]
  transfers between devices with their start and end apart: 7 -> 8, of which waited for: 5 -> 6; matrix products, arithmetic and copies ran while one was open for 3% -> 3% of each run, Pallas kernels for 0% -> 4%
where the time goes in v4:
time: 78.3 us; the launch traced here: 78 us
  waiting for transfers between devices  33.7 us (43%)
  starting transfers between devices  25.9 us (33%)
  Pallas kernels  15.4 us (20%)
  local copies, waits for them, and re-layouts  1.78 us (2%)
  between operations  0.95 us (1%)
    all_to_all x1, starting transfers between devices, steps(): mine = lax.all_to_all(sent, CHIPS, 0, 0, tiled=True)  15.4 us
    all_to_all x1, waiting for transfers between devices, steps(): mine = lax.all_to_all(sent, CHIPS, 0, 0, tiled=True)  13.5 us
    all_to_all x1, waiting for transfers between devices, steps(): arrived = lax.all_to_all(sent, PLANE, 0, 0, tiled=True)  10.6 us
    all_to_all x1, waiting for transfers between devices, steps(): arrived = lax.all_to_all(sent, 'z', 0, 0, tiled=True)  8.27 us
    pallas_call x2, Pallas kernels, shares(): pl.pallas_call(share_kernel, name='shares', out_shape=(jax.ShapeDtypeStru...  6.93 us
    all_to_all x1, starting transfers between devices, steps(): arrived = lax.all_to_all(sent, PLANE, 0, 0, tiled=True)  5.8 us
    pallas_call x1, Pallas kernels, last(): pl.pallas_call(last_kernel, name='last', out_shape=(jax.ShapeDtypeStruct(...  4.77 us
    all_to_all x1, starting transfers between devices, steps(): arrived = lax.all_to_all(sent, 'z', 0, 0, tiled=True)  3.35 us
  transfers between devices with their start and end apart: 8, of which 6 were waited for; matrix products, arithmetic and copies ran while one was open for 3% of the time, Pallas kernels for 4%

profile of v4, /device:TPU:8, one launch (start us, length us, event | category | flops | bytes accessed | tf_op | source)
XLA Modules:
  0.0 78.0 jit_solution(15227487716014892151)
XLA Ops:
  0.6 1.5 %spread.1 = bf16[128,4,256]{2,1,0:T(4,128)(2,1)} custom-call(s32[3]{0:T(128)} %targets_hbm.1, bf16[3,256]{1,0:T(4,128)(2,1)} %hidden_ref.1), custom_call_target="tpu_custom_call" | custom-call | tf_op jit(solution)/shard_map/spread/pallas_call | solution.py:49
  2.1 15.4 %all-to-all-start = ((bf16[128,4,256]{2,1,0:T(4,128)(2,1)}), bf16[128,4,256]{2,1,0:T(4,128)(2,1)S(1)}, u32[]{:S(2)}, u32[]{:S(2)}) async-start(bf16[128,4,256]{2,1,0:T(4,128)(2,1)} %spread.1), calls=%async_computation | async-start | bytes 524288 | tf_op jit(solution)/shard_map/all_to_all | solution.py:374
  17.5 13.5 %all-to-all-done = bf16[128,4,256]{2,1,0:T(4,128)(2,1)S(1)} async-done(((bf16[128,4,256]{2,1,0:T(4,128)(2,1)}), bf16[128,4,256]{2,1,0:T(4,128)(2,1)S(1)}, u32[]{:S(2)}, u32[]{:S(2)}) %all-to-all-start) | async-done | bytes 262176 | tf_op jit(solution)/shard_map/all_to_all | solution.py:374
  31.1 0.1 collective-permute-start
  31.2 1.7 %constant_dynamic-slice_fusion.items_ref = bf16[4096,256]{1,0:T(8,128)(2,1)S(1)} fusion(bf16[8192,256]{1,0:T(8,128)(2,1)} %param.13, s32[]{:T(128)S(6)} %select_n.87), kind=kLoop, calls=%fused_computation.83 | loop fusion | bytes 4194308 | tf_op jit(solution)/shard_map/dynamic_slice | solution.py:370
  32.9 0.0 copy-start.1
  32.9 0.0 collective-permute-done.given_ref
  32.9 3.5 %shares.3 = (f32[384,256]{1,0:T(8,128)S(1)}, bf16[384,256]{1,0:T(8,128)(2,1)S(1)}, f32[1,384]{1,0:T(1,128)S(1)}, s32[1,384]{1,0:T(1,128)S(1)}, bf16[384,256]{1,0:T(8,128)(2,1)S(1)}) custom-call(s32[1]{0:T(128)} %bitcast.2.first_ref, bf16[4,128,256]{2,1,0:T(8,128)(2,1)S(1)} %collective-permute-done.given_ref, ...), custom_call_target="tpu_custom_call" | custom-call | tf_op jit(solution)/shard_map/shares/pallas_call | solution.py:152
  36.4 0.6 collective-permute-start.1
  37.0 0.0 copy-done.1
  37.0 0.1 select_reduce_fusion.1
  37.1 3.5 %shares.2 = (f32[384,256]{1,0:T(8,128)S(1)}, bf16[384,256]{1,0:T(8,128)(2,1)S(1)}, f32[1,384]{1,0:T(1,128)S(1)}, s32[1,384]{1,0:T(1,128)S(1)}, bf16[384,256]{1,0:T(8,128)(2,1)S(1)}) custom-call(s32[1]{0:T(128)} %bitcast.2.first_ref, bf16[4,128,256]{2,1,0:T(8,128)(2,1)S(1)} %bitcast.8, bf16[4096,256]{1,0:T(8,128)(2,1)S(1)} %constant_dynamic-slice_fusion.items_ref), custom_call_target="tpu_custom_call" | custom-call | tf_op jit(solution)/shard_map/shares/pallas_call | solution.py:152
  40.5 0.0 copy-start
  40.5 0.1 collective-permute-start.3
  40.7 0.5 collective-permute-start.4
  41.1 0.1 collective-permute-start.2
  41.2 0.5 collective-permute-done.3.refs_6_
  41.8 0.2 collective-permute-done.4.refs_7_
  42.0 0.6 collective-permute-done.2.refs_3_
  42.6 0.0 collective-permute-done.1.refs_1_
  42.6 1.2 %packed.1 = bf16[16,64,256]{2,1,0:T(8,128)(2,1)} custom-call(f32[384,256]{1,0:T(8,128)S(1)} %get-tuple-element.46.refs_0_, f32[384,256]{1,0:T(8,128)S(1)} %collective-permute-done.1.refs_1_, bf16[384,256]{1,0:T(8,128)(2,1)S(1)} %get-tuple-element.48.refs_2_, bf16[384,256]{1,0:T(8,128)(2,1)S(1)} %collective-permute-done.2.refs_3_, ...), custom_call_target="tpu_custom_call" | custom-call | tf_op jit(solution)/shard_map/packed/pallas_call | solution.py:209
  43.8 5.8 %all-to-all-start.1 = ((bf16[16,64,256]{2,1,0:T(8,128)(2,1)}), bf16[16,64,256]{2,1,0:T(8,128)(2,1)S(1)}, u32[]{:S(2)}, u32[]{:S(2)}) async-start(bf16[16,64,256]{2,1,0:T(8,128)(2,1)} %packed.1), calls=%async_computation.1 | async-start | bytes 1048576 | tf_op jit(solution)/shard_map/all_to_all | solution.py:384
  49.6 0.1 fusion.9
  49.7 0.1 select_reduce_fusion
  49.8 10.6 %all-to-all-done.1.refs_1_ = bf16[16,64,256]{2,1,0:T(8,128)(2,1)S(1)} async-done(((bf16[16,64,256]{2,1,0:T(8,128)(2,1)}), bf16[16,64,256]{2,1,0:T(8,128)(2,1)S(1)}, u32[]{:S(2)}, u32[]{:S(2)}) %all-to-all-start.1) | async-done | bytes 524320 | tf_op jit(solution)/shard_map/all_to_all | solution.py:384
  60.4 1.0 %middle.1 = bf16[8,16,256]{2,1,0:T(8,128)(2,1)} custom-call(s32[1]{0:T(128)} %bitcast.1.refs_0_, bf16[16,64,256]{2,1,0:T(8,128)(2,1)S(1)} %all-to-all-done.1.refs_1_), custom_call_target="tpu_custom_call" | custom-call | tf_op jit(solution)/shard_map/middle/pallas_call | solution.py:263
  61.4 3.4 %all-to-all-start.2 = ((bf16[8,16,256]{2,1,0:T(8,128)(2,1)}), bf16[8,16,256]{2,1,0:T(8,128)(2,1)S(1)}, u32[]{:S(2)}, u32[]{:S(2)}) async-start(bf16[8,16,256]{2,1,0:T(8,128)(2,1)} %middle.1), calls=%async_computation.2 | async-start | bytes 131072 | tf_op jit(solution)/shard_map/all_to_all | solution.py:386
  64.8 8.3 %all-to-all-done.2.arrived_ref = bf16[8,16,256]{2,1,0:T(8,128)(2,1)S(1)} async-done(((bf16[8,16,256]{2,1,0:T(8,128)(2,1)}), bf16[8,16,256]{2,1,0:T(8,128)(2,1)S(1)}, u32[]{:S(2)}, u32[]{:S(2)}) %all-to-all-start.2) | async-done | bytes 65568 | tf_op jit(solution)/shard_map/all_to_all | solution.py:386
  73.0 0.0 copy-done
  73.0 4.8 %last.1 = (f32[1,3]{1,0:T(1,128)}, bf16[3,256]{1,0:T(4,128)(2,1)}, bf16[4096,256]{1,0:T(8,128)(2,1)}) custom-call(s32[1]{0:T(128)} %bitcast.chip_ref, bf16[8,16,256]{2,1,0:T(8,128)(2,1)S(1)} %all-to-all-done.2.arrived_ref, s32[1,384]{1,0:T(1,128)S(1)} %get-tuple-element.52.place_ref, s32[1,384]{1,0:T(1,128)S(1)} %get-tuple-element.53.far_place_ref, ...), custom_call_target="tpu_custom_call" | custom-call | tf_op jit(solution)/shard_map/last/pallas_call | solution.py:344
  (7 shorter events, 0.1 us)
Async XLA Ops:
  2.1 28.9 %all-to-all-start = ((bf16[128,4,256]{2,1,0:T(4,128)(2,1)}), bf16[128,4,256]{2,1,0:T(4,128)(2,1)S(1)}, u32[]{:S(2)}, u32[]{:S(2)}) async-start(bf16[128,4,256]{2,1,0:T(4,128)(2,1)} %spread.1), calls=%async_computation | async-start | bytes 524288 | tf_op jit(solution)/shard_map/all_to_all | solution.py:374
  31.1 1.9 %collective-permute-start = (bf16[4,128,256]{2,1,0:T(8,128)(2,1)S(1)}, bf16[4,128,256]{2,1,0:T(8,128)(2,1)S(1)}, u32[]{:S(2)}, u32[]{:S(2)}) collective-permute-start(bf16[4,128,256]{2,1,0:T(8,128)(2,1)S(1)} %bitcast.7), channel_id=1, source_target_pairs={{0,2},{2,0},{1,3},{3,1},{4,6},{6,4},{5,7},{7,5},{8,10},{10,8},{9,1... | collective-permute-start | bytes 786440 | tf_op jit(solution)/shard_map/ppermute | solution.py:22
  32.9 4.1 %copy-start.1 = (s32[2,16]{1,0:T(2,128)S(1)}, s32[2,16]{1,0:T(2,128)}, u32[]{:S(2)}) copy-start(s32[2,16]{1,0:T(2,128)} %param.15) | copy-start | bytes 388
  36.4 6.2 %collective-permute-start.1 = (f32[384,256]{1,0:T(8,128)S(1)}, f32[384,256]{1,0:T(8,128)S(1)}, u32[]{:S(2)}, u32[]{:S(2)}) collective-permute-start(f32[384,256]{1,0:T(8,128)S(1)} %get-tuple-element.47), channel_id=1, source_target_pairs={{0,2},{2,0},{1,3},{3,1},{4,6},{6,4},{5,7},{7,5},{8,10},{10,8},{9,1... | collective-permute-start | bytes 1179656 | tf_op jit(solution)/shard_map/ppermute | solution.py:22
  40.5 32.5 %copy-start = (bf16[3,256]{1,0:T(4,128)(2,1)S(1)}, bf16[3,256]{1,0:T(4,128)(2,1)}, u32[]{:S(2)}) copy-start(bf16[3,256]{1,0:T(4,128)(2,1)} %hidden_ref.1) | copy-start | bytes 4612
  40.5 1.2 %collective-permute-start.3 = (f32[1,384]{1,0:T(1,128)S(1)}, f32[1,384]{1,0:T(1,128)S(1)}, u32[]{:S(2)}, u32[]{:S(2)}) collective-permute-start(f32[1,384]{1,0:T(1,128)S(1)} %get-tuple-element.50.refs_4_), channel_id=1, source_target_pairs={{0,2},{2,0},{1,3},{3,1},{4,6},{6,4},{5,7},{7,5},{8,10},{10,8},{9,1... | collective-permute-start | bytes 4616 | tf_op jit(solution)/shard_map/ppermute | solution.py:22
  40.7 1.3 %collective-permute-start.4 = (f32[1,384]{1,0:T(1,128)S(1)}, f32[1,384]{1,0:T(1,128)S(1)}, u32[]{:S(2)}, u32[]{:S(2)}) collective-permute-start(f32[1,384]{1,0:T(1,128)S(1)} %get-tuple-element.51.refs_5_), channel_id=1, source_target_pairs={{0,2},{2,0},{1,3},{3,1},{4,6},{6,4},{5,7},{7,5},{8,10},{10,8},{9,1... | collective-permute-start | bytes 4616 | tf_op jit(solution)/shard_map/ppermute | solution.py:22
  41.1 1.4 %collective-permute-start.2 = (bf16[384,256]{1,0:T(8,128)(2,1)S(1)}, bf16[384,256]{1,0:T(8,128)(2,1)S(1)}, u32[]{:S(2)}, u32[]{:S(2)}) collective-permute-start(bf16[384,256]{1,0:T(8,128)(2,1)S(1)} %get-tuple-element.49), channel_id=1, source_target_pairs={{0,2},{2,0},{1,3},{3,1},{4,6},{6,4},{5,7},{7,5},{8,10},{10,8},{9,1... | collective-permute-start | bytes 589832 | tf_op jit(solution)/shard_map/ppermute | solution.py:22
  43.8 16.6 %all-to-all-start.1 = ((bf16[16,64,256]{2,1,0:T(8,128)(2,1)}), bf16[16,64,256]{2,1,0:T(8,128)(2,1)S(1)}, u32[]{:S(2)}, u32[]{:S(2)}) async-start(bf16[16,64,256]{2,1,0:T(8,128)(2,1)} %packed.1), calls=%async_computation.1 | async-start | bytes 1048576 | tf_op jit(solution)/shard_map/all_to_all | solution.py:384
  61.4 11.7 %all-to-all-start.2 = ((bf16[8,16,256]{2,1,0:T(8,128)(2,1)}), bf16[8,16,256]{2,1,0:T(8,128)(2,1)S(1)}, u32[]{:S(2)}, u32[]{:S(2)}) async-start(bf16[8,16,256]{2,1,0:T(8,128)(2,1)} %middle.1), calls=%async_computation.2 | async-start | bytes 131072 | tf_op jit(solution)/shard_map/all_to_all | solution.py:386

commit v5 on v4

--- a/solution.py
+++ b/solution.py
@@ -93,13 +93,20 @@
     return jnp.broadcast_to(line, (128, line.shape[1])).T[:, :1]
 
 
+def three_parts(x):
+    high = x.astype(BF16).astype(F32)
+    rest = x - high
+    middle = rest.astype(BF16).astype(F32)
+    return [high, middle, rest - middle]
+
+
 def share_kernel(
-    first_ref, given_ref, items_ref, grad_ref, rows_ref, log_ref, place_ref, states_ref,
-    scores, places, grad, picked,
+    far, first_ref, given_ref, items_ref, log_ref, place_ref, states_ref, grad_ref, *rest
 ):
+    scores, places, grad, picked = rest[-4:]
     rows = given_ref.shape[0] - 1
     chips = given_ref.shape[1]
-    count, _ = states_ref.shape
+    count, width = states_ref.shape
     items = items_ref.shape[0]
     block = min(BLOCK, items)
     lanes = min(128, block)
@@ -141,26 +148,45 @@
         more = jnp.dot(jnp.concatenate(hot, axis=1), table, preferred_element_type=F32)
         picked[...] = more if at == 0 else picked[...] + more
     log_sum = high + jnp.log(jnp.sum(total, axis=1, keepdims=True))
-    log_ref[...] = jnp.broadcast_to(log_sum, (count, 128)).T[:1, :]
-    grad_ref[...] = grad[...] * jnp.exp(high - log_sum)
-    rows_ref[...] = picked[...].astype(BF16)
-
-
-def shares(first, given, items):
+    line = jnp.broadcast_to(log_sum, (count, 128)).T[:1, :]
+    log_ref[...] = line
+    share = grad[...] * jnp.exp(high - log_sum)
+    if not far:
+        grad_ref[...] = share
+        rest[0][...] = picked[...].astype(BF16)
+        return
+    grad_ref[:count, :] = share.astype(BF16)
+    grad_ref[count : 2 * count, :] = picked[...].astype(BF16)
+    lines = [
+        piece[:, at : at + chips] for piece in three_parts(line) for at in range(0, count, chips)
+    ]
+    lines = jnp.concatenate(lines + [jnp.zeros((-len(lines) % 16, chips), F32)])
+    lines = jnp.concatenate([lines, jnp.zeros((lines.shape[0], width - chips), F32)], axis=1)
+    grad_ref[2 * count :, :] = lines.astype(BF16)
+
+
+def shares(far, first, given, items):
     height, chips, width = given.shape
     count = (height - 1) * chips
-    return pl.pallas_call(
-        share_kernel,
-        name="shares",
-        out_shape=(
+    lines = 3 * (height - 1)
+    results = [
+        jax.ShapeDtypeStruct((1, count), F32),
+        jax.ShapeDtypeStruct((1, count), jnp.int32),
+        jax.ShapeDtypeStruct((count, width), BF16),
+    ]
+    if far:
+        results += [jax.ShapeDtypeStruct((2 * count + lines + -lines % 16, width), BF16)]
+    else:
+        results += [
             jax.ShapeDtypeStruct((count, width), F32),
             jax.ShapeDtypeStruct((count, width), BF16),
-            jax.ShapeDtypeStruct((1, count), F32),
-            jax.ShapeDtypeStruct((1, count), jnp.int32),
-            jax.ShapeDtypeStruct((count, width), BF16),
-        ),
+        ]
+    return pl.pallas_call(
+        lambda *refs: share_kernel(far, *refs),
+        name="shares",
+        out_shape=results,
         in_specs=[pl.BlockSpec(memory_space=pltpu.SMEM), *in_vmem(2)],
-        out_specs=in_vmem(5),
+        out_specs=in_vmem(len(results)),
         scratch_shapes=[
             pltpu.VMEM((count, items.shape[0]), F32),
             pltpu.VMEM((count, min(128, BLOCK)), jnp.int32),
@@ -171,30 +197,27 @@
     )(first, given, items)
 
 
-def three_parts(x):
-    high = x.astype(BF16).astype(F32)
-    rest = x - high
-    middle = rest.astype(BF16).astype(F32)
-    return [high, middle, rest - middle]
-
-
 def pack_kernel(
-    rows, own_grad_ref, other_grad_ref, own_rows_ref, other_rows_ref,
-    own_log_ref, far_log_ref, other_log_ref, other_far_log_ref, out_ref,
+    rows, own_grad_ref, own_rows_ref, other_ref, own_log_ref, far_log_ref, other_log_ref, out_ref
 ):
     length, _, width = out_ref.shape
     part = own_grad_ref.shape[0]
     own = jnp.concatenate([own_log_ref[...], far_log_ref[...]], axis=1)
-    other = jnp.concatenate([other_far_log_ref[...], other_log_ref[...]], axis=1)
+    lines = other_ref[2 * part :, :].astype(F32)
+    chips = part // rows
+    other = [
+        sum(lines[j * rows + k : j * rows + k + 1, :chips] for j in range(3)) for k in range(rows)
+    ]
+    other = jnp.concatenate(other + [other_log_ref[...]], axis=1)
     top = jnp.maximum(own, other)
     both = top + jnp.log(jnp.exp(own - top) + jnp.exp(other - top))
     grad = own_grad_ref[...] * column(jnp.exp(own - both)[:, :part])
-    grad += other_grad_ref[...] * column(jnp.exp(other - both)[:, :part])
-    picked = own_rows_ref[...].astype(F32) + other_rows_ref[...].astype(F32)
+    grad += other_ref[:part, :].astype(F32) * column(jnp.exp(other - both)[:, :part])
+    picked = own_rows_ref[...].astype(F32) + other_ref[part : 2 * part, :].astype(F32)
     lines = [
         piece[:, at : at + width] for piece in three_parts(both) for at in range(0, 2 * part, width)
     ]
-    lines = jnp.concatenate(lines + [jnp.zeros((-len(lines) % 8, width), F32)])
+    lines = jnp.concatenate(lines)
     across = lambda x: [
         x.reshape(rows, length, -1, width)[k] for k in range(rows)
     ]
@@ -205,12 +228,12 @@
 def packed(rows, length, *pieces):
     part, width = pieces[0].shape
     lines = 3 * 2 * part // width
-    height = 2 * (part // length) + lines + -lines % 8
+    height = 2 * (part // length) + lines
     return pl.pallas_call(
         lambda *refs: pack_kernel(rows, *refs),
         name="packed",
         out_shape=jax.ShapeDtypeStruct((length, height, width), BF16),
-        in_specs=in_vmem(8),
+        in_specs=in_vmem(6),
         out_specs=pl.BlockSpec(memory_space=pltpu.VMEM),
         compiler_params=pltpu.CompilerParams(vmem_limit_bytes=12 * MIB),
     )(*pieces)
@@ -375,11 +398,12 @@
     mine = jnp.swapaxes(mine, 0, 1)
     first_own = first_own.reshape(1)
     other = from_pair(mine)
-    own_grad, own_picked, own_logs, place, states = shares(first_own, mine, items)
-    far_grad, far_picked, far_logs, far_place, far_states = shares(first_own, other, items)
+    own_logs, place, states, own_grad, own_picked = shares(False, first_own, mine, items)
+    other_logs = from_pair(own_logs)
+    far_logs, far_place, far_states, far_share = shares(True, first_own, other, items)
     sent = packed(
-        rows, lax.axis_size(PLANE), own_grad, from_pair(far_grad), own_picked,
-        from_pair(far_picked), own_logs, far_logs, from_pair(own_logs), from_pair(far_logs),
+        rows, lax.axis_size(PLANE), own_grad, own_picked, from_pair(far_share),
+        own_logs, far_logs, other_logs,
     )
     arrived = lax.all_to_all(sent, PLANE, 0, 0, tiled=True)
     sent = middle(rows, lax.axis_size("z"), lax.axis_index(PLANE).reshape(1), arrived)

time: 78.3 us -> 84 us (1.073)
  local copies, waits for them, and re-layouts: 1.78 us -> 5.23 us
  Pallas kernels: 15.4 us -> 17.3 us
    unnamed x4 -> x20, local copies, waits for them, and re-layouts: 0.01 us -> 3.47 us
    pallas_call x2, Pallas kernels: 6.93 us -> 8.18 us  [shares(): pl.pallas_call(lambda *refs: share_kernel(far, *refs), name='shares', out...]
  transfers between devices with their start and end apart: 8 -> 6, of which waited for: 6 -> 4; matrix products, arithmetic and copies ran while one was open for 3% -> 3% of each run, Pallas kernels for 4% -> 5%
where the time goes in v5:
time: 84 us; the launch traced here: 83.6 us
  waiting for transfers between devices  33.6 us (40%)
  starting transfers between devices  25.6 us (30%)
  Pallas kernels  17.3 us (21%)
  local copies, waits for them, and re-layouts  5.23 us (6%)
  between operations  0.95 us (1%)
  other arithmetic  0.91 us (1%)
    all_to_all x1, starting transfers between devices, steps(): mine = lax.all_to_all(sent, CHIPS, 0, 0, tiled=True)  15.4 us
    all_to_all x1, waiting for transfers between devices, steps(): mine = lax.all_to_all(sent, CHIPS, 0, 0, tiled=True)  13.5 us
    all_to_all x1, waiting for transfers between devices, steps(): arrived = lax.all_to_all(sent, PLANE, 0, 0, tiled=True)  10.8 us
    all_to_all x1, waiting for transfers between devices, steps(): arrived = lax.all_to_all(sent, 'z', 0, 0, tiled=True)  8.27 us
    pallas_call x2, Pallas kernels, shares(): pl.pallas_call(lambda *refs: share_kernel(far, *refs), name='shares', out...  8.18 us
    all_to_all x1, starting transfers between devices, steps(): arrived = lax.all_to_all(sent, PLANE, 0, 0, tiled=True)  5.8 us
    pallas_call x1, Pallas kernels, last(): pl.pallas_call(last_kernel, name='last', out_shape=(jax.ShapeDtypeStruct(...  4.77 us
    unnamed x20, local copies, waits for them, and re-layouts  3.47 us
  transfers between devices with their start and end apart: 6, of which 4 were waited for; matrix products, arithmetic and copies ran while one was open for 3% of the time, Pallas kernels for 5%

profile of v5, /device:TPU:8, one launch (start us, length us, event | category | flops | bytes accessed | tf_op | source)
XLA Modules:
  0.0 83.6 jit_solution(14302411464439130935)
XLA Ops:
  0.6 1.5 %spread.1 = bf16[128,4,256]{2,1,0:T(4,128)(2,1)} custom-call(s32[3]{0:T(128)} %targets_hbm.1, bf16[3,256]{1,0:T(4,128)(2,1)} %hidden_ref.1), custom_call_target="tpu_custom_call" | custom-call | tf_op jit(solution)/shard_map/spread/pallas_call | solution.py:49
  2.1 15.4 %all-to-all-start = ((bf16[128,4,256]{2,1,0:T(4,128)(2,1)}), bf16[128,4,256]{2,1,0:T(4,128)(2,1)S(1)}, u32[]{:S(2)}, u32[]{:S(2)}) async-start(bf16[128,4,256]{2,1,0:T(4,128)(2,1)} %spread.1), calls=%async_computation | async-start | bytes 524288 | tf_op jit(solution)/shard_map/all_to_all | solution.py:397
  17.5 13.5 %all-to-all-done = bf16[128,4,256]{2,1,0:T(4,128)(2,1)S(1)} async-done(((bf16[128,4,256]{2,1,0:T(4,128)(2,1)}), bf16[128,4,256]{2,1,0:T(4,128)(2,1)S(1)}, u32[]{:S(2)}, u32[]{:S(2)}) %all-to-all-start) | async-done | bytes 262176 | tf_op jit(solution)/shard_map/all_to_all | solution.py:397
  31.1 0.1 collective-permute-start
  31.2 1.7 %constant_dynamic-slice_fusion.refs_2_.items_ref = bf16[4096,256]{1,0:T(8,128)(2,1)S(1)} fusion(bf16[8192,256]{1,0:T(8,128)(2,1)} %param.13, s32[]{:T(128)S(6)} %select_n.87), kind=kLoop, calls=%fused_computation.83 | loop fusion | bytes 4194308 | tf_op jit(solution)/shard_map/dynamic_slice | solution.py:393
  32.9 0.0 copy-start.9
  32.9 0.0 collective-permute-done.refs_1_
  32.9 4.2 %shares.3 = (f32[1,384]{1,0:T(1,128)S(1)}, s32[1,384]{1,0:T(1,128)S(1)}, bf16[384,256]{1,0:T(8,128)(2,1)S(1)}, bf16[784,256]{1,0:T(8,128)(2,1)}) custom-call(s32[1]{0:T(128)} %bitcast.2.refs_0_, bf16[4,128,256]{2,1,0:T(8,128)(2,1)S(1)} %collective-permute-done.refs_1_, bf16[4096,256]{1,0:T(8,128)(2,1)S(1)} %constant_dynamic-slice_fusion.refs_2_.items_ref), custom_call_target="tpu_custom_call" | custom-call | tf_op jit(solution)/shard_map/shares/pallas_call | solution.py:184
  37.2 0.0 copy-start.5
  37.2 0.5 collective-permute-start.1
  37.7 0.0 copy-done.9
  37.7 0.1 select_reduce_fusion.1
  37.8 0.0 copy-done.5
  37.8 0.6 fusion.41
  38.4 4.0 %shares.2 = (f32[1,384]{1,0:T(1,128)}, s32[1,384]{1,0:T(1,128)S(1)}, bf16[384,256]{1,0:T(8,128)(2,1)S(1)}, f32[384,256]{1,0:T(8,128)S(1)}, bf16[384,256]{1,0:T(8,128)(2,1)S(1)}) custom-call(s32[1]{0:T(128)} %bitcast.2.refs_0_, bf16[4,128,256]{2,1,0:T(8,128)(2,1)S(1)} %bitcast.8, bf16[4096,256]{1,0:T(8,128)(2,1)S(1)} %constant_dynamic-slice_fusion.refs_2_.items_ref), custom_call_target="tpu_custom_call" | custom-call | tf_op jit(solution)/shard_map/shares/pallas_call | solution.py:184
  42.3 0.0 copy-start
  42.3 0.7 copy-done
  43.0 0.0 copy-start.3
  43.0 0.5 copy-done.3
  43.5 0.0 copy-start.7
  43.5 0.0 copy-start.8
  43.5 0.0 copy-start.2
  43.5 0.5 collective-permute-start.2
  44.0 0.1 fusion.9
  44.1 1.0 %collective-permute-done.2.refs_5_ = f32[1,384]{1,0:T(1,128)S(1)} collective-permute-done((f32[1,384]{1,0:T(1,128)}, f32[1,384]{1,0:T(1,128)S(1)}, u32[]{:S(2)}, u32[]{:S(2)}) %collective-permute-start.2) | collective-permute-done | bytes 1568 | tf_op jit(solution)/shard_map/ppermute | solution.py:22
  45.0 0.0 collective-permute-done.1.refs_2_
  45.0 0.0 copy-start.1
  45.1 0.9 %copy-done.1 = bf16[384,256]{1,0:T(8,128)(2,1)S(1)} copy-done((bf16[384,256]{1,0:T(8,128)(2,1)S(1)}, bf16[384,256]{1,0:T(8,128)(2,1)}, u32[]{:S(2)}) %copy-start.1) | copy-done | bytes 196632
  46.0 0.0 copy-start.6
  46.0 0.7 copy-done.6
  46.6 1.9 %packed.1 = bf16[16,57,256]{2,1,0:T(8,128)(2,1)} custom-call(f32[384,256]{1,0:T(8,128)S(1)} %get-tuple-element.45.refs_0_, bf16[384,256]{1,0:T(8,128)(2,1)S(1)} %copy-done.1, bf16[784,256]{1,0:T(8,128)(2,1)S(1)} %collective-permute-done.1.refs_2_, f32[1,384]{1,0:T(1,128)} %get-tuple-element.48.refs_3_, f32[1,384]{1,0:T(1,128)S(1)} %copy-done.6, ...), custom_call_target="tpu_custom_call" | custom-call | tf_op jit(solution)/shard_map/packed/pallas_call | solution.py:232
  48.5 5.8 %all-to-all-start.1 = ((bf16[16,57,256]{2,1,0:T(8,128)(2,1)}), bf16[16,57,256]{2,1,0:T(8,128)(2,1)S(1)}, u32[]{:S(2)}, u32[]{:S(2)}) async-start(bf16[16,57,256]{2,1,0:T(8,128)(2,1)} %packed.1), calls=%async_computation.1 | async-start | bytes 1048576 | tf_op jit(solution)/shard_map/all_to_all | solution.py:408
  54.4 0.0 copy-done.7
  54.4 0.0 copy-done.8
  54.4 0.1 select_reduce_fusion
  54.5 10.8 %all-to-all-done.1.refs_1_ = bf16[16,57,256]{2,1,0:T(8,128)(2,1)S(1)} async-done(((bf16[16,57,256]{2,1,0:T(8,128)(2,1)}), bf16[16,57,256]{2,1,0:T(8,128)(2,1)S(1)}, u32[]{:S(2)}, u32[]{:S(2)}) %all-to-all-start.1) | async-done | bytes 466976 | tf_op jit(solution)/shard_map/all_to_all | solution.py:408
  65.3 1.0 %middle.1 = bf16[8,16,256]{2,1,0:T(8,128)(2,1)} custom-call(s32[1]{0:T(128)} %bitcast.1.refs_0_, bf16[16,57,256]{2,1,0:T(8,128)(2,1)S(1)} %all-to-all-done.1.refs_1_), custom_call_target="tpu_custom_call" | custom-call | tf_op jit(solution)/shard_map/middle/pallas_call | solution.py:286
  66.3 3.4 %all-to-all-start.2 = ((bf16[8,16,256]{2,1,0:T(8,128)(2,1)}), bf16[8,16,256]{2,1,0:T(8,128)(2,1)S(1)}, u32[]{:S(2)}, u32[]{:S(2)}) async-start(bf16[8,16,256]{2,1,0:T(8,128)(2,1)} %middle.1), calls=%async_computation.2 | async-start | bytes 131072 | tf_op jit(solution)/shard_map/all_to_all | solution.py:410
  69.7 8.3 %all-to-all-done.2.arrived_ref = bf16[8,16,256]{2,1,0:T(8,128)(2,1)S(1)} async-done(((bf16[8,16,256]{2,1,0:T(8,128)(2,1)}), bf16[8,16,256]{2,1,0:T(8,128)(2,1)S(1)}, u32[]{:S(2)}, u32[]{:S(2)}) %all-to-all-start.2) | async-done | bytes 65568 | tf_op jit(solution)/shard_map/all_to_all | solution.py:410
  78.0 0.0 copy-done.2
  78.0 0.0 copy-start.4
  78.0 0.6 copy-done.4
  78.6 4.8 %last.1 = (f32[1,3]{1,0:T(1,128)}, bf16[3,256]{1,0:T(4,128)(2,1)}, bf16[4096,256]{1,0:T(8,128)(2,1)}) custom-call(s32[1]{0:T(128)} %bitcast.chip_ref, bf16[8,16,256]{2,1,0:T(8,128)(2,1)S(1)} %all-to-all-done.2.arrived_ref, s32[1,384]{1,0:T(1,128)S(1)} %copy-done.4, s32[1,384]{1,0:T(1,128)S(1)} %get-tuple-element.51.far_place_ref, ...), custom_call_target="tpu_custom_call" | custom-call | tf_op jit(solution)/shard_map/last/pallas_call | solution.py:367
  (6 shorter events, 0.1 us)
Async XLA Ops:
  2.1 28.9 %all-to-all-start = ((bf16[128,4,256]{2,1,0:T(4,128)(2,1)}), bf16[128,4,256]{2,1,0:T(4,128)(2,1)S(1)}, u32[]{:S(2)}, u32[]{:S(2)}) async-start(bf16[128,4,256]{2,1,0:T(4,128)(2,1)} %spread.1), calls=%async_computation | async-start | bytes 524288 | tf_op jit(solution)/shard_map/all_to_all | solution.py:397
  31.1 1.9 %collective-permute-start = (bf16[4,128,256]{2,1,0:T(8,128)(2,1)S(1)}, bf16[4,128,256]{2,1,0:T(8,128)(2,1)S(1)}, u32[]{:S(2)}, u32[]{:S(2)}) collective-permute-start(bf16[4,128,256]{2,1,0:T(8,128)(2,1)S(1)} %bitcast.7), channel_id=1, source_target_pairs={{0,2},{2,0},{1,3},{3,1},{4,6},{6,4},{5,7},{7,5},{8,10},{10,8},{9,1... | collective-permute-start | bytes 786440 | tf_op jit(solution)/shard_map/ppermute | solution.py:22
  32.9 4.8 %copy-start.9 = (s32[2,16]{1,0:T(2,128)S(1)}, s32[2,16]{1,0:T(2,128)}, u32[]{:S(2)}) copy-start(s32[2,16]{1,0:T(2,128)} %param.15) | copy-start | bytes 388
  37.2 0.6 copy-start.5
  37.2 7.9 %collective-permute-start.1 = (bf16[784,256]{1,0:T(8,128)(2,1)}, bf16[784,256]{1,0:T(8,128)(2,1)S(1)}, u32[]{:S(2)}, u32[]{:S(2)}) collective-permute-start(bf16[784,256]{1,0:T(8,128)(2,1)} %get-tuple-element.47), channel_id=1, source_target_pairs={{0,2},{2,0},{1,3},{3,1},{4,6},{6,4},{5,7},{7,5},{8,10},{10,8},{9,1... | collective-permute-start | bytes 1204232 | tf_op jit(solution)/shard_map/ppermute | solution.py:22
  42.3 0.7 copy-start
  43.0 0.5 copy-start.3
  43.5 10.8 %copy-start.7 = (s32[2,16]{1,0:T(2,128)S(1)}, s32[2,16]{1,0:T(2,128)}, u32[]{:S(2)}) copy-start(s32[2,16]{1,0:T(2,128)} %get-tuple-element.69) | copy-start | bytes 388
  43.5 10.8 %copy-start.8 = (f32[2,16]{1,0:T(2,128)S(1)}, f32[2,16]{1,0:T(2,128)}, u32[]{:S(2)}) copy-start(f32[2,16]{1,0:T(2,128)} %get-tuple-element.70) | copy-start | bytes 388
  43.5 34.5 %copy-start.2 = (bf16[3,256]{1,0:T(4,128)(2,1)S(1)}, bf16[3,256]{1,0:T(4,128)(2,1)}, u32[]{:S(2)}) copy-start(bf16[3,256]{1,0:T(4,128)(2,1)} %hidden_ref.1) | copy-start | bytes 4612
  43.5 1.5 %collective-permute-start.2 = (f32[1,384]{1,0:T(1,128)}, f32[1,384]{1,0:T(1,128)S(1)}, u32[]{:S(2)}, u32[]{:S(2)}) collective-permute-start(f32[1,384]{1,0:T(1,128)} %get-tuple-element.48.refs_3_), channel_id=1, source_target_pairs={{0,2},{2,0},{1,3},{3,1},{4,6},{6,4},{5,7},{7,5},{8,10},{10,8},{9,1... | collective-permute-start | bytes 4616 | tf_op jit(solution)/shard_map/ppermute | solution.py:22
  45.0 0.9 %copy-start.1 = (bf16[384,256]{1,0:T(8,128)(2,1)S(1)}, bf16[384,256]{1,0:T(8,128)(2,1)}, u32[]{:S(2)}) copy-start(bf16[384,256]{1,0:T(8,128)(2,1)} %copy-done) | copy-start | bytes 589828
  46.0 0.7 copy-start.6
  48.5 16.8 %all-to-all-start.1 = ((bf16[16,57,256]{2,1,0:T(8,128)(2,1)}), bf16[16,57,256]{2,1,0:T(8,128)(2,1)S(1)}, u32[]{:S(2)}, u32[]{:S(2)}) async-start(bf16[16,57,256]{2,1,0:T(8,128)(2,1)} %packed.1), calls=%async_computation.1 | async-start | bytes 1048576 | tf_op jit(solution)/shard_map/all_to_all | solution.py:408
  66.3 11.7 %all-to-all-start.2 = ((bf16[8,16,256]{2,1,0:T(8,128)(2,1)}), bf16[8,16,256]{2,1,0:T(8,128)(2,1)S(1)}, u32[]{:S(2)}, u32[]{:S(2)}) async-start(bf16[8,16,256]{2,1,0:T(8,128)(2,1)} %middle.1), calls=%async_computation.2 | async-start | bytes 131072 | tf_op jit(solution)/shard_map/all_to_all | solution.py:410
  78.0 0.6 copy-start.4

commit v6 on v5

--- a/solution.py
+++ b/solution.py
@@ -101,7 +101,8 @@
 
 
 def share_kernel(
-    far, first_ref, given_ref, items_ref, log_ref, place_ref, states_ref, grad_ref, *rest
+    far, first_ref, given_ref, items_ref, near_log_ref, log_ref, place_ref, states_ref, grad_ref,
+    *rest,
 ):
     scores, places, grad, picked = rest[-4:]
     rows = given_ref.shape[0] - 1
@@ -158,17 +159,20 @@
     grad_ref[:count, :] = share.astype(BF16)
     grad_ref[count : 2 * count, :] = picked[...].astype(BF16)
     lines = [
-        piece[:, at : at + chips] for piece in three_parts(line) for at in range(0, count, chips)
+        piece[:, at : at + chips]
+        for source in (line, near_log_ref[...])
+        for piece in three_parts(source)
+        for at in range(0, count, chips)
     ]
     lines = jnp.concatenate(lines + [jnp.zeros((-len(lines) % 16, chips), F32)])
     lines = jnp.concatenate([lines, jnp.zeros((lines.shape[0], width - chips), F32)], axis=1)
     grad_ref[2 * count :, :] = lines.astype(BF16)
 
 
-def shares(far, first, given, items):
+def shares(far, first, given, items, near_logs):
     height, chips, width = given.shape
     count = (height - 1) * chips
-    lines = 3 * (height - 1)
+    lines = 6 * (height - 1)
     results = [
         jax.ShapeDtypeStruct((1, count), F32),
         jax.ShapeDtypeStruct((1, count), jnp.int32),
@@ -185,7 +189,7 @@
         lambda *refs: share_kernel(far, *refs),
         name="shares",
         out_shape=results,
-        in_specs=[pl.BlockSpec(memory_space=pltpu.SMEM), *in_vmem(2)],
+        in_specs=[pl.BlockSpec(memory_space=pltpu.SMEM), *in_vmem(3)],
         out_specs=in_vmem(len(results)),
         scratch_shapes=[
             pltpu.VMEM((count, items.shape[0]), F32),
@@ -194,11 +198,11 @@
             pltpu.VMEM((count, width), F32),
         ],
         compiler_params=pltpu.CompilerParams(vmem_limit_bytes=24 * MIB),
-    )(first, given, items)
+    )(first, given, items, near_logs)
 
 
 def pack_kernel(
-    rows, own_grad_ref, own_rows_ref, other_ref, own_log_ref, far_log_ref, other_log_ref, out_ref
+    rows, own_grad_ref, own_rows_ref, other_ref, own_log_ref, far_log_ref, out_ref
 ):
     length, _, width = out_ref.shape
     part = own_grad_ref.shape[0]
@@ -206,9 +210,11 @@
     lines = other_ref[2 * part :, :].astype(F32)
     chips = part // rows
     other = [
-        sum(lines[j * rows + k : j * rows + k + 1, :chips] for j in range(3)) for k in range(rows)
-    ]
-    other = jnp.concatenate(other + [other_log_ref[...]], axis=1)
+        sum(lines[at + j * rows + k : at + j * rows + k + 1, :chips] for j in range(3))
+        for at in (0, 3 * rows)
+        for k in range(rows)
+    ]
+    other = jnp.concatenate(other, axis=1)
     top = jnp.maximum(own, other)
     both = top + jnp.log(jnp.exp(own - top) + jnp.exp(other - top))
     grad = own_grad_ref[...] * column(jnp.exp(own - both)[:, :part])
@@ -233,7 +239,7 @@
         lambda *refs: pack_kernel(rows, *refs),
         name="packed",
         out_shape=jax.ShapeDtypeStruct((length, height, width), BF16),
-        in_specs=in_vmem(6),
+        in_specs=in_vmem(5),
         out_specs=pl.BlockSpec(memory_space=pltpu.VMEM),
         compiler_params=pltpu.CompilerParams(vmem_limit_bytes=12 * MIB),
     )(*pieces)
@@ -297,10 +303,41 @@
     )(plane, arrived)
 
 
+def early_kernel(log_ref, far_log_ref, states_ref, far_states_ref, items_ref, out_ref, states):
+    part = states_ref.shape[0]
+    items, block = out_ref.shape[0], min(BLOCK, items_ref.shape[0])
+    first = items_ref.shape[0] - items
+    states[:part, :] = states_ref[...]
+    states[part:, :] = far_states_ref[...]
+    logs = jnp.concatenate([log_ref[...], far_log_ref[...]], axis=1)
+    for at in range(0, items, block):
+        scores = lax.dot_general(
+            items_ref[first + at : first + at + block, :], states[...], (((1,), (1,)), ((), ())),
+            preferred_element_type=F32,
+        )
+        out_ref[at : at + block, :] = jnp.exp(scores - logs)
+
+
+def early(logs, far_logs, states, far_states, items):
+    part, width = states.shape
+    block = min(BLOCK, items.shape[0])
+    steps = items.shape[0] // block // 2
+    return pl.pallas_call(
+        early_kernel,
+        name="early",
+        out_shape=jax.ShapeDtypeStruct((steps * block, 2 * part), F32),
+        in_specs=in_vmem(5),
+        out_specs=pl.BlockSpec(memory_space=pltpu.VMEM),
+        scratch_shapes=[pltpu.VMEM((2 * part, width), BF16)],
+        compiler_params=pltpu.CompilerParams(vmem_limit_bytes=24 * MIB),
+    )(logs, far_logs, states, far_states, items)
+
+
 def last_kernel(
     chip_ref, arrived_ref, place_ref, far_place_ref, weight_ref, hidden_ref, states_ref,
-    far_states_ref, items_ref, loss_hbm, hidden_grad_hbm, table_grad_hbm,
-    states, buffer, loss_ref, hidden_grad_ref, sems,
+    far_states_ref, items_ref, log_ref, far_log_ref, early_hbm,
+    loss_hbm, hidden_grad_hbm, table_grad_hbm,
+    states, buffer, loss_ref, hidden_grad_ref, early_ref, sems, early_sems,
 ):
     rows, width = hidden_ref.shape
     depth = arrived_ref.shape[0]
@@ -310,6 +347,14 @@
     chips = count // (2 * rows)
     wide = count // width
     copies = []
+    fetches = [
+        pltpu.make_async_copy(
+            early_hbm.at[pl.ds(at, block)], early_ref.at[pl.ds(at, block)], early_sems.at[step]
+        )
+        for step, at in enumerate(range(0, early_ref.shape[0], block))
+    ]
+    for fetch in fetches:
+        fetch.start()
 
     def send(source, target):
         copies.append(pltpu.make_async_copy(source, target, sems.at[len(copies)]))
@@ -346,14 +391,22 @@
     places = jnp.concatenate([place_ref[...], far_place_ref[...]], axis=1)
     states[: count // 2, :] = states_ref[...]
     states[count // 2 :, :] = far_states_ref[...]
+    given = jnp.concatenate([log_ref[...], far_log_ref[...]], axis=1)
+    factor = weight * jnp.exp(given - line)
+    first = items - early_ref.shape[0]
     for at in range(0, items, block):
-        scores = lax.dot_general(
-            items_ref[at : at + block, :], states[...], (((1,), (1,)), ((), ())),
-            preferred_element_type=F32,
-        )
-        parts = jnp.exp(scores - line)
-        matched = lax.broadcasted_iota(jnp.int32, parts.shape, 0) == places - at
-        signal = (weight * jnp.where(matched, parts - 1.0, parts)).astype(BF16)
+        matched = lax.broadcasted_iota(jnp.int32, (block, count), 0) == places - at
+        if at < first:
+            scores = lax.dot_general(
+                items_ref[at : at + block, :], states[...], (((1,), (1,)), ((), ())),
+                preferred_element_type=F32,
+            )
+            parts = jnp.exp(scores - line)
+            signal = (weight * jnp.where(matched, parts - 1.0, parts)).astype(BF16)
+        else:
+            fetches[(at - first) // block].wait()
+            parts = early_ref[at - first : at - first + block, :] * factor
+            signal = jnp.where(matched, parts - weight, parts).astype(BF16)
         buffer[at : at + block, :] = jnp.dot(
             signal, states[...], preferred_element_type=F32
         ).astype(BF16)
@@ -362,7 +415,9 @@
         copy.wait()
 
 
-def last(chip, arrived, place, far_place, weight, hidden, states, far_states, items):
+def last(
+    chip, arrived, place, far_place, weight, hidden, states, far_states, items, logs, far_logs, parts
+):
     rows, width = hidden.shape
     return pl.pallas_call(
         last_kernel,
@@ -372,17 +427,22 @@
             jax.ShapeDtypeStruct((rows, width), BF16),
             jax.ShapeDtypeStruct(items.shape, BF16),
         ),
-        in_specs=[pl.BlockSpec(memory_space=pltpu.SMEM), *in_vmem(8)],
+        in_specs=[pl.BlockSpec(memory_space=pltpu.SMEM), *in_vmem(10), pl.BlockSpec(memory_space=pltpu.HBM)],
         out_specs=[pl.BlockSpec(memory_space=pltpu.HBM)] * 3,
         scratch_shapes=[
             pltpu.VMEM((2 * states.shape[0], width), BF16),
             pltpu.VMEM(items.shape, BF16),
             pltpu.VMEM((1, rows), F32),
             pltpu.VMEM((rows, width), BF16),
+            pltpu.VMEM(parts.shape, F32),
             pltpu.SemaphoreType.DMA((2 + items.shape[0] // min(BLOCK, items.shape[0]),)),
+            pltpu.SemaphoreType.DMA((parts.shape[0] // min(BLOCK, items.shape[0]),)),
         ],
-        compiler_params=pltpu.CompilerParams(vmem_limit_bytes=16 * MIB),
-    )(chip, arrived, place, far_place, weight, hidden, states, far_states, items)
+        compiler_params=pltpu.CompilerParams(vmem_limit_bytes=24 * MIB),
+    )(
+        chip, arrived, place, far_place, weight, hidden, states, far_states, items,
+        logs, far_logs, in_hbm(parts),
+    )
 
 
 def steps(hidden, item_table, targets, lengths):
@@ -398,18 +458,22 @@
     mine = jnp.swapaxes(mine, 0, 1)
     first_own = first_own.reshape(1)
     other = from_pair(mine)
-    own_logs, place, states, own_grad, own_picked = shares(False, first_own, mine, items)
-    other_logs = from_pair(own_logs)
-    far_logs, far_place, far_states, far_share = shares(True, first_own, other, items)
+    no_logs = jnp.zeros((1, rows * lax.axis_size(CHIPS)), F32)
+    own_logs, place, states, own_grad, own_picked = shares(False, first_own, mine, items, no_logs)
+    far_logs, far_place, far_states, far_share = shares(
+        True, first_own, other, items, own_logs
+    )
     sent = packed(
         rows, lax.axis_size(PLANE), own_grad, own_picked, from_pair(far_share),
-        own_logs, far_logs, other_logs,
+        own_logs, far_logs,
     )
     arrived = lax.all_to_all(sent, PLANE, 0, 0, tiled=True)
     sent = middle(rows, lax.axis_size("z"), lax.axis_index(PLANE).reshape(1), arrived)
     arrived = lax.all_to_all(sent, "z", 0, 0, tiled=True)
+    parts = early(own_logs, far_logs, states, far_states, items)
     row_loss, hidden_grad, table_grad = last(
-        chip, arrived, place, far_place, weight, hidden, states, far_states, items
+        chip, arrived, place, far_place, weight, hidden, states, far_states, items,
+        own_logs, far_logs, parts,
     )
     return (row_loss.reshape(-1), hidden_grad, table_grad)
 

time: 84 us -> 80.3 us (0.956)
  waiting for transfers between devices: 33.6 us -> 30 us
  Pallas kernels: 17.3 us -> 18.8 us
    all_to_all x1, waiting for transfers between devices: 8.27 us -> 4.38 us  [steps(): arrived = lax.all_to_all(sent, 'z', 0, 0, tiled=True)]
    pallas_call x1, Pallas kernels: 4.77 us -> 7.16 us  [last(): pl.pallas_call(last_kernel, name='last', out_shape=(jax.ShapeDtypeStruct(...]
    pallas_call x2, Pallas kernels: 8.18 us -> 6.95 us  [shares(): pl.pallas_call(lambda *refs: share_kernel(far, *refs), name='shares', out...]
    pallas_call x0 -> x1, Pallas kernels: none -> 1.01 us  [early(): pl.pallas_call(early_kernel, name='early', out_shape=jax.ShapeDtypeStruct...]
    unnamed x20 -> x6, local copies, waits for them, and re-layouts: 3.47 us -> 2.67 us
  transfers between devices with their start and end apart: 6 -> 5, of which waited for: 4 -> 4; matrix products, arithmetic and copies ran while one was open for 3% -> 3% of each run, Pallas kernels for 5% -> 6%
where the time goes in v6:
time: 80.3 us; the launch traced here: 79.9 us
  waiting for transfers between devices  30 us (37%)
  starting transfers between devices  25.4 us (32%)
  Pallas kernels  18.8 us (23%)
  local copies, waits for them, and re-layouts  4.44 us (6%)
  between operations  0.95 us (1%)
    all_to_all x1, starting transfers between devices, steps(): mine = lax.all_to_all(sent, CHIPS, 0, 0, tiled=True)  15.4 us
    all_to_all x1, waiting for transfers between devices, steps(): mine = lax.all_to_all(sent, CHIPS, 0, 0, tiled=True)  13.5 us
    all_to_all x1, waiting for transfers between devices, steps(): arrived = lax.all_to_all(sent, PLANE, 0, 0, tiled=True)  10.9 us
    pallas_call x1, Pallas kernels, last(): pl.pallas_call(last_kernel, name='last', out_shape=(jax.ShapeDtypeStruct(...  7.16 us
    pallas_call x2, Pallas kernels, shares(): pl.pallas_call(lambda *refs: share_kernel(far, *refs), name='shares', out...  6.95 us
    all_to_all x1, starting transfers between devices, steps(): arrived = lax.all_to_all(sent, PLANE, 0, 0, tiled=True)  5.8 us
    all_to_all x1, waiting for transfers between devices, steps(): arrived = lax.all_to_all(sent, 'z', 0, 0, tiled=True)  4.38 us
    all_to_all x1, starting transfers between devices, steps(): arrived = lax.all_to_all(sent, 'z', 0, 0, tiled=True)  3.53 us
  transfers between devices with their start and end apart: 5, of which 4 were waited for; matrix products, arithmetic and copies ran while one was open for 3% of the time, Pallas kernels for 6%

profile of v6, /device:TPU:8, one launch (start us, length us, event | category | flops | bytes accessed | tf_op | source)
XLA Modules:
  0.0 79.9 jit_solution(2175256877622535198)
XLA Ops:
  0.6 1.5 %spread.1 = bf16[128,4,256]{2,1,0:T(4,128)(2,1)} custom-call(s32[3]{0:T(128)} %targets_hbm.1, bf16[3,256]{1,0:T(4,128)(2,1)} %hidden_ref.1), custom_call_target="tpu_custom_call" | custom-call | tf_op jit(solution)/shard_map/spread/pallas_call | solution.py:49
  2.1 15.4 %all-to-all-start = ((bf16[128,4,256]{2,1,0:T(4,128)(2,1)}), bf16[128,4,256]{2,1,0:T(4,128)(2,1)S(1)}, u32[]{:S(2)}, u32[]{:S(2)}) async-start(bf16[128,4,256]{2,1,0:T(4,128)(2,1)} %spread.1), calls=%async_computation | async-start | bytes 524288 | tf_op jit(solution)/shard_map/all_to_all | solution.py:457
  17.5 13.5 %all-to-all-done = bf16[128,4,256]{2,1,0:T(4,128)(2,1)S(1)} async-done(((bf16[128,4,256]{2,1,0:T(4,128)(2,1)}), bf16[128,4,256]{2,1,0:T(4,128)(2,1)S(1)}, u32[]{:S(2)}, u32[]{:S(2)}) %all-to-all-start) | async-done | bytes 262176 | tf_op jit(solution)/shard_map/all_to_all | solution.py:457
  31.1 0.0 copy-start.2
  31.1 0.1 collective-permute-start
  31.2 1.7 %constant_dynamic-slice_fusion.refs_2_.items_ref = bf16[4096,256]{1,0:T(8,128)(2,1)S(1)} fusion(bf16[8192,256]{1,0:T(8,128)(2,1)} %param.13, s32[]{:T(128)S(6)} %select_n.87), kind=kLoop, calls=%fused_computation.83 | loop fusion | bytes 4194308 | tf_op jit(solution)/shard_map/dynamic_slice | solution.py:453
  32.9 0.1 fusion.9
  33.0 3.5 %shares.2 = (f32[1,384]{1,0:T(1,128)S(1)}, s32[1,384]{1,0:T(1,128)S(1)}, bf16[384,256]{1,0:T(8,128)(2,1)S(1)}, f32[384,256]{1,0:T(8,128)S(1)}, bf16[384,256]{1,0:T(8,128)(2,1)S(1)}) custom-call(s32[1]{0:T(128)} %bitcast.2.refs_0_, bf16[4,128,256]{2,1,0:T(8,128)(2,1)S(1)} %bitcast.8, bf16[4096,256]{1,0:T(8,128)(2,1)S(1)} %constant_dynamic-slice_fusion.refs_2_.items_ref, ...), custom_call_target="tpu_custom_call" | custom-call | tf_op jit(solution)/shard_map/shares/pallas_call | solution.py:188
  36.5 0.0 collective-permute-done.refs_1_
  36.5 3.5 %shares.3 = (f32[1,384]{1,0:T(1,128)S(1)}, s32[1,384]{1,0:T(1,128)S(1)}, bf16[384,256]{1,0:T(8,128)(2,1)S(1)}, bf16[800,256]{1,0:T(8,128)(2,1)S(1)}) custom-call(s32[1]{0:T(128)} %bitcast.2.refs_0_, bf16[4,128,256]{2,1,0:T(8,128)(2,1)S(1)} %collective-permute-done.refs_1_, bf16[4096,256]{1,0:T(8,128)(2,1)S(1)} %constant_dynamic-slice_fusion.refs_2_.items_ref, ...), custom_call_target="tpu_custom_call" | custom-call | tf_op jit(solution)/shard_map/shares/pallas_call | solution.py:188
  40.0 0.6 collective-permute-start.1
  40.5 0.0 copy-done.2
  40.6 0.1 select_reduce_fusion.1
  40.6 1.3 %collective-permute-done.1.refs_2_ = bf16[800,256]{1,0:T(8,128)(2,1)S(1)} collective-permute-done((bf16[800,256]{1,0:T(8,128)(2,1)S(1)}, bf16[800,256]{1,0:T(8,128)(2,1)S(1)}, u32[]{:S(2)}, u32[]{:S(2)}) %collective-permute-start.1) | collective-permute-done | bytes 409632 | tf_op jit(solution)/shard_map/ppermute | solution.py:22
  41.9 1.2 %packed.1 = bf16[16,57,256]{2,1,0:T(8,128)(2,1)} custom-call(f32[384,256]{1,0:T(8,128)S(1)} %get-tuple-element.45.refs_0_, bf16[384,256]{1,0:T(8,128)(2,1)S(1)} %get-tuple-element.46.refs_1_, bf16[800,256]{1,0:T(8,128)(2,1)S(1)} %collective-permute-done.1.refs_2_, f32[1,384]{1,0:T(1,128)S(1)} %get-tuple-element.47.refs_3_.log_ref, ...), custom_call_target="tpu_custom_call" | custom-call | tf_op jit(solution)/shard_map/packed/pallas_call | solution.py:238
  43.1 5.8 %all-to-all-start.1 = ((bf16[16,57,256]{2,1,0:T(8,128)(2,1)}), bf16[16,57,256]{2,1,0:T(8,128)(2,1)S(1)}, u32[]{:S(2)}, u32[]{:S(2)}) async-start(bf16[16,57,256]{2,1,0:T(8,128)(2,1)} %packed.1), calls=%async_computation.1 | async-start | bytes 1048576 | tf_op jit(solution)/shard_map/all_to_all | solution.py:470
  48.9 0.1 select_reduce_fusion
  49.0 10.9 %all-to-all-done.1.refs_1_ = bf16[16,57,256]{2,1,0:T(8,128)(2,1)S(1)} async-done(((bf16[16,57,256]{2,1,0:T(8,128)(2,1)}), bf16[16,57,256]{2,1,0:T(8,128)(2,1)S(1)}, u32[]{:S(2)}, u32[]{:S(2)}) %all-to-all-start.1) | async-done | bytes 466976 | tf_op jit(solution)/shard_map/all_to_all | solution.py:470
  59.9 1.0 %middle.1 = bf16[8,16,256]{2,1,0:T(8,128)(2,1)} custom-call(s32[1]{0:T(128)} %bitcast.1.refs_0_, bf16[16,57,256]{2,1,0:T(8,128)(2,1)S(1)} %all-to-all-done.1.refs_1_), custom_call_target="tpu_custom_call" | custom-call | tf_op jit(solution)/shard_map/middle/pallas_call | solution.py:292
  60.9 3.5 %all-to-all-start.2 = ((bf16[8,16,256]{2,1,0:T(8,128)(2,1)}), bf16[8,16,256]{2,1,0:T(8,128)(2,1)S(1)}, u32[]{:S(2)}, u32[]{:S(2)}) async-start(bf16[8,16,256]{2,1,0:T(8,128)(2,1)} %middle.1), calls=%async_computation.2 | async-start | bytes 131072 | tf_op jit(solution)/shard_map/all_to_all | solution.py:472
  64.5 0.0 copy-start.1
  64.5 1.0 %early.1.early_hbm = f32[2048,768]{1,0:T(8,128)S(1)} custom-call(f32[1,384]{1,0:T(1,128)S(1)} %get-tuple-element.47.refs_3_.log_ref, f32[1,384]{1,0:T(1,128)S(1)} %get-tuple-element.49.refs_4_.far_log_ref, bf16[384,256]{1,0:T(8,128)(2,1)S(1)} %get-tuple-element.64.states_ref, bf16[384,256]{1,0:T(8,128)(2,1)S(1)} %get-tuple-element.65.far_states_ref, ...), custom_call_target="tpu_custom_call" | custom-call | tf_op jit(solution)/shard_map/early/pallas_call | solution.py:325
  65.5 0.0 copy-start
  65.5 2.7 %copy-done = f32[2048,768]{1,0:T(8,128)} copy-done((f32[2048,768]{1,0:T(8,128)}, f32[2048,768]{1,0:T(8,128)S(1)}, u32[]{:S(2)}) %copy-start) | copy-done | bytes 6291480
  68.2 4.4 %all-to-all-done.2.arrived_ref = bf16[8,16,256]{2,1,0:T(8,128)(2,1)S(1)} async-done(((bf16[8,16,256]{2,1,0:T(8,128)(2,1)}), bf16[8,16,256]{2,1,0:T(8,128)(2,1)S(1)}, u32[]{:S(2)}, u32[]{:S(2)}) %all-to-all-start.2) | async-done | bytes 65568 | tf_op jit(solution)/shard_map/all_to_all | solution.py:472
  72.6 0.0 copy-done.1
  72.6 7.2 %last.1 = (f32[1,3]{1,0:T(1,128)}, bf16[3,256]{1,0:T(4,128)(2,1)}, bf16[4096,256]{1,0:T(8,128)(2,1)}) custom-call(s32[1]{0:T(128)} %bitcast.chip_ref, bf16[8,16,256]{2,1,0:T(8,128)(2,1)S(1)} %all-to-all-done.2.arrived_ref, s32[1,384]{1,0:T(1,128)S(1)} %get-tuple-element.50.place_ref, s32[1,384]{1,0:T(1,128)S(1)} %get-tuple-element.51.far_place_ref, ...), custom_call_target="tpu_custom_call" | custom-call | tf_op jit(solution)/shard_map/last/pallas_call | solution.py:422
  (8 shorter events, 0.1 us)
Async XLA Ops:
  2.1 28.9 %all-to-all-start = ((bf16[128,4,256]{2,1,0:T(4,128)(2,1)}), bf16[128,4,256]{2,1,0:T(4,128)(2,1)S(1)}, u32[]{:S(2)}, u32[]{:S(2)}) async-start(bf16[128,4,256]{2,1,0:T(4,128)(2,1)} %spread.1), calls=%async_computation | async-start | bytes 524288 | tf_op jit(solution)/shard_map/all_to_all | solution.py:457
  31.1 9.5 %copy-start.2 = (s32[2,16]{1,0:T(2,128)S(1)}, s32[2,16]{1,0:T(2,128)}, u32[]{:S(2)}) copy-start(s32[2,16]{1,0:T(2,128)} %param.15) | copy-start | bytes 388
  31.1 5.4 %collective-permute-start = (bf16[4,128,256]{2,1,0:T(8,128)(2,1)S(1)}, bf16[4,128,256]{2,1,0:T(8,128)(2,1)S(1)}, u32[]{:S(2)}, u32[]{:S(2)}) collective-permute-start(bf16[4,128,256]{2,1,0:T(8,128)(2,1)S(1)} %bitcast.7), channel_id=1, source_target_pairs={{0,2},{2,0},{1,3},{3,1},{4,6},{6,4},{5,7},{7,5},{8,10},{10,8},{9,1... | collective-permute-start | bytes 786440 | tf_op jit(solution)/shard_map/ppermute | solution.py:22
  40.0 1.9 %collective-permute-start.1 = (bf16[800,256]{1,0:T(8,128)(2,1)S(1)}, bf16[800,256]{1,0:T(8,128)(2,1)S(1)}, u32[]{:S(2)}, u32[]{:S(2)}) collective-permute-start(bf16[800,256]{1,0:T(8,128)(2,1)S(1)} %get-tuple-element.48), channel_id=1, source_target_pairs={{0,2},{2,0},{1,3},{3,1},{4,6},{6,4},{5,7},{7,5},{8,10},{10,8},{9,1... | collective-permute-start | bytes 1228808 | tf_op jit(solution)/shard_map/ppermute | solution.py:22
  43.1 16.8 %all-to-all-start.1 = ((bf16[16,57,256]{2,1,0:T(8,128)(2,1)}), bf16[16,57,256]{2,1,0:T(8,128)(2,1)S(1)}, u32[]{:S(2)}, u32[]{:S(2)}) async-start(bf16[16,57,256]{2,1,0:T(8,128)(2,1)} %packed.1), calls=%async_computation.1 | async-start | bytes 1048576 | tf_op jit(solution)/shard_map/all_to_all | solution.py:470
  60.9 11.6 %all-to-all-start.2 = ((bf16[8,16,256]{2,1,0:T(8,128)(2,1)}), bf16[8,16,256]{2,1,0:T(8,128)(2,1)S(1)}, u32[]{:S(2)}, u32[]{:S(2)}) async-start(bf16[8,16,256]{2,1,0:T(8,128)(2,1)} %middle.1), calls=%async_computation.2 | async-start | bytes 131072 | tf_op jit(solution)/shard_map/all_to_all | solution.py:472
  64.5 8.1 %copy-start.1 = (bf16[3,256]{1,0:T(4,128)(2,1)S(1)}, bf16[3,256]{1,0:T(4,128)(2,1)}, u32[]{:S(2)}) copy-start(bf16[3,256]{1,0:T(4,128)(2,1)} %hidden_ref.1) | copy-start | bytes 4612
  65.5 2.7 %copy-start = (f32[2048,768]{1,0:T(8,128)}, f32[2048,768]{1,0:T(8,128)S(1)}, u32[]{:S(2)}) copy-start(f32[2048,768]{1,0:T(8,128)S(1)} %early.1.early_hbm) | copy-start | bytes 18874372

commit v7 on v5

--- a/solution.py
+++ b/solution.py
@@ -101,7 +101,8 @@
 
 
 def share_kernel(
-    far, first_ref, given_ref, items_ref, log_ref, place_ref, states_ref, grad_ref, *rest
+    far, first_ref, given_ref, items_ref, near_log_ref, log_ref, place_ref, states_ref, grad_ref,
+    *rest,
 ):
     scores, places, grad, picked = rest[-4:]
     rows = given_ref.shape[0] - 1
@@ -158,17 +159,20 @@
     grad_ref[:count, :] = share.astype(BF16)
     grad_ref[count : 2 * count, :] = picked[...].astype(BF16)
     lines = [
-        piece[:, at : at + chips] for piece in three_parts(line) for at in range(0, count, chips)
+        piece[:, at : at + chips]
+        for source in (line, near_log_ref[...])
+        for piece in three_parts(source)
+        for at in range(0, count, chips)
     ]
     lines = jnp.concatenate(lines + [jnp.zeros((-len(lines) % 16, chips), F32)])
     lines = jnp.concatenate([lines, jnp.zeros((lines.shape[0], width - chips), F32)], axis=1)
     grad_ref[2 * count :, :] = lines.astype(BF16)
 
 
-def shares(far, first, given, items):
+def shares(far, first, given, items, near_logs):
     height, chips, width = given.shape
     count = (height - 1) * chips
-    lines = 3 * (height - 1)
+    lines = 6 * (height - 1)
     results = [
         jax.ShapeDtypeStruct((1, count), F32),
         jax.ShapeDtypeStruct((1, count), jnp.int32),
@@ -185,7 +189,7 @@
         lambda *refs: share_kernel(far, *refs),
         name="shares",
         out_shape=results,
-        in_specs=[pl.BlockSpec(memory_space=pltpu.SMEM), *in_vmem(2)],
+        in_specs=[pl.BlockSpec(memory_space=pltpu.SMEM), *in_vmem(3)],
         out_specs=in_vmem(len(results)),
         scratch_shapes=[
             pltpu.VMEM((count, items.shape[0]), F32),
@@ -194,11 +198,11 @@
             pltpu.VMEM((count, width), F32),
         ],
         compiler_params=pltpu.CompilerParams(vmem_limit_bytes=24 * MIB),
-    )(first, given, items)
+    )(first, given, items, near_logs)
 
 
 def pack_kernel(
-    rows, own_grad_ref, own_rows_ref, other_ref, own_log_ref, far_log_ref, other_log_ref, out_ref
+    rows, own_grad_ref, own_rows_ref, other_ref, own_log_ref, far_log_ref, out_ref
 ):
     length, _, width = out_ref.shape
     part = own_grad_ref.shape[0]
@@ -206,9 +210,11 @@
     lines = other_ref[2 * part :, :].astype(F32)
     chips = part // rows
     other = [
-        sum(lines[j * rows + k : j * rows + k + 1, :chips] for j in range(3)) for k in range(rows)
-    ]
-    other = jnp.concatenate(other + [other_log_ref[...]], axis=1)
+        sum(lines[at + j * rows + k : at + j * rows + k + 1, :chips] for j in range(3))
+        for at in (0, 3 * rows)
+        for k in range(rows)
+    ]
+    other = jnp.concatenate(other, axis=1)
     top = jnp.maximum(own, other)
     both = top + jnp.log(jnp.exp(own - top) + jnp.exp(other - top))
     grad = own_grad_ref[...] * column(jnp.exp(own - both)[:, :part])
@@ -233,7 +239,7 @@
         lambda *refs: pack_kernel(rows, *refs),
         name="packed",
         out_shape=jax.ShapeDtypeStruct((length, height, width), BF16),
-        in_specs=in_vmem(6),
+        in_specs=in_vmem(5),
         out_specs=pl.BlockSpec(memory_space=pltpu.VMEM),
         compiler_params=pltpu.CompilerParams(vmem_limit_bytes=12 * MIB),
     )(*pieces)
@@ -398,12 +404,14 @@
     mine = jnp.swapaxes(mine, 0, 1)
     first_own = first_own.reshape(1)
     other = from_pair(mine)
-    own_logs, place, states, own_grad, own_picked = shares(False, first_own, mine, items)
-    other_logs = from_pair(own_logs)
-    far_logs, far_place, far_states, far_share = shares(True, first_own, other, items)
+    no_logs = jnp.zeros((1, rows * lax.axis_size(CHIPS)), F32)
+    own_logs, place, states, own_grad, own_picked = shares(False, first_own, mine, items, no_logs)
+    far_logs, far_place, far_states, far_share = shares(
+        True, first_own, other, items, own_logs
+    )
     sent = packed(
         rows, lax.axis_size(PLANE), own_grad, own_picked, from_pair(far_share),
-        own_logs, far_logs, other_logs,
+        own_logs, far_logs,
     )
     arrived = lax.all_to_all(sent, PLANE, 0, 0, tiled=True)
     sent = middle(rows, lax.axis_size("z"), lax.axis_index(PLANE).reshape(1), arrived)

time: 84 us -> 77.9 us (0.927)
  local copies, waits for them, and re-layouts: 5.23 us -> 1.78 us
  Pallas kernels: 17.3 us -> 15.4 us
    unnamed x20 -> x4, local copies, waits for them, and re-layouts: 3.47 us -> 0.01 us
    pallas_call x2, Pallas kernels: 8.18 us -> 6.95 us  [shares(): pl.pallas_call(lambda *refs: share_kernel(far, *refs), name='shares', out...]
  transfers between devices with their start and end apart: 6 -> 5, of which waited for: 4 -> 4; matrix products, arithmetic and copies ran while one was open for 3% -> 3% of each run, Pallas kernels for 5% -> 4%
where the time goes in v7:
time: 77.9 us; the launch traced here: 77.5 us
  waiting for transfers between devices  33.7 us (43%)
  starting transfers between devices  25.4 us (33%)
  Pallas kernels  15.4 us (20%)
  local copies, waits for them, and re-layouts  1.78 us (2%)
  between operations  0.93 us (1%)
    all_to_all x1, starting transfers between devices, steps(): mine = lax.all_to_all(sent, CHIPS, 0, 0, tiled=True)  15.4 us
    all_to_all x1, waiting for transfers between devices, steps(): mine = lax.all_to_all(sent, CHIPS, 0, 0, tiled=True)  13.5 us
    all_to_all x1, waiting for transfers between devices, steps(): arrived = lax.all_to_all(sent, PLANE, 0, 0, tiled=True)  10.9 us
    all_to_all x1, waiting for transfers between devices, steps(): arrived = lax.all_to_all(sent, 'z', 0, 0, tiled=True)  8.08 us
    pallas_call x2, Pallas kernels, shares(): pl.pallas_call(lambda *refs: share_kernel(far, *refs), name='shares', out...  6.95 us
    all_to_all x1, starting transfers between devices, steps(): arrived = lax.all_to_all(sent, PLANE, 0, 0, tiled=True)  5.8 us
    pallas_call x1, Pallas kernels, last(): pl.pallas_call(last_kernel, name='last', out_shape=(jax.ShapeDtypeStruct(...  4.74 us
    all_to_all x1, starting transfers between devices, steps(): arrived = lax.all_to_all(sent, 'z', 0, 0, tiled=True)  3.53 us
  transfers between devices with their start and end apart: 5, of which 4 were waited for; matrix products, arithmetic and copies ran while one was open for 3% of the time, Pallas kernels for 4%

profile of v7, /device:TPU:8, one launch (start us, length us, event | category | flops | bytes accessed | tf_op | source)
XLA Modules:
  0.0 77.5 jit_solution(106519838357479173)
XLA Ops:
  0.6 1.5 %spread.1 = bf16[128,4,256]{2,1,0:T(4,128)(2,1)} custom-call(s32[3]{0:T(128)} %targets_hbm.1, bf16[3,256]{1,0:T(4,128)(2,1)} %hidden_ref.1), custom_call_target="tpu_custom_call" | custom-call | tf_op jit(solution)/shard_map/spread/pallas_call | solution.py:49
  2.1 15.4 %all-to-all-start = ((bf16[128,4,256]{2,1,0:T(4,128)(2,1)}), bf16[128,4,256]{2,1,0:T(4,128)(2,1)S(1)}, u32[]{:S(2)}, u32[]{:S(2)}) async-start(bf16[128,4,256]{2,1,0:T(4,128)(2,1)} %spread.1), calls=%async_computation | async-start | bytes 524288 | tf_op jit(solution)/shard_map/all_to_all | solution.py:403
  17.5 13.5 %all-to-all-done = bf16[128,4,256]{2,1,0:T(4,128)(2,1)S(1)} async-done(((bf16[128,4,256]{2,1,0:T(4,128)(2,1)}), bf16[128,4,256]{2,1,0:T(4,128)(2,1)S(1)}, u32[]{:S(2)}, u32[]{:S(2)}) %all-to-all-start) | async-done | bytes 262176 | tf_op jit(solution)/shard_map/all_to_all | solution.py:403
  31.1 0.1 collective-permute-start
  31.2 1.7 %constant_dynamic-slice_fusion.refs_2_.items_ref = bf16[4096,256]{1,0:T(8,128)(2,1)S(1)} fusion(bf16[8192,256]{1,0:T(8,128)(2,1)} %param.13, s32[]{:T(128)S(6)} %select_n.87), kind=kLoop, calls=%fused_computation.83 | loop fusion | bytes 4194308 | tf_op jit(solution)/shard_map/dynamic_slice | solution.py:399
  32.9 0.1 fusion.9
  33.0 0.0 copy-start.1
  33.0 3.5 %shares.2 = (f32[1,384]{1,0:T(1,128)S(1)}, s32[1,384]{1,0:T(1,128)S(1)}, bf16[384,256]{1,0:T(8,128)(2,1)S(1)}, f32[384,256]{1,0:T(8,128)S(1)}, bf16[384,256]{1,0:T(8,128)(2,1)S(1)}) custom-call(s32[1]{0:T(128)} %bitcast.2.refs_0_, bf16[4,128,256]{2,1,0:T(8,128)(2,1)S(1)} %bitcast.8, bf16[4096,256]{1,0:T(8,128)(2,1)S(1)} %constant_dynamic-slice_fusion.refs_2_.items_ref, ...), custom_call_target="tpu_custom_call" | custom-call | tf_op jit(solution)/shard_map/shares/pallas_call | solution.py:188
  36.5 0.0 collective-permute-done.refs_1_
  36.5 3.5 %shares.3 = (f32[1,384]{1,0:T(1,128)S(1)}, s32[1,384]{1,0:T(1,128)S(1)}, bf16[384,256]{1,0:T(8,128)(2,1)S(1)}, bf16[800,256]{1,0:T(8,128)(2,1)S(1)}) custom-call(s32[1]{0:T(128)} %bitcast.2.refs_0_, bf16[4,128,256]{2,1,0:T(8,128)(2,1)S(1)} %collective-permute-done.refs_1_, bf16[4096,256]{1,0:T(8,128)(2,1)S(1)} %constant_dynamic-slice_fusion.refs_2_.items_ref, ...), custom_call_target="tpu_custom_call" | custom-call | tf_op jit(solution)/shard_map/shares/pallas_call | solution.py:188
  40.0 0.0 copy-start
  40.0 0.6 collective-permute-start.1
  40.6 0.0 copy-done.1
  40.6 0.1 select_reduce_fusion.1
  40.7 1.3 %collective-permute-done.1.refs_2_ = bf16[800,256]{1,0:T(8,128)(2,1)S(1)} collective-permute-done((bf16[800,256]{1,0:T(8,128)(2,1)S(1)}, bf16[800,256]{1,0:T(8,128)(2,1)S(1)}, u32[]{:S(2)}, u32[]{:S(2)}) %collective-permute-start.1) | collective-permute-done | bytes 409632 | tf_op jit(solution)/shard_map/ppermute | solution.py:22
  41.9 1.2 %packed.1 = bf16[16,57,256]{2,1,0:T(8,128)(2,1)} custom-call(f32[384,256]{1,0:T(8,128)S(1)} %get-tuple-element.45.refs_0_, bf16[384,256]{1,0:T(8,128)(2,1)S(1)} %get-tuple-element.46.refs_1_, bf16[800,256]{1,0:T(8,128)(2,1)S(1)} %collective-permute-done.1.refs_2_, f32[1,384]{1,0:T(1,128)S(1)} %get-tuple-element.47.refs_3_, ...), custom_call_target="tpu_custom_call" | custom-call | tf_op jit(solution)/shard_map/packed/pallas_call | solution.py:238
  43.1 5.8 %all-to-all-start.1 = ((bf16[16,57,256]{2,1,0:T(8,128)(2,1)}), bf16[16,57,256]{2,1,0:T(8,128)(2,1)S(1)}, u32[]{:S(2)}, u32[]{:S(2)}) async-start(bf16[16,57,256]{2,1,0:T(8,128)(2,1)} %packed.1), calls=%async_computation.1 | async-start | bytes 1048576 | tf_op jit(solution)/shard_map/all_to_all | solution.py:416
  48.9 0.1 select_reduce_fusion
  49.1 10.9 %all-to-all-done.1.refs_1_ = bf16[16,57,256]{2,1,0:T(8,128)(2,1)S(1)} async-done(((bf16[16,57,256]{2,1,0:T(8,128)(2,1)}), bf16[16,57,256]{2,1,0:T(8,128)(2,1)S(1)}, u32[]{:S(2)}, u32[]{:S(2)}) %all-to-all-start.1) | async-done | bytes 466976 | tf_op jit(solution)/shard_map/all_to_all | solution.py:416
  59.9 1.0 %middle.1 = bf16[8,16,256]{2,1,0:T(8,128)(2,1)} custom-call(s32[1]{0:T(128)} %bitcast.1.refs_0_, bf16[16,57,256]{2,1,0:T(8,128)(2,1)S(1)} %all-to-all-done.1.refs_1_), custom_call_target="tpu_custom_call" | custom-call | tf_op jit(solution)/shard_map/middle/pallas_call | solution.py:292
  60.9 3.5 %all-to-all-start.2 = ((bf16[8,16,256]{2,1,0:T(8,128)(2,1)}), bf16[8,16,256]{2,1,0:T(8,128)(2,1)S(1)}, u32[]{:S(2)}, u32[]{:S(2)}) async-start(bf16[8,16,256]{2,1,0:T(8,128)(2,1)} %middle.1), calls=%async_computation.2 | async-start | bytes 131072 | tf_op jit(solution)/shard_map/all_to_all | solution.py:418
  64.5 8.1 %all-to-all-done.2.arrived_ref = bf16[8,16,256]{2,1,0:T(8,128)(2,1)S(1)} async-done(((bf16[8,16,256]{2,1,0:T(8,128)(2,1)}), bf16[8,16,256]{2,1,0:T(8,128)(2,1)S(1)}, u32[]{:S(2)}, u32[]{:S(2)}) %all-to-all-start.2) | async-done | bytes 65568 | tf_op jit(solution)/shard_map/all_to_all | solution.py:418
  72.6 0.0 copy-done
  72.6 4.7 %last.1 = (f32[1,3]{1,0:T(1,128)}, bf16[3,256]{1,0:T(4,128)(2,1)}, bf16[4096,256]{1,0:T(8,128)(2,1)}) custom-call(s32[1]{0:T(128)} %bitcast.chip_ref, bf16[8,16,256]{2,1,0:T(8,128)(2,1)S(1)} %all-to-all-done.2.arrived_ref, s32[1,384]{1,0:T(1,128)S(1)} %get-tuple-element.50.place_ref, s32[1,384]{1,0:T(1,128)S(1)} %get-tuple-element.51.far_place_ref, ...), custom_call_target="tpu_custom_call" | custom-call | tf_op jit(solution)/shard_map/last/pallas_call | solution.py:373
  (8 shorter events, 0.1 us)
Async XLA Ops:
  2.1 28.9 %all-to-all-start = ((bf16[128,4,256]{2,1,0:T(4,128)(2,1)}), bf16[128,4,256]{2,1,0:T(4,128)(2,1)S(1)}, u32[]{:S(2)}, u32[]{:S(2)}) async-start(bf16[128,4,256]{2,1,0:T(4,128)(2,1)} %spread.1), calls=%async_computation | async-start | bytes 524288 | tf_op jit(solution)/shard_map/all_to_all | solution.py:403
  31.1 5.4 %collective-permute-start = (bf16[4,128,256]{2,1,0:T(8,128)(2,1)S(1)}, bf16[4,128,256]{2,1,0:T(8,128)(2,1)S(1)}, u32[]{:S(2)}, u32[]{:S(2)}) collective-permute-start(bf16[4,128,256]{2,1,0:T(8,128)(2,1)S(1)} %bitcast.7), channel_id=1, source_target_pairs={{0,2},{2,0},{1,3},{3,1},{4,6},{6,4},{5,7},{7,5},{8,10},{10,8},{9,1... | collective-permute-start | bytes 786440 | tf_op jit(solution)/shard_map/ppermute | solution.py:22
  33.0 7.6 %copy-start.1 = (s32[2,16]{1,0:T(2,128)S(1)}, s32[2,16]{1,0:T(2,128)}, u32[]{:S(2)}) copy-start(s32[2,16]{1,0:T(2,128)} %param.15) | copy-start | bytes 388
  40.0 32.6 %copy-start = (bf16[3,256]{1,0:T(4,128)(2,1)S(1)}, bf16[3,256]{1,0:T(4,128)(2,1)}, u32[]{:S(2)}) copy-start(bf16[3,256]{1,0:T(4,128)(2,1)} %hidden_ref.1) | copy-start | bytes 4612
  40.0 1.9 %collective-permute-start.1 = (bf16[800,256]{1,0:T(8,128)(2,1)S(1)}, bf16[800,256]{1,0:T(8,128)(2,1)S(1)}, u32[]{:S(2)}, u32[]{:S(2)}) collective-permute-start(bf16[800,256]{1,0:T(8,128)(2,1)S(1)} %get-tuple-element.48), channel_id=1, source_target_pairs={{0,2},{2,0},{1,3},{3,1},{4,6},{6,4},{5,7},{7,5},{8,10},{10,8},{9,1... | collective-permute-start | bytes 1228808 | tf_op jit(solution)/shard_map/ppermute | solution.py:22
  43.1 16.8 %all-to-all-start.1 = ((bf16[16,57,256]{2,1,0:T(8,128)(2,1)}), bf16[16,57,256]{2,1,0:T(8,128)(2,1)S(1)}, u32[]{:S(2)}, u32[]{:S(2)}) async-start(bf16[16,57,256]{2,1,0:T(8,128)(2,1)} %packed.1), calls=%async_computation.1 | async-start | bytes 1048576 | tf_op jit(solution)/shard_map/all_to_all | solution.py:416
  60.9 11.6 %all-to-all-start.2 = ((bf16[8,16,256]{2,1,0:T(8,128)(2,1)}), bf16[8,16,256]{2,1,0:T(8,128)(2,1)S(1)}, u32[]{:S(2)}, u32[]{:S(2)}) async-start(bf16[8,16,256]{2,1,0:T(8,128)(2,1)} %middle.1), calls=%async_computation.2 | async-start | bytes 131072 | tf_op jit(solution)/shard_map/all_to_all | solution.py:418

commit v8 on v7

--- a/solution.py
+++ b/solution.py
@@ -349,6 +349,7 @@
     hidden_grad_ref[...] = jnp.concatenate(grads).astype(BF16)
     send(hidden_grad_ref, hidden_grad_hbm)
     line = jnp.concatenate([logs[c : c + 1] for c in range(wide)], axis=1)
+    weighted = line - jnp.log(weight)
     places = jnp.concatenate([place_ref[...], far_place_ref[...]], axis=1)
     states[: count // 2, :] = states_ref[...]
     states[count // 2 :, :] = far_states_ref[...]
@@ -357,9 +358,9 @@
             items_ref[at : at + block, :], states[...], (((1,), (1,)), ((), ())),
             preferred_element_type=F32,
         )
-        parts = jnp.exp(scores - line)
+        parts = jnp.exp(scores - weighted)
         matched = lax.broadcasted_iota(jnp.int32, parts.shape, 0) == places - at
-        signal = (weight * jnp.where(matched, parts - 1.0, parts)).astype(BF16)
+        signal = jnp.where(matched, parts - weight, parts).astype(BF16)
         buffer[at : at + block, :] = jnp.dot(
             signal, states[...], preferred_element_type=F32
         ).astype(BF16)

time: 77.9 us -> 77.6 us (level)
  no operation moved by 1% of the time
where the time goes in v8:
time: 77.6 us; the launch traced here: 77.2 us
  waiting for transfers between devices  33.7 us (43%)
  starting transfers between devices  25.4 us (33%)
  Pallas kernels  15.1 us (19%)
  local copies, waits for them, and re-layouts  1.78 us (2%)
  between operations  0.93 us (1%)
    all_to_all x1, starting transfers between devices, steps(): mine = lax.all_to_all(sent, CHIPS, 0, 0, tiled=True)  15.4 us
    all_to_all x1, waiting for transfers between devices, steps(): mine = lax.all_to_all(sent, CHIPS, 0, 0, tiled=True)  13.5 us
    all_to_all x1, waiting for transfers between devices, steps(): arrived = lax.all_to_all(sent, PLANE, 0, 0, tiled=True)  10.9 us
    all_to_all x1, waiting for transfers between devices, steps(): arrived = lax.all_to_all(sent, 'z', 0, 0, tiled=True)  8.08 us
    pallas_call x2, Pallas kernels, shares(): pl.pallas_call(lambda *refs: share_kernel(far, *refs), name='shares', out...  6.95 us
    all_to_all x1, starting transfers between devices, steps(): arrived = lax.all_to_all(sent, PLANE, 0, 0, tiled=True)  5.8 us
    pallas_call x1, Pallas kernels, last(): pl.pallas_call(last_kernel, name='last', out_shape=(jax.ShapeDtypeStruct(...  4.45 us
    all_to_all x1, starting transfers between devices, steps(): arrived = lax.all_to_all(sent, 'z', 0, 0, tiled=True)  3.53 us
  transfers between devices with their start and end apart: 5, of which 4 were waited for; matrix products, arithmetic and copies ran while one was open for 3% of the time, Pallas kernels for 4%

profile of v8, /device:TPU:8, one launch (start us, length us, event | category | flops | bytes accessed | tf_op | source)
XLA Modules:
  0.0 77.2 jit_solution(11786952320688634169)
XLA Ops:
  0.6 1.5 %spread.1 = bf16[128,4,256]{2,1,0:T(4,128)(2,1)} custom-call(s32[3]{0:T(128)} %targets_hbm.1, bf16[3,256]{1,0:T(4,128)(2,1)} %hidden_ref.1), custom_call_target="tpu_custom_call" | custom-call | tf_op jit(solution)/shard_map/spread/pallas_call | solution.py:49
  2.1 15.4 %all-to-all-start = ((bf16[128,4,256]{2,1,0:T(4,128)(2,1)}), bf16[128,4,256]{2,1,0:T(4,128)(2,1)S(1)}, u32[]{:S(2)}, u32[]{:S(2)}) async-start(bf16[128,4,256]{2,1,0:T(4,128)(2,1)} %spread.1), calls=%async_computation | async-start | bytes 524288 | tf_op jit(solution)/shard_map/all_to_all | solution.py:404
  17.5 13.5 %all-to-all-done = bf16[128,4,256]{2,1,0:T(4,128)(2,1)S(1)} async-done(((bf16[128,4,256]{2,1,0:T(4,128)(2,1)}), bf16[128,4,256]{2,1,0:T(4,128)(2,1)S(1)}, u32[]{:S(2)}, u32[]{:S(2)}) %all-to-all-start) | async-done | bytes 262176 | tf_op jit(solution)/shard_map/all_to_all | solution.py:404
  31.1 0.1 collective-permute-start
  31.2 1.7 %constant_dynamic-slice_fusion.refs_2_.items_ref = bf16[4096,256]{1,0:T(8,128)(2,1)S(1)} fusion(bf16[8192,256]{1,0:T(8,128)(2,1)} %param.13, s32[]{:T(128)S(6)} %select_n.87), kind=kLoop, calls=%fused_computation.83 | loop fusion | bytes 4194308 | tf_op jit(solution)/shard_map/dynamic_slice | solution.py:400
  32.9 0.1 fusion.9
  33.0 0.0 copy-start.1
  33.0 3.5 %shares.2 = (f32[1,384]{1,0:T(1,128)S(1)}, s32[1,384]{1,0:T(1,128)S(1)}, bf16[384,256]{1,0:T(8,128)(2,1)S(1)}, f32[384,256]{1,0:T(8,128)S(1)}, bf16[384,256]{1,0:T(8,128)(2,1)S(1)}) custom-call(s32[1]{0:T(128)} %bitcast.2.refs_0_, bf16[4,128,256]{2,1,0:T(8,128)(2,1)S(1)} %bitcast.8, bf16[4096,256]{1,0:T(8,128)(2,1)S(1)} %constant_dynamic-slice_fusion.refs_2_.items_ref, ...), custom_call_target="tpu_custom_call" | custom-call | tf_op jit(solution)/shard_map/shares/pallas_call | solution.py:188
  36.5 0.0 collective-permute-done.refs_1_
  36.5 3.5 %shares.3 = (f32[1,384]{1,0:T(1,128)S(1)}, s32[1,384]{1,0:T(1,128)S(1)}, bf16[384,256]{1,0:T(8,128)(2,1)S(1)}, bf16[800,256]{1,0:T(8,128)(2,1)S(1)}) custom-call(s32[1]{0:T(128)} %bitcast.2.refs_0_, bf16[4,128,256]{2,1,0:T(8,128)(2,1)S(1)} %collective-permute-done.refs_1_, bf16[4096,256]{1,0:T(8,128)(2,1)S(1)} %constant_dynamic-slice_fusion.refs_2_.items_ref, ...), custom_call_target="tpu_custom_call" | custom-call | tf_op jit(solution)/shard_map/shares/pallas_call | solution.py:188
  40.0 0.0 copy-start
  40.0 0.6 collective-permute-start.1
  40.6 0.0 copy-done.1
  40.6 0.1 select_reduce_fusion.1
  40.7 1.3 %collective-permute-done.1.refs_2_ = bf16[800,256]{1,0:T(8,128)(2,1)S(1)} collective-permute-done((bf16[800,256]{1,0:T(8,128)(2,1)S(1)}, bf16[800,256]{1,0:T(8,128)(2,1)S(1)}, u32[]{:S(2)}, u32[]{:S(2)}) %collective-permute-start.1) | collective-permute-done | bytes 409632 | tf_op jit(solution)/shard_map/ppermute | solution.py:22
  41.9 1.2 %packed.1 = bf16[16,57,256]{2,1,0:T(8,128)(2,1)} custom-call(f32[384,256]{1,0:T(8,128)S(1)} %get-tuple-element.45.refs_0_, bf16[384,256]{1,0:T(8,128)(2,1)S(1)} %get-tuple-element.46.refs_1_, bf16[800,256]{1,0:T(8,128)(2,1)S(1)} %collective-permute-done.1.refs_2_, f32[1,384]{1,0:T(1,128)S(1)} %get-tuple-element.47.refs_3_, ...), custom_call_target="tpu_custom_call" | custom-call | tf_op jit(solution)/shard_map/packed/pallas_call | solution.py:238
  43.1 5.8 %all-to-all-start.1 = ((bf16[16,57,256]{2,1,0:T(8,128)(2,1)}), bf16[16,57,256]{2,1,0:T(8,128)(2,1)S(1)}, u32[]{:S(2)}, u32[]{:S(2)}) async-start(bf16[16,57,256]{2,1,0:T(8,128)(2,1)} %packed.1), calls=%async_computation.1 | async-start | bytes 1048576 | tf_op jit(solution)/shard_map/all_to_all | solution.py:417
  48.9 0.1 select_reduce_fusion
  49.1 10.9 %all-to-all-done.1.refs_1_ = bf16[16,57,256]{2,1,0:T(8,128)(2,1)S(1)} async-done(((bf16[16,57,256]{2,1,0:T(8,128)(2,1)}), bf16[16,57,256]{2,1,0:T(8,128)(2,1)S(1)}, u32[]{:S(2)}, u32[]{:S(2)}) %all-to-all-start.1) | async-done | bytes 466976 | tf_op jit(solution)/shard_map/all_to_all | solution.py:417
  59.9 1.0 %middle.1 = bf16[8,16,256]{2,1,0:T(8,128)(2,1)} custom-call(s32[1]{0:T(128)} %bitcast.1.refs_0_, bf16[16,57,256]{2,1,0:T(8,128)(2,1)S(1)} %all-to-all-done.1.refs_1_), custom_call_target="tpu_custom_call" | custom-call | tf_op jit(solution)/shard_map/middle/pallas_call | solution.py:292
  60.9 3.5 %all-to-all-start.2 = ((bf16[8,16,256]{2,1,0:T(8,128)(2,1)}), bf16[8,16,256]{2,1,0:T(8,128)(2,1)S(1)}, u32[]{:S(2)}, u32[]{:S(2)}) async-start(bf16[8,16,256]{2,1,0:T(8,128)(2,1)} %middle.1), calls=%async_computation.2 | async-start | bytes 131072 | tf_op jit(solution)/shard_map/all_to_all | solution.py:419
  64.5 8.1 %all-to-all-done.2.arrived_ref = bf16[8,16,256]{2,1,0:T(8,128)(2,1)S(1)} async-done(((bf16[8,16,256]{2,1,0:T(8,128)(2,1)}), bf16[8,16,256]{2,1,0:T(8,128)(2,1)S(1)}, u32[]{:S(2)}, u32[]{:S(2)}) %all-to-all-start.2) | async-done | bytes 65568 | tf_op jit(solution)/shard_map/all_to_all | solution.py:419
  72.6 0.0 copy-done
  72.6 4.4 %last.1 = (f32[1,3]{1,0:T(1,128)}, bf16[3,256]{1,0:T(4,128)(2,1)}, bf16[4096,256]{1,0:T(8,128)(2,1)}) custom-call(s32[1]{0:T(128)} %bitcast.chip_ref, bf16[8,16,256]{2,1,0:T(8,128)(2,1)S(1)} %all-to-all-done.2.arrived_ref, s32[1,384]{1,0:T(1,128)S(1)} %get-tuple-element.50.place_ref, s32[1,384]{1,0:T(1,128)S(1)} %get-tuple-element.51.far_place_ref, ...), custom_call_target="tpu_custom_call" | custom-call | tf_op jit(solution)/shard_map/last/pallas_call | solution.py:374
  (8 shorter events, 0.1 us)
Async XLA Ops:
  2.1 28.9 %all-to-all-start = ((bf16[128,4,256]{2,1,0:T(4,128)(2,1)}), bf16[128,4,256]{2,1,0:T(4,128)(2,1)S(1)}, u32[]{:S(2)}, u32[]{:S(2)}) async-start(bf16[128,4,256]{2,1,0:T(4,128)(2,1)} %spread.1), calls=%async_computation | async-start | bytes 524288 | tf_op jit(solution)/shard_map/all_to_all | solution.py:404
  31.1 5.4 %collective-permute-start = (bf16[4,128,256]{2,1,0:T(8,128)(2,1)S(1)}, bf16[4,128,256]{2,1,0:T(8,128)(2,1)S(1)}, u32[]{:S(2)}, u32[]{:S(2)}) collective-permute-start(bf16[4,128,256]{2,1,0:T(8,128)(2,1)S(1)} %bitcast.7), channel_id=1, source_target_pairs={{0,2},{2,0},{1,3},{3,1},{4,6},{6,4},{5,7},{7,5},{8,10},{10,8},{9,1... | collective-permute-start | bytes 786440 | tf_op jit(solution)/shard_map/ppermute | solution.py:22
  33.0 7.6 %copy-start.1 = (s32[2,16]{1,0:T(2,128)S(1)}, s32[2,16]{1,0:T(2,128)}, u32[]{:S(2)}) copy-start(s32[2,16]{1,0:T(2,128)} %param.15) | copy-start | bytes 388
  40.0 32.6 %copy-start = (bf16[3,256]{1,0:T(4,128)(2,1)S(1)}, bf16[3,256]{1,0:T(4,128)(2,1)}, u32[]{:S(2)}) copy-start(bf16[3,256]{1,0:T(4,128)(2,1)} %hidden_ref.1) | copy-start | bytes 4612
  40.0 1.9 %collective-permute-start.1 = (bf16[800,256]{1,0:T(8,128)(2,1)S(1)}, bf16[800,256]{1,0:T(8,128)(2,1)S(1)}, u32[]{:S(2)}, u32[]{:S(2)}) collective-permute-start(bf16[800,256]{1,0:T(8,128)(2,1)S(1)} %get-tuple-element.48), channel_id=1, source_target_pairs={{0,2},{2,0},{1,3},{3,1},{4,6},{6,4},{5,7},{7,5},{8,10},{10,8},{9,1... | collective-permute-start | bytes 1228808 | tf_op jit(solution)/shard_map/ppermute | solution.py:22
  43.1 16.8 %all-to-all-start.1 = ((bf16[16,57,256]{2,1,0:T(8,128)(2,1)}), bf16[16,57,256]{2,1,0:T(8,128)(2,1)S(1)}, u32[]{:S(2)}, u32[]{:S(2)}) async-start(bf16[16,57,256]{2,1,0:T(8,128)(2,1)} %packed.1), calls=%async_computation.1 | async-start | bytes 1048576 | tf_op jit(solution)/shard_map/all_to_all | solution.py:417
  60.9 11.6 %all-to-all-start.2 = ((bf16[8,16,256]{2,1,0:T(8,128)(2,1)}), bf16[8,16,256]{2,1,0:T(8,128)(2,1)S(1)}, u32[]{:S(2)}, u32[]{:S(2)}) async-start(bf16[8,16,256]{2,1,0:T(8,128)(2,1)} %middle.1), calls=%async_computation.2 | async-start | bytes 131072 | tf_op jit(solution)/shard_map/all_to_all | solution.py:419
